TPU v7x, 16 devices: a 4x2x1 block of a 4x4x8 slice. The times are simulated.
16 devices in a mesh: rep: 4 (over y, z, core), dp: 4 (over x).
Axes of the slice: x: 4, y: 2, z: 1, core: 2. Of those that a mesh axis runs over, the one named last changes fastest.
The devices are a block of a 4x4x8 slice.
Arguments:
- x: bfloat16 [16, 4096, 768], P(('rep', 'dp')), parts along dimension 0
- dy: bfloat16 [16, 4096, 768], P(('rep', 'dp')), parts along dimension 0
- w_gate: bfloat16 [2, 768, 3072], replicated
- w_up: bfloat16 [2, 768, 3072], replicated
- w_down: bfloat16 [2, 3072, 768], replicated
- m_w_gate: float32 [2, 768, 3072], P(None, 'dp')
- m_w_up: float32 [2, 768, 3072], P(None, 'dp')
- m_w_down: float32 [2, 3072, 768], P(None, 'dp')
- v_w_gate: float32 [2, 768, 3072], P(None, 'dp')
- v_w_up: float32 [2, 768, 3072], P(None, 'dp')
- v_w_down: float32 [2, 3072, 768], P(None, 'dp')
Outputs:
- output 1: bfloat16 [8, 768, 3072], P('rep'), parts along dimension 0
- output 2: bfloat16 [8, 768, 3072], P('rep'), parts along dimension 0
- output 3: bfloat16 [8, 3072, 768], P('rep'), parts along dimension 0
- output 4: float32 [8, 768, 3072], P('rep', 'dp'), parts along dimension 0
- output 5: float32 [8, 768, 3072], P('rep', 'dp'), parts along dimension 0
- output 6: float32 [8, 3072, 768], P('rep', 'dp'), parts along dimension 0
- output 7: float32 [8, 768, 3072], P('rep', 'dp'), parts along dimension 0
- output 8: float32 [8, 768, 3072], P('rep', 'dp'), parts along dimension 0
- output 9: float32 [8, 3072, 768], P('rep', 'dp'), parts along dimension 0
There are 4 independent parts. A program takes and returns all parts, laid end to end along the dimension named above; an argument that names none is the same for every part.
All inputs are finite; a program needn't handle non-finite values.
Results may differ from a plain program's by a relative error of at most 0.022.
Values are sent between devices in bfloat16 or wider.
A program may use at most 768 MiB of HBM per device.

v0:
```python
import functools

import jax
import jax.numpy as jnp
from jax import lax
from jax.experimental import pallas as pl
from jax.experimental.pallas import tpu as pltpu
from jax.sharding import PartitionSpec as P


F32, BF16 = jnp.float32, jnp.bfloat16
STRIPE = 128
VMEM_LIMIT = 60 << 20
PIECES = ((0, 0, 1), (0, 1, 3), (2, 0, 2), (1, 0, 3), (1, 3, 1))


def dot(a, b):
    return jnp.dot(a, b, preferred_element_type=F32)


def dot_nt(a, b):
    return lax.dot_general(a, b, (((1,), (1,)), ((), ())), preferred_element_type=F32)


def sigmoid(x):
    return 0.5 * jnp.tanh(0.5 * x) + 0.5


def normed(h):
    wide = h.astype(F32)
    scale = lax.rsqrt(jnp.mean(wide * wide, -1, keepdims=True) + 1e-6)
    return (wide * scale).astype(BF16)


def cost(flops, read_and_written):
    return pl.CostEstimate(flops=int(flops), bytes_accessed=int(read_and_written), transcendentals=0)


def params(**more):
    return pltpu.CompilerParams(vmem_limit_bytes=VMEM_LIMIT, **more)


def nbytes(*arrays):
    return sum(a.size * jnp.dtype(a.dtype).itemsize for a in arrays)


def once(shape, index_map):
    return pl.BlockSpec(shape, index_map, pipeline_mode=pl.Buffered(1))


def stripes(n, chunks, c):
    return [slice((o * chunks + c) * STRIPE, (o * chunks + c + 1) * STRIPE) for o in range(n)]


def forward_kernel(n, chunks, tiles, *refs):
    x_first, x_next, x_before, dy, wg, wu, wd, *refs = refs
    gate, up, a_t, h1, a1, a1_t, dy_t, act, normal, y = refs
    m = pl.program_id(0)
    width = n * STRIPE

    def finish():
        h = (x_before[...].astype(F32) + y[...].astype(F32)).astype(BF16)
        h1[...] = h
        out = normed(h)
        a1[...] = out
        a1_t[...] = out.T

    @pl.when(m == 0)
    def _():
        normal[0] = normed(x_first[...])

    @pl.when(m < tiles)
    def _():
        a = normal[lax.rem(m, 2)]

        def dots(c):
            for o, w in ((gate, wg), (up, wu)):
                o[c] = dot(a, jnp.concatenate([w[0, :, s] for s in stripes(n, chunks, c)], 1))

        dots(0)
        for c in range(chunks):
            if c + 1 < chunks:
                dots(c + 1)
            g = gate[c]
            act[:, c * width : (c + 1) * width] = (g * sigmoid(g) * up[c]).astype(BF16)
        a_t[...] = a.T
        dy_t[...] = dy[...].T
        finish()
        down = jnp.concatenate([wd[0, s, :] for c in range(chunks) for s in stripes(n, chunks, c)], 0)
        y[...] = dot(act[...], down).astype(BF16)
        normal[lax.rem(m + 1, 2)] = normed(x_next[...])

    pl.when(m == tiles)(finish)


def forward(n, chunks, x, dy, w_gate, w_up, w_down, tm=256):
    t, d = x.shape
    ff, tiles, width = w_gate.shape[2], t // tm, n * STRIPE
    here, before = lambda m: jnp.minimum(m, tiles - 1), lambda m: jnp.maximum(m - 1, 0)
    row = lambda at: pl.BlockSpec((tm, d), lambda m: (at(m), 0))
    col = lambda at: pl.BlockSpec((d, tm), lambda m: (0, at(m)))
    wide = pl.BlockSpec((chunks, tm, width), lambda m: (0, here(m), 0))
    out = [jax.ShapeDtypeStruct((chunks, t, width), F32)] * 2 + [
        jax.ShapeDtypeStruct(s, BF16) for s in ((d, t), (t, d), (t, d), (d, t), (d, t))
    ]
    return pl.pallas_call(
        functools.partial(forward_kernel, n, chunks, tiles),
        grid=(tiles + 1,),
        in_specs=[once((tm, d), lambda m: (0, 0)), row(lambda m: jnp.minimum(m + 1, tiles - 1)), row(before), row(here)]
        + [once((1, d, ff), lambda m: (0, 0, 0))] * 2
        + [once((1, ff, d), lambda m: (0, 0, 0))],
        out_specs=[wide] * 2 + [col(here), row(before), row(before), col(before), col(here)],
        out_shape=out,
        scratch_shapes=[
            pltpu.VMEM((tm, ff), BF16),
            pltpu.VMEM((2, tm, d), BF16),
            pltpu.VMEM((tm, d), BF16),
        ],
        compiler_params=params(),
        cost_estimate=cost(6 * t * d * ff, nbytes(*out)),
        name="forward",
    )(x, x, x, dy, w_gate, w_up, w_down)


def neighbours(n):
    me = lax.axis_index("dp")
    return lax.rem(me + 1, n), lax.rem(me + 2, n), lax.rem(me + n - 1, n)


def greet(devices):
    barrier = pltpu.get_barrier_semaphore()
    for device in devices:
        pl.semaphore_signal(barrier, inc=1, device_id={"dp": device}, device_id_type=pl.DeviceIdType.MESH)
    pl.semaphore_wait(barrier, len(devices))


def remote(src, dst, send, recv, device):
    return pltpu.make_async_remote_copy(
        src_ref=src, dst_ref=dst, send_sem=send, recv_sem=recv, device_id={"dp": device}, device_id_type=pl.DeviceIdType.MESH
    )


class Ring:
    def __init__(self, n, raw, got, mid, send, recv):
        half = raw.shape[1] // 2
        self.a, self.b = pl.ds(0, half), pl.ds(half, half)
        self.raw, self.got, self.mid = raw, got, mid
        self.send, self.recv = send, recv
        self.right, _, self.left = neighbours(n)

    def copy(self, k):
        source = (
            lambda: self.raw.at[2, self.a],
            lambda: self.raw.at[1, self.b],
            lambda: self.mid.at[0],
            lambda: self.raw.at[2, self.b],
            lambda: self.raw.at[3, self.a],
            lambda: self.mid.at[1],
        )[k]()
        return remote(source, self.got.at[k], self.send.at[k], self.recv.at[k], self.right if k < 3 else self.left)

    def begin(self, which=(0, 3, 1, 4)):
        for k in which:
            self.copy(k).start()

    def go_on(self):
        for k, owner, half in ((0, 1, self.a), (3, 3, self.b)):
            self.copy(k).wait_recv()
            self.mid[k // 3] = (self.raw[owner, half].astype(F32) + self.got[k].astype(F32)).astype(BF16)
            self.copy(k + 2).start()

    def end(self, out, squares):
        for plain, summed, half in ((4, 2, self.a), (1, 5, self.b)):
            self.copy(plain).wait_recv()
            self.copy(summed).wait_recv()
            total = self.raw[0, half].astype(F32) + self.got[plain].astype(F32) + self.got[summed].astype(F32)
            total = total.astype(BF16)
            out[0, half] = total
            total = total.astype(F32)
            squares[...] += jnp.sum((total * total).reshape(-1, 8, total.shape[1]), 0)

    def sent(self, *which):
        for k in which:
            self.copy(k).wait_send()


def lay_out(n, raw, gacc, uacc, dacc):
    me = lax.axis_index("dp")
    rows = gacc.shape[0] // n
    for o in range(n):
        turn = lax.rem(o - me + n, n)
        raw[turn, :rows] = gacc[o * rows : (o + 1) * rows].astype(BF16)
        raw[turn, rows : 2 * rows] = uacc[o * rows : (o + 1) * rows].astype(BF16)
        for q in range(n):
            raw[turn, 2 * rows :, q * STRIPE : (q + 1) * STRIPE] = dacc[
                q * rows : (q + 1) * rows, o * STRIPE : (o + 1) * STRIPE
            ].astype(BF16)


def backward_parts(g, u, dact):
    dact = dact.astype(BF16).astype(F32)
    s = sigmoid(g)
    silu = g * s
    act = (silu * u).astype(BF16)
    du = (dact * silu).astype(BF16)
    dg = (dact * u * (s + silu * (1 - s))).astype(BF16)
    return act, dg, du


def states_gradient(da, h, dy):
    da = da.astype(BF16).astype(F32)
    wide = h.astype(F32)
    mean = jnp.mean(wide * wide, -1, keepdims=True) + 1e-6
    scale = lax.rsqrt(mean)
    dmean = jnp.sum(da * wide, -1, keepdims=True) * (-0.5 * scale / mean)
    back = (da * scale + wide * (dmean * (2.0 / wide.shape[1]))).astype(BF16)
    return (dy.astype(F32) + back.astype(F32)).astype(BF16)


def fetch(chunks, layer, whole, part, sems, c):
    n = sems.shape[0]
    for o in range(n):
        at = pl.ds(pl.multiple_of((o * chunks + c) * STRIPE, STRIPE), STRIPE)
        yield pltpu.make_async_copy(whole.at[layer, :, at], part.at[:, o * STRIPE : (o + 1) * STRIPE], sems.at[o])


def top_kernel(n, chunks, tiles, layer, *refs):
    a, a_t, dy, dy_t, h, wd, wg, wu, *refs = refs
    dh, dh_t, g_out, last, squares_out, *refs = refs
    gacc, uacc, dacc, da, raw, got, mid, squares, send, recv, local, wg_part, wu_part, w_sems = refs
    c, i = pl.program_id(0), pl.program_id(1)
    tm = a.shape[0]
    right, _, left = neighbours(n)
    before = jnp.maximum(c - 1, 0)
    slot, here, there = lax.rem(before, 2), lax.rem(c, 2), lax.rem(c + 1, 2)
    ring = Ring(n, raw, got.at[slot], mid, send.at[slot], recv.at[slot])

    def weights(c, slot):
        yield from fetch(chunks, layer, wg, wg_part.at[slot], w_sems.at[slot, 0], c)
        yield from fetch(chunks, layer, wu, wu_part.at[slot], w_sems.at[slot, 1], c)

    @pl.when(i == 0)
    def _():
        @pl.when(c == 0)
        def _():
            for copy in weights(c, here):
                copy.start()
            greet((right, left))
            squares[...] = jnp.zeros_like(squares)

        @pl.when(c > 0)
        def _():
            ring.begin()

        for copy in weights(c, here):
            copy.wait()

        @pl.when(c < chunks - 1)
        def _():
            for copy in weights(c + 1, there):
                copy.start()

    rows = pl.ds(pl.multiple_of(i * tm, tm), tm)
    pair = 2

    def work(at_end):
        parts = []
        for j in range(0, n, pair):
            to = slice(j * STRIPE, (j + pair) * STRIPE)
            w1, w2 = wg_part[here, :, to], wu_part[here, :, to]
            w3 = wd[0, j : j + pair, 0].reshape(pair * STRIPE, wd.shape[4])
            parts.append((to, w1, w2, dot(a[...], w1), dot(a[...], w2), dot_nt(dy[...], w3)))

        def states(fresh, dg, du, w1, w2):
            more = dot_nt(jnp.concatenate([dg, du], 1), jnp.concatenate([w1, w2], 1))
            da[rows, :] = jnp.where(fresh, 0.0, da[rows, :]) + more

        def weight_gradients(to, act, dg, du):
            for acc, left, right in ((gacc, a_t, dg), (uacc, a_t, du), (dacc, dy_t, act)):
                acc[:, to] = jnp.where(i == 0, 0.0, acc[:, to]) + dot(left[...], right)

        later = []
        for k, (to, w1, w2, g, u, dact) in enumerate(parts):
            fresh = (c == 0) & (k == 0)
            act, dg, du = backward_parts(g, u, dact)
            if at_end:
                states(fresh, dg, du, w1, w2)
                later.append((to, act, dg, du))
            else:
                weight_gradients(to, act, dg, du)
                states(fresh, dg, du, w1, w2)
        for one in later:
            weight_gradients(*one)
        if at_end:
            out = states_gradient(da[rows, :], h[...], dy[...])
            dh[...] = out
            dh_t[...] = out.T

    pl.when(c < chunks - 1)(lambda: work(False))
    pl.when(c == chunks - 1)(lambda: work(True))
    pl.when((c > 0) & (i == tiles // 2 - 1))(ring.go_on)

    @pl.when(i == tiles - 1)
    def _():
        @pl.when(c > 0)
        def _():
            ring.end(g_out, squares)
            ring.sent(*range(6))

        lay_out(n, raw, gacc, uacc, dacc)

        @pl.when(c == chunks - 1)
        def _():
            copy = pltpu.make_async_copy(raw, last, local)
            copy.start()
            squares_out[...] = squares[...]
            copy.wait()


def by_owner(n, w_down):
    layers, ff, d = w_down.shape
    return w_down.reshape(layers, n, ff // (n * STRIPE), STRIPE, d)


def top(n, chunks, layer, a, a_t, dy, dy_t, h, w_gate, w_up, w_down, tm=1024):
    t, d = a.shape
    width, tiles, block = n * STRIPE, t // tm, 3 * d // n
    row, col = pl.BlockSpec((tm, d), lambda c, i: (i, 0)), pl.BlockSpec((d, tm), lambda c, i: (0, i))
    at_end = lambda c, i: jnp.where(c == chunks - 1, i, 0)
    row_end, col_end = pl.BlockSpec((tm, d), lambda c, i: (at_end(c, i), 0)), pl.BlockSpec((d, tm), lambda c, i: (0, at_end(c, i)))
    down = pl.BlockSpec((1, n, 1, STRIPE, d), lambda c, i: (layer, 0, c, 0, 0))
    shapes = [
        jax.ShapeDtypeStruct((t, d), BF16),
        jax.ShapeDtypeStruct((d, t), BF16),
        jax.ShapeDtypeStruct((chunks - 1, block, width), BF16),
        jax.ShapeDtypeStruct((n, block, width), BF16),
        jax.ShapeDtypeStruct((8, width), F32),
    ]
    return pl.pallas_call(
        functools.partial(top_kernel, n, chunks, tiles, layer),
        grid=(chunks, tiles),
        in_specs=[row, col, row, col, row_end, down] + [pl.BlockSpec(memory_space=pl.ANY)] * 2,
        out_specs=[
            row_end,
            col_end,
            pl.BlockSpec((1, block, width), lambda c, i: (jnp.maximum(c - 1, 0), 0, 0)),
            pl.BlockSpec(memory_space=pl.ANY),
            pl.BlockSpec((8, width), lambda c, i: (0, 0)),
        ],
        out_shape=shapes,
        scratch_shapes=[pltpu.VMEM((d, width), F32)] * 3
        + [
            pltpu.VMEM((t, d), F32),
            pltpu.VMEM((n, block, width), BF16),
            pltpu.VMEM((2, 6, block // 2, width), BF16),
            pltpu.VMEM((2, block // 2, width), BF16),
            pltpu.VMEM((8, width), F32),
            pltpu.SemaphoreType.DMA((2, 6)),
            pltpu.SemaphoreType.DMA((2, 6)),
            pltpu.SemaphoreType.DMA,
            pltpu.VMEM((2, d, width), BF16),
            pltpu.VMEM((2, d, width), BF16),
            pltpu.SemaphoreType.DMA((2, 2, n)),
        ],
        compiler_params=pltpu.CompilerParams(vmem_limit_bytes=67043328, collective_id=0, has_side_effects=True),
        cost_estimate=cost(16 * t * d * width * chunks, chunks * nbytes(a, a_t, dy, dy_t)),
        name="top",
    )(a, a_t, dy, dy_t, h, by_owner(n, w_down), w_gate, w_up)


def bottom_kernel(n, chunks, tiles, *refs):
    a_t, dy, dy_t, gate, up, *refs = refs
    wd, *refs = refs
    first, squares_in, g_out, squares_out, gacc, uacc, dacc, raw, got, mid, squares, send, recv, local, others, to, fro = refs
    c, i = pl.program_id(0), pl.program_id(1)
    right, opposite, left = neighbours(n)

    def ring(k):
        slot = lax.rem(k, 2)
        return Ring(n, raw.at[slot], got.at[k], mid.at[slot], send.at[k], recv.at[k])

    @pl.when((c == 0) & (i == 0))
    def _():
        copy = pltpu.make_async_copy(first, raw.at[0], local)
        copy.start()
        greet((right, opposite, left))
        squares[...] = squares_in[...]
        copy.wait()

    @pl.when(i == 0)
    def _():
        ring(c).begin((0, 3))

    @pl.when(c < chunks)
    def _():
        pair = 2
        parts = []
        for j in range(0, n, pair):
            w = wd[0, j : j + pair, 0].reshape(pair * STRIPE, wd.shape[4])
            parts.append((slice(j * STRIPE, (j + pair) * STRIPE), dot_nt(dy[...], w)))
        for to, dact in parts:
            act, dg, du = backward_parts(gate[0, :, to], up[0, :, to], dact)
            for acc, left, right in ((gacc, a_t, dg), (uacc, a_t, du), (dacc, dy_t, act)):
                acc[:, to] = jnp.where(i == 0, 0.0, acc[:, to]) + dot(left[...], right)

    @pl.when(i == tiles // 4)
    def _():
        @pl.when(c > 0)
        def _():
            before = ring(c - 1)
            before.end(g_out, squares)
            before.sent(*range(6))

        ring(c).begin((1, 4))

    pl.when(i == tiles // 2)(lambda: ring(c).go_on())

    @pl.when((c < chunks) & (i == tiles - 1))
    def _():
        lay_out(n, raw.at[lax.rem(c + 1, 2)], gacc, uacc, dacc)

    @pl.when((c == chunks) & (i == tiles - 1))
    def _():
        final = ring(c)
        final.end(g_out, squares)
        final.sent(*range(6))
        copies = [
            remote(squares, others.at[k], to.at[k], fro.at[k], device) for k, device in enumerate((right, opposite, left))
        ]
        for copy in copies:
            copy.start()
        for copy in copies:
            copy.wait()
        squares_out[...] = squares[...] + (others[0] + others[1] + others[2])


def bottom(n, chunks, layer, a_t, dy, dy_t, gate, up, w_down, first, squares, tm=1024):
    d, t = a_t.shape
    width, tiles, block = n * STRIPE, t // tm, 3 * d // n
    tile = lambda c, i: jnp.where(c < chunks, i, tiles - 1)
    chunk = lambda c: jnp.minimum(c, chunks - 1)
    row, col = pl.BlockSpec((tm, d), lambda c, i: (tile(c, i), 0)), pl.BlockSpec((d, tm), lambda c, i: (0, tile(c, i)))
    wide = pl.BlockSpec((1, tm, width), lambda c, i: (chunk(c), tile(c, i), 0))
    small = pl.BlockSpec((8, width), lambda c, i: (0, 0))
    down = pl.BlockSpec((1, n, 1, STRIPE, d), lambda c, i: (layer, 0, chunk(c), 0, 0))
    done = lambda c, i: jnp.where((c == chunks) & (i == tiles - 1), chunks, jnp.maximum(c - 1, 0))
    return pl.pallas_call(
        functools.partial(bottom_kernel, n, chunks, tiles),
        grid=(chunks + 1, tiles),
        in_specs=[col, row, col, wide, wide, down, pl.BlockSpec(memory_space=pl.ANY), small],
        out_specs=[pl.BlockSpec((1, block, width), lambda c, i: (done(c, i), 0, 0)), small],
        out_shape=[
            jax.ShapeDtypeStruct((chunks + 1, block, width), BF16),
            jax.ShapeDtypeStruct((8, width), F32),
        ],
        scratch_shapes=[pltpu.VMEM((d, width), F32)] * 3
        + [
            pltpu.VMEM((2, n, block, width), BF16),
            pltpu.VMEM((chunks + 1, 6, block // 2, width), BF16),
            pltpu.VMEM((2, 2, block // 2, width), BF16),
            pltpu.VMEM((8, width), F32),
            pltpu.SemaphoreType.DMA((chunks + 1, 6)),
            pltpu.SemaphoreType.DMA((chunks + 1, 6)),
            pltpu.SemaphoreType.DMA,
            pltpu.VMEM((3, 8, width), F32),
            pltpu.SemaphoreType.DMA((3,)),
            pltpu.SemaphoreType.DMA((3,)),
        ],
        compiler_params=pltpu.CompilerParams(vmem_limit_bytes=VMEM_LIMIT, collective_id=1, has_side_effects=True),
        cost_estimate=cost(8 * t * d * width * chunks, nbytes(gate, up) + chunks * nbytes(a_t, dy, dy_t)),
        name="bottom",
    )(a_t, dy, dy_t, gate, up, by_owner(n, w_down), first, squares)


def adam_kernel(chunks, tall, count, squares, w, m, v, g_top, g_bottom, *refs):
    *w_out, m_out, v_out = refs
    factor = jnp.minimum(1.0, 0.5 * lax.rsqrt(jnp.full((1, 1), jnp.sum(squares[...])) / count + 1e-30))

    def work(layer, c, g):
        at = pl.ds(pl.multiple_of(c * STRIPE, STRIPE), STRIPE)
        i = (at, slice(None)) if tall else (slice(None), at)
        g = g.astype(F32)
        if tall:
            g = jnp.concatenate([g[:, q : q + STRIPE].T for q in range(0, g.shape[1], STRIPE)], 1)
        g = g * factor
        m_new = 0.9 * m[layer, *i] + 0.1 * g
        v_new = 0.95 * v[layer, *i] + 0.05 * g * g
        old = w[layer, *i].astype(F32)
        step = m_new * lax.rsqrt(v_new + 1e-8) + 0.1 * old
        w_out[layer][i] = (old - 0.02 * step).astype(BF16)
        m_out[layer, *i] = m_new
        v_out[layer, *i] = v_new

    @pl.loop(0, chunks - 1)
    def _(c):
        work(0, c, g_bottom[c + 1])
        work(1, c, g_top[c])

    work(0, chunks - 1, g_bottom[chunks])
    work(1, chunks - 1, g_bottom[0])


def adam(me, squares, w, m, v, g_top, g_bottom, which, count, chunks, tall, first, blocks, begun):
    layers, rows, _ = m.shape
    g_rows = g_top.shape[1] // 3
    g_width, width = (2 * STRIPE, 2 * g_rows) if tall else (STRIPE, STRIPE * chunks)
    block = pl.BlockSpec((layers, rows, width), lambda i, me: (0, 0, first + i))
    out = [jax.ShapeDtypeStruct((rows, width * blocks), BF16)] * layers + [jax.ShapeDtypeStruct(m.shape, F32)] * 2
    fixed = list(begun)

    def body(me_ref, *refs):
        adam_kernel(chunks, tall, count, *refs[:6], *refs[6 + len(fixed) :])

    outs = pl.pallas_call(
        body,
        grid_spec=pltpu.PrefetchScalarGridSpec(
            num_scalar_prefetch=1,
            grid=(blocks,),
            in_specs=[pl.BlockSpec(squares.shape, lambda i, me: (0, 0))]
            + [pl.BlockSpec((layers, rows, width), lambda i, me: (0, me[0], first + i)), block, block]
            + [pl.BlockSpec((g.shape[0], g_rows, g_width), lambda i, me: (0, which, first + i)) for g in (g_top, g_bottom)]
            + [pl.BlockSpec(memory_space=pl.ANY)] * len(fixed),
            out_specs=[pl.BlockSpec((rows, width), lambda i, me: (0, i))] * layers + [block, block],
        ),
        out_shape=out,
        input_output_aliases={7 + k: layers + k for k in range(len(fixed))},
        compiler_params=params(),
        cost_estimate=cost(16 * rows * width * blocks * layers, 22 * rows * width * blocks * layers),
        name="adam",
    )(me, squares, w, m, v, g_top, g_bottom, *fixed)
    return outs[:layers], outs[layers:]


def place_kernel(sources, me_ref, *refs):
    pieces, out = refs[:sources], refs[-1]
    k = pl.program_id(1)
    for at, piece in enumerate(pieces):
        pl.when(k == at)(lambda piece=piece: out.__setitem__(0, piece[...]))


def place(me, shape, pieces, first, blocks, begun):
    arrays, where = zip(*pieces, strict=True)
    rows, width = arrays[0].shape[0], arrays[0].shape[1] // blocks
    n = shape[1] // rows

    def at(j, k, me):
        layer, turn = 0, 0
        for i, (its_layer, its_turn) in enumerate(where):
            layer, turn = jnp.where(k == i, its_layer, layer), jnp.where(k == i, its_turn, turn)
        return layer, lax.rem(me[0] + turn, n), first + j

    fixed = list(begun)
    return pl.pallas_call(
        functools.partial(place_kernel, len(arrays)),
        grid_spec=pltpu.PrefetchScalarGridSpec(
            num_scalar_prefetch=1,
            grid=(blocks, len(arrays)),
            in_specs=[pl.BlockSpec((rows, width), lambda j, k, me: (0, j))] * len(arrays)
            + [pl.BlockSpec(memory_space=pl.ANY)] * len(fixed),
            out_specs=pl.BlockSpec((1, rows, width), at),
        ),
        out_shape=jax.ShapeDtypeStruct(shape, arrays[0].dtype),
        input_output_aliases={1 + len(arrays): 0} if fixed else {},
        compiler_params=params(),
        cost_estimate=cost(arrays[0].size, 4 * nbytes(*arrays)),
        name="place",
    )(me, *arrays, *fixed)


def send_around(n, own):
    right, left = [(i, (i + 1) % n) for i in range(n)], [(i, (i - 1) % n) for i in range(n)]

    def send(one, way):
        return lax.ppermute(one, "dp", way)

    l0, r1 = send(own[0], right), send(own[1], left)
    l1, r0 = send(own[1], right), send(own[0], left)
    return (l0, l1), (r0, r1), lambda: (send(l0, right), send(r1, left))


def solution(mesh):
    n = mesh.shape["dp"]

    def step(x, dy, w_gate, w_up, w_down, m_gate, m_up, m_down, v_gate, v_up, v_down):
        x, dy = x[0], dy[0]
        chunks = w_gate.shape[2] // (n * STRIPE)
        me = lax.axis_index("dp").astype(jnp.int32).reshape(1)

        gate, up, a0_t, h1, a1, a1_t, dy_t = forward(n, chunks, x, dy, w_gate, w_up, w_down)
        dh, dh_t, g_top, last, squares = top(n, chunks, 1, a1, a1_t, dy, dy_t, h1, w_gate, w_up, w_down)
        g_bottom, squares = bottom(n, chunks, 0, a0_t, dh, dh_t, gate, up, w_down, last, squares)

        states = ((w_gate, m_gate, v_gate), (w_up, m_up, v_up), (w_down, m_down, v_down))
        moments, whole, sent, count = [[], [], []], [[], [], []], [], 3 * w_gate.size
        for which, first, blocks in PIECES:
            own, moments[which] = adam(
                me, squares, *states[which], g_top, g_bottom, which, count, chunks, which == 2, first, blocks, moments[which]
            )
            squares = lax.optimization_barrier((squares, *own))[0]
            sent.append((own, *send_around(n, own)))
        for k, (which, first, blocks) in enumerate(PIECES):
            own, left, right, _ = sent[k]
            near = [(one, (layer, turn)) for turn, pair in ((0, own), (n - 1, left), (1, right)) for layer, one in enumerate(pair)]
            whole[which] = [place(me, states[which][0].shape, near, first, blocks, whole[which])]
        for k, (which, first, blocks) in enumerate(PIECES):
            far = [(one, (layer, 2)) for layer, one in enumerate(sent[k][3]())]
            whole[which] = [place(me, states[which][0].shape, far, first, blocks, whole[which])]
        return (*(one[0] for one in whole), *(one[0] for one in moments), *(one[1] for one in moments))

    seq, part, rows = P(("rep", "dp"), None, None), P("rep", None, None), P("rep", "dp", None)
    state = P(None, "dp", None)
    step = jax.shard_map(
        step,
        mesh=mesh,
        in_specs=(seq, seq) + (P(None, None, None),) * 3 + (state,) * 6,
        out_specs=(part,) * 3 + (rows,) * 6,
        check_vma=False,
    )
    return step
```

profile of v0, /device:TPU:112, one launch (start us, length us, event | category | flops | bytes accessed | tf_op | source)
XLA Modules:
  0.0 704.9 jit_solution(11602092357266447903)
XLA Ops:
  0.6 75.7 %forward.1 = (f32[6,4096,512]{2,1,0:T(8,128)}, f32[6,4096,512]{2,1,0:T(8,128)}, bf16[768,4096]{1,0:T(8,128)(2,1)}, bf16[4096,768]{1,0:T(8,128)(2,1)}, bf16[4096,...) custom-call(bf16[4096,768]{1,0:T(8,128)(2,1)} %bitcast.6, bf16[4096,768]{1,0:T(8,128)(2,1)} %bitcast.7, ...), custom_call_target="tpu_custom_call" | custom-call | flops 57982058496 | bytes 132120576 | tf_op jit(solution)/shard_map/forward/pallas_call | solution.py:106
  76.3 189.1 %top.1 = (bf16[4096,768]{1,0:T(8,128)(2,1)}, bf16[768,4096]{1,0:T(8,128)(2,1)}, bf16[5,576,512]{2,1,0:T(8,128)(2,1)}, bf16[4,576,512]{2,1,0:T(8,128)(2,1)}, f32[8,512]{1,0:T(8,128)}) custom-call(bf16[4096,768]{1,0:T(8,128)(2,1)} %get-tuple-element.48.refs_0_, bf16[768,4096]{1,0:T(8,128)(2,1)} %get-tuple-element.49.refs_1_, bf16[4096,768]{1,0:T(8,128)(2,1)} %bitcast.10, ...), custom_call_target="tpu_custom_call" | custom-call | flops 154618822656 | bytes 150994944 | tf_op jit(solution)/shard_map/top/pallas_call | solution.py:339
  265.4 149.4 %bottom.1 = (bf16[7,576,512]{2,1,0:T(8,128)(2,1)}, f32[8,512]{1,0:T(8,128)}) custom-call(bf16[768,4096]{1,0:T(8,128)(2,1)} %get-tuple-element.47.refs_0_, bf16[4096,768]{1,0:T(8,128)(2,1)} %get-tuple-element.52.refs_1_, bf16[768,4096]{1,0:T(8,128)(2,1)} %get-tuple-element.53.refs_2_, f32[6,4096,512]{2,1,0:T(8,128)} %get-tuple-element.54.refs_3_, ...), custom_call_target="tpu_custom_call" | custom-call | flops 77309411328 | bytes 213909504 | tf_op jit(solution)/shard_map/bottom/pallas_call | solution.py:447
  414.8 4.4 adam.5
  419.2 9.4 %adam.6 = (bf16[192,2304]{1,0:T(8,128)(2,1)}, bf16[192,2304]{1,0:T(8,128)(2,1)}, f32[2,192,3072]{2,1,0:T(8,128)}, f32[2,192,3072]{2,1,0:T(8,128)}) custom-call(s32[1]{0:T(128)} %bitcast.me_ref, f32[8,512]{1,0:T(8,128)} %get-tuple-element.74.refs_0_, bf16[2,768,3072]{2,1,0:T(8,128)(2,1)} %refs_1_.6, ...), custom_call_target="tpu_custom_call", output_to_operand_aliasing={{2}: (7, {}), {3}: (8, {})} | custom-call | flops 14155776 | bytes 19464192 | tf_op jit(solution)/shard_map/adam/pallas_call | solution.py:514
  428.6 9.9 %adam.7 = (bf16[768,768]{1,0:T(8,128)(2,1)}, bf16[768,768]{1,0:T(8,128)(2,1)}, f32[2,768,768]{2,1,0:T(8,128)}, f32[2,768,768]{2,1,0:T(8,128)}) custom-call(s32[1]{0:T(128)} %bitcast.me_ref, f32[8,512]{1,0:T(8,128)} %get-tuple-element.74.refs_0_, bf16[2,3072,768]{2,1,0:T(8,128)(2,1)} %refs_1_.7, f32[2,768,768]{2,1,0:T(8,128)} %refs_2_.7, ...), custom_call_target="tpu_custom_call" | custom-call | flops 18874368 | bytes 25952256 | tf_op jit(solution)/shard_map/adam/pallas_call | solution.py:514
  438.4 9.4 %adam.8 = (bf16[192,2304]{1,0:T(8,128)(2,1)}, bf16[192,2304]{1,0:T(8,128)(2,1)}, f32[2,192,3072]{2,1,0:T(8,128)}, f32[2,192,3072]{2,1,0:T(8,128)}) custom-call(s32[1]{0:T(128)} %bitcast.me_ref, f32[8,512]{1,0:T(8,128)} %get-tuple-element.74.refs_0_, bf16[2,768,3072]{2,1,0:T(8,128)(2,1)} %refs_1_.9, f32[2,192,3072]{2,1,0:T(8,128)} %refs_2_.9, ...), custom_call_target="tpu_custom_call" | custom-call | flops 14155776 | bytes 19464192 | tf_op jit(solution)/shard_map/adam/pallas_call | solution.py:514
  447.9 4.6 adam.9
  452.5 0.5 collective-permute-start.12
  453.0 2.7 collective-permute-start.14
  455.7 3.2 collective-permute-start.21
  459.0 4.8 collective-permute-done.12.refs_2_
  463.8 0.5 collective-permute-start.11
  464.3 1.5 collective-permute-start.16
  465.8 4.3 collective-permute-done.20.refs_3_
  470.1 3.3 collective-permute-start.18
  473.5 3.0 collective-permute-done.10.refs_3_
  476.4 0.5 collective-permute-start.6
  477.0 1.5 collective-permute-start.13
  478.5 23.2 %collective-permute-done.4.refs_2_ = bf16[192,768]{1,0:T(8,128)(2,1)S(1)} collective-permute-done((bf16[192,768]{1,0:T(8,128)(2,1)}, bf16[192,768]{1,0:T(8,128)(2,1)S(1)}, u32[]{:S(2)}, u32[]{:S(2)}) %collective-permute-start.4) | collective-permute-done | bytes 294944 | tf_op jit(solution)/shard_map/ppermute | solution.py:574
  501.8 0.9 collective-permute-start.22
  502.7 5.3 collective-permute-done.13.refs_0_
  508.0 0.5 collective-permute-start.7
  508.6 0.2 copy-done.22
  508.7 5.6 collective-permute-done.5.refs_0_
  514.4 0.5 collective-permute-start.23
  514.9 2.6 collective-permute-done.7.refs_1_
  517.5 3.2 collective-permute-start.2
  520.7 12.6 %collective-permute-done.22.refs_3_ = bf16[192,2304]{1,0:T(8,128)(2,1)S(1)} collective-permute-done((bf16[192,2304]{1,0:T(8,128)(2,1)S(1)}, bf16[192,2304]{1,0:T(8,128)(2,1)S(1)}, u32[]{:S(2)}, u32[]{:S(2)}) %collective-permute-start.22) | collective-permute-done | bytes 884768 | tf_op jit(solution)/shard_map/ppermute | solution.py:574
  533.3 0.5 collective-permute-start.9
  533.8 3.0 collective-permute-done.23.refs_4_
  536.9 15.5 %collective-permute-done.refs_2_ = bf16[192,2304]{1,0:T(8,128)(2,1)} collective-permute-done((bf16[192,2304]{1,0:T(8,128)(2,1)}, bf16[192,2304]{1,0:T(8,128)(2,1)}, u32[]{:S(2)}, u32[]{:S(2)}) %collective-permute-start) | collective-permute-done | bytes 884768 | tf_op jit(solution)/shard_map/ppermute | solution.py:574
  552.4 0.5 collective-permute-start.26
  552.9 3.0 collective-permute-done.2.refs_5_
  556.0 15.4 %collective-permute-done.8.refs_3_ = bf16[192,2304]{1,0:T(8,128)(2,1)} collective-permute-done((bf16[192,2304]{1,0:T(8,128)(2,1)}, bf16[192,2304]{1,0:T(8,128)(2,1)}, u32[]{:S(2)}, u32[]{:S(2)}) %collective-permute-start.8) | collective-permute-done | bytes 884768 | tf_op jit(solution)/shard_map/ppermute | solution.py:574
  571.3 0.5 collective-permute-start.29
  571.9 2.9 collective-permute-done.9.refs_4_
  574.8 1.0 copy-done.15
  575.8 20.8 %collective-permute-done.24.refs_2_ = bf16[768,768]{1,0:T(8,128)(2,1)S(1)} collective-permute-done((bf16[768,768]{1,0:T(8,128)(2,1)S(1)}, bf16[768,768]{1,0:T(8,128)(2,1)S(1)}, u32[]{:S(2)}, u32[]{:S(2)}) %collective-permute-start.24) | collective-permute-done | bytes 1179680 | tf_op jit(solution)/shard_map/ppermute | solution.py:574
  596.5 0.5 collective-permute-start.19
  597.0 3.2 collective-permute-done.26.refs_5_
  600.2 21.6 %collective-permute-done.28.refs_3_ = bf16[768,768]{1,0:T(8,128)(2,1)S(1)} collective-permute-done((bf16[768,768]{1,0:T(8,128)(2,1)S(1)}, bf16[768,768]{1,0:T(8,128)(2,1)S(1)}, u32[]{:S(2)}, u32[]{:S(2)}) %collective-permute-start.28) | collective-permute-done | bytes 1179680 | tf_op jit(solution)/shard_map/ppermute | solution.py:574
  621.8 0.5 collective-permute-start.27
  622.3 3.0 collective-permute-done.29.refs_4_
  625.4 1.0 copy-done.5
  626.4 14.3 %collective-permute-done.17.refs_0_ = bf16[192,2304]{1,0:T(8,128)(2,1)S(1)} collective-permute-done((bf16[192,2304]{1,0:T(8,128)(2,1)S(1)}, bf16[192,2304]{1,0:T(8,128)(2,1)S(1)}, u32[]{:S(2)}, u32[]{:S(2)}) %collective-permute-start.17) | collective-permute-done | bytes 884768 | tf_op jit(solution)/shard_map/ppermute | solution.py:574
  640.8 0.5 collective-permute-start.3
  641.3 3.0 collective-permute-done.19.refs_1_
  644.3 0.9 copy-done.13
  645.2 1.7 collective-permute-start.15
  646.9 3.8 place.10.refs_6_
  650.7 10.2 %place.14.refs_6_ = bf16[2,768,3072]{2,1,0:T(8,128)(2,1)} custom-call(s32[1]{0:T(128)} %bitcast.me_ref, bf16[192,2304]{1,0:T(8,128)(2,1)} %get-tuple-element.72.refs_0_, bf16[192,2304]{1,0:T(8,128)(2,1)} %get-tuple-element.73.refs_1_, bf16[192,2304]{1,0:T(8,128)(2,1)} %copy-done.8, bf16[192,2304]{1,0:T(8,128)(2,1)} %copy-done.10, ...), custom_call_target="tpu_custom_call" | custom-call | flops 442368 | bytes 21233664 | tf_op jit(solution)/shard_map/place/pallas_call | solution.py:553
  660.9 10.3 %place.11.refs_2_ = bf16[2,768,3072]{2,1,0:T(8,128)(2,1)} custom-call(s32[1]{0:T(128)} %bitcast.me_ref, bf16[192,2304]{1,0:T(8,128)(2,1)} %get-tuple-element.66.refs_0_, bf16[192,2304]{1,0:T(8,128)(2,1)} %get-tuple-element.67.refs_1_, bf16[192,2304]{1,0:T(8,128)(2,1)} %collective-permute-done.refs_2_, ...), custom_call_target="tpu_custom_call", output_to_operand_aliasing={{}: (7, {})} | custom-call | flops 442368 | bytes 21233664 | tf_op jit(solution)/shard_map/place/pallas_call | solution.py:553
  671.2 3.8 place.15.refs_2_
  675.1 1.9 place.12.refs_2_
  677.0 9.0 %place.18.refs_2_ = bf16[2,3072,768]{2,1,0:T(8,128)(2,1)} custom-call(s32[1]{0:T(128)} %bitcast.me_ref, bf16[768,768]{1,0:T(8,128)(2,1)} %get-tuple-element.69.refs_0_, bf16[768,768]{1,0:T(8,128)(2,1)} %get-tuple-element.70.refs_1_, bf16[768,768]{1,0:T(8,128)(2,1)} %copy-done.2, bf16[768,768]{1,0:T(8,128)(2,1)} %copy-done.4, bf16[768,768]{1,0:T(8,128)(2,1)} %copy-done.5, ...), custom_call_target="tpu_custom_call" | custom-call | flops 589824 | bytes 28311552 | tf_op jit(solution)/shard_map/place/pallas_call | solution.py:553
  686.0 4.5 place.16.refs_2_
  690.6 1.2 collective-permute-done.15.refs_1_
  691.7 0.7 copy-done.25
  692.4 1.9 place.17
  694.3 0.9 copy-done.14
  695.3 4.5 place.13
  699.8 1.0 copy-done.3
  700.8 4.1 place.19
  (66 shorter events, 0.1 us)
Async XLA Ops:
  447.9 16.4 %copy-start.6 = (bf16[192,2304]{1,0:T(8,128)(2,1)S(1)}, bf16[192,2304]{1,0:T(8,128)(2,1)}, u32[]{:S(2)}) copy-start(bf16[192,2304]{1,0:T(8,128)(2,1)} %get-tuple-element.72.refs_0_) | copy-start | bytes 2654212
  447.9 22.2 %copy-start.7 = (bf16[192,2304]{1,0:T(8,128)(2,1)S(1)}, bf16[192,2304]{1,0:T(8,128)(2,1)}, u32[]{:S(2)}) copy-start(bf16[192,2304]{1,0:T(8,128)(2,1)} %get-tuple-element.73.refs_1_) | copy-start | bytes 2654212
  447.9 89.0 %copy-start = (bf16[768,768]{1,0:T(8,128)(2,1)S(1)}, bf16[768,768]{1,0:T(8,128)(2,1)}, u32[]{:S(2)}) copy-start(bf16[768,768]{1,0:T(8,128)(2,1)} %get-tuple-element.69.refs_0_) | copy-start | bytes 3538948
  447.9 104.5 %copy-start.1 = (bf16[768,768]{1,0:T(8,128)(2,1)S(1)}, bf16[768,768]{1,0:T(8,128)(2,1)}, u32[]{:S(2)}) copy-start(bf16[768,768]{1,0:T(8,128)(2,1)} %get-tuple-element.70.refs_1_) | copy-start | bytes 3538948
  452.5 11.3 %collective-permute-start.12 = (bf16[192,768]{1,0:T(8,128)(2,1)}, bf16[192,768]{1,0:T(8,128)(2,1)S(1)}, u32[]{:S(2)}, u32[]{:S(2)}) collective-permute-start(bf16[192,768]{1,0:T(8,128)(2,1)} %get-tuple-element.77.refs_0_), channel_id=1, source_target_pairs={{0,1},{1,2},{2,3},{3,0},{4,5},{5,6},{6,7},{7,4},{8,9},{9,10},{10,1... | collective-permute-start | bytes 884744 | tf_op jit(solution)/shard_map/ppermute | solution.py:574
  453.0 11.3 %collective-permute-start.14 = (bf16[192,768]{1,0:T(8,128)(2,1)}, bf16[192,768]{1,0:T(8,128)(2,1)}, u32[]{:S(2)}, u32[]{:S(2)}) collective-permute-start(bf16[192,768]{1,0:T(8,128)(2,1)} %get-tuple-element.78.refs_1_), channel_id=1, source_target_pairs={{0,3},{1,0},{2,1},{3,2},{4,7},{5,4},{6,5},{7,6},{8,11},{9,8},{10,9... | collective-permute-start | bytes 884744 | tf_op jit(solution)/shard_map/ppermute | solution.py:574
  455.7 14.4 %collective-permute-start.20 = (bf16[192,768]{1,0:T(8,128)(2,1)}, bf16[192,768]{1,0:T(8,128)(2,1)S(1)}, u32[]{:S(2)}, u32[]{:S(2)}) collective-permute-start(bf16[192,768]{1,0:T(8,128)(2,1)} %get-tuple-element.78.refs_1_), channel_id=1, source_target_pairs={{0,1},{1,2},{2,3},{3,0},{4,5},{5,6},{6,7},{7,4},{8,9},{9,10},{10,1... | collective-permute-start | bytes 884744 | tf_op jit(solution)/shard_map/ppermute | solution.py:574
  455.7 14.4 %collective-permute-start.21 = (bf16[192,768]{1,0:T(8,128)(2,1)}, bf16[192,768]{1,0:T(8,128)(2,1)}, u32[]{:S(2)}, u32[]{:S(2)}) collective-permute-start(bf16[192,768]{1,0:T(8,128)(2,1)} %get-tuple-element.77.refs_0_), channel_id=1, source_target_pairs={{0,3},{1,0},{2,1},{3,2},{4,7},{5,4},{6,5},{7,6},{8,11},{9,8},{10,9... | collective-permute-start | bytes 884744 | tf_op jit(solution)/shard_map/ppermute | solution.py:574
  459.0 17.5 %collective-permute-start.10 = (bf16[192,768]{1,0:T(8,128)(2,1)}, bf16[192,768]{1,0:T(8,128)(2,1)S(1)}, u32[]{:S(2)}, u32[]{:S(2)}) collective-permute-start(bf16[192,768]{1,0:T(8,128)(2,1)} %get-tuple-element.62.refs_1_), channel_id=1, source_target_pairs={{0,1},{1,2},{2,3},{3,0},{4,5},{5,6},{6,7},{7,4},{8,9},{9,10},{10,1... | collective-permute-start | bytes 884744 | tf_op jit(solution)/shard_map/ppermute | solution.py:574
  463.8 44.8 %copy-start.20 = (bf16[192,768]{1,0:T(8,128)(2,1)}, bf16[192,768]{1,0:T(8,128)(2,1)S(1)}, u32[]{:S(2)}) copy-start(bf16[192,768]{1,0:T(8,128)(2,1)S(1)} %collective-permute-done.12.refs_2_) | copy-start | bytes 884740
  463.8 13.2 %collective-permute-start.11 = (bf16[192,768]{1,0:T(8,128)(2,1)}, bf16[192,768]{1,0:T(8,128)(2,1)S(1)}, u32[]{:S(2)}, u32[]{:S(2)}) collective-permute-start(bf16[192,768]{1,0:T(8,128)(2,1)} %get-tuple-element.61.refs_0_), channel_id=1, source_target_pairs={{0,3},{1,0},{2,1},{3,2},{4,7},{5,4},{6,5},{7,6},{8,11},{9,8},{10,9... | collective-permute-start | bytes 884744 | tf_op jit(solution)/shard_map/ppermute | solution.py:574
  464.3 53.2 %collective-permute-start.16 = (bf16[192,2304]{1,0:T(8,128)(2,1)S(1)}, bf16[192,2304]{1,0:T(8,128)(2,1)S(1)}, u32[]{:S(2)}, u32[]{:S(2)}) collective-permute-start(bf16[192,2304]{1,0:T(8,128)(2,1)S(1)} %copy-done.6), channel_id=1, source_target_pairs={{0,1},{1,2},{2,3},{3,0},{4,5},{5,6},{6,7},{7,4},{8,9},{9,10},{10,1... | collective-permute-start | bytes 2654216 | tf_op jit(solution)/shard_map/ppermute | solution.py:574
  470.1 31.6 %copy-start.21 = (bf16[192,768]{1,0:T(8,128)(2,1)}, bf16[192,768]{1,0:T(8,128)(2,1)S(1)}, u32[]{:S(2)}) copy-start(bf16[192,768]{1,0:T(8,128)(2,1)S(1)} %collective-permute-done.20.refs_3_) | copy-start | bytes 884740
  470.1 31.6 %collective-permute-start.4 = (bf16[192,768]{1,0:T(8,128)(2,1)}, bf16[192,768]{1,0:T(8,128)(2,1)S(1)}, u32[]{:S(2)}, u32[]{:S(2)}) collective-permute-start(bf16[192,768]{1,0:T(8,128)(2,1)} %get-tuple-element.61.refs_0_), channel_id=1, source_target_pairs={{0,1},{1,2},{2,3},{3,0},{4,5},{5,6},{6,7},{7,4},{8,9},{9,10},{10,1... | collective-permute-start | bytes 884744 | tf_op jit(solution)/shard_map/ppermute | solution.py:574
  470.1 50.6 %collective-permute-start.18 = (bf16[192,2304]{1,0:T(8,128)(2,1)S(1)}, bf16[192,2304]{1,0:T(8,128)(2,1)S(1)}, u32[]{:S(2)}, u32[]{:S(2)}) collective-permute-start(bf16[192,2304]{1,0:T(8,128)(2,1)S(1)} %copy-done.7), channel_id=1, source_target_pairs={{0,3},{1,0},{2,1},{3,2},{4,7},{5,4},{6,5},{7,6},{8,11},{9,8},{10,9... | collective-permute-start | bytes 2654216 | tf_op jit(solution)/shard_map/ppermute | solution.py:574
  476.4 25.3 %copy-start.16 = (bf16[192,768]{1,0:T(8,128)(2,1)}, bf16[192,768]{1,0:T(8,128)(2,1)S(1)}, u32[]{:S(2)}) copy-start(bf16[192,768]{1,0:T(8,128)(2,1)S(1)} %collective-permute-done.10.refs_3_) | copy-start | bytes 884740
  476.4 25.3 %collective-permute-start.6 = (bf16[192,768]{1,0:T(8,128)(2,1)}, bf16[192,768]{1,0:T(8,128)(2,1)S(1)}, u32[]{:S(2)}, u32[]{:S(2)}) collective-permute-start(bf16[192,768]{1,0:T(8,128)(2,1)} %get-tuple-element.62.refs_1_), channel_id=1, source_target_pairs={{0,3},{1,0},{2,1},{3,2},{4,7},{5,4},{6,5},{7,6},{8,11},{9,8},{10,9... | collective-permute-start | bytes 884744 | tf_op jit(solution)/shard_map/ppermute | solution.py:574
  477.0 24.8 %copy-start.17 = (bf16[192,768]{1,0:T(8,128)(2,1)}, bf16[192,768]{1,0:T(8,128)(2,1)S(1)}, u32[]{:S(2)}) copy-start(bf16[192,768]{1,0:T(8,128)(2,1)S(1)} %collective-permute-done.11.refs_4_) | copy-start | bytes 884740
  477.0 31.1 %collective-permute-start.13 = (bf16[192,768]{1,0:T(8,128)(2,1)S(1)}, bf16[192,768]{1,0:T(8,128)(2,1)S(1)}, u32[]{:S(2)}, u32[]{:S(2)}) collective-permute-start(bf16[192,768]{1,0:T(8,128)(2,1)S(1)} %collective-permute-done.12.refs_2_), channel_id=1, source_target_pairs={{0,1},{1,2},{2,3},{3,0},{4,5},{5,6},{6,7},{7,4},{8,9},{9,10},{10,1... | collective-permute-start | bytes 884744 | tf_op jit(solution)/shard_map/ppermute | solution.py:574
  501.7 6.8 copy-start.18
  501.7 12.6 %collective-permute-start.5 = (bf16[192,768]{1,0:T(8,128)(2,1)S(1)}, bf16[192,768]{1,0:T(8,128)(2,1)S(1)}, u32[]{:S(2)}, u32[]{:S(2)}) collective-permute-start(bf16[192,768]{1,0:T(8,128)(2,1)S(1)} %collective-permute-done.4.refs_2_), channel_id=1, source_target_pairs={{0,1},{1,2},{2,3},{3,0},{4,5},{5,6},{6,7},{7,4},{8,9},{9,10},{10,1... | collective-permute-start | bytes 884744 | tf_op jit(solution)/shard_map/ppermute | solution.py:574
  501.8 70.1 %copy-start.19 = (bf16[192,768]{1,0:T(8,128)(2,1)}, bf16[192,768]{1,0:T(8,128)(2,1)S(1)}, u32[]{:S(2)}) copy-start(bf16[192,768]{1,0:T(8,128)(2,1)S(1)} %collective-permute-done.6.refs_5_) | copy-start | bytes 884740
  501.8 31.5 %collective-permute-start.22 = (bf16[192,2304]{1,0:T(8,128)(2,1)S(1)}, bf16[192,2304]{1,0:T(8,128)(2,1)S(1)}, u32[]{:S(2)}, u32[]{:S(2)}) collective-permute-start(bf16[192,2304]{1,0:T(8,128)(2,1)S(1)} %copy-done.7), channel_id=1, source_target_pairs={{0,1},{1,2},{2,3},{3,0},{4,5},{5,6},{6,7},{7,4},{8,9},{9,10},{10,1... | collective-permute-start | bytes 2654216 | tf_op jit(solution)/shard_map/ppermute | solution.py:574
  508.0 0.7 copy-start.22
  508.0 9.4 %collective-permute-start.7 = (bf16[192,768]{1,0:T(8,128)(2,1)S(1)}, bf16[192,768]{1,0:T(8,128)(2,1)S(1)}, u32[]{:S(2)}, u32[]{:S(2)}) collective-permute-start(bf16[192,768]{1,0:T(8,128)(2,1)S(1)} %collective-permute-done.6.refs_5_), channel_id=1, source_target_pairs={{0,3},{1,0},{2,1},{3,2},{4,7},{5,4},{6,5},{7,6},{8,11},{9,8},{10,9... | collective-permute-start | bytes 884744 | tf_op jit(solution)/shard_map/ppermute | solution.py:574
  514.4 41.6 %copy-start.23 = (bf16[192,768]{1,0:T(8,128)(2,1)}, bf16[192,768]{1,0:T(8,128)(2,1)S(1)}, u32[]{:S(2)}) copy-start(bf16[192,768]{1,0:T(8,128)(2,1)S(1)} %collective-permute-done.5.refs_0_) | copy-start | bytes 884740
  514.4 22.5 %collective-permute-start.23 = (bf16[192,2304]{1,0:T(8,128)(2,1)S(1)}, bf16[192,2304]{1,0:T(8,128)(2,1)S(1)}, u32[]{:S(2)}, u32[]{:S(2)}) collective-permute-start(bf16[192,2304]{1,0:T(8,128)(2,1)S(1)} %copy-done.6), channel_id=1, source_target_pairs={{0,3},{1,0},{2,1},{3,2},{4,7},{5,4},{6,5},{7,6},{8,11},{9,8},{10,9... | collective-permute-start | bytes 2654216 | tf_op jit(solution)/shard_map/ppermute | solution.py:574
  517.5 38.5 %copy-start.24 = (bf16[192,768]{1,0:T(8,128)(2,1)}, bf16[192,768]{1,0:T(8,128)(2,1)S(1)}, u32[]{:S(2)}) copy-start(bf16[192,768]{1,0:T(8,128)(2,1)S(1)} %collective-permute-done.7.refs_1_) | copy-start | bytes 884740
  517.5 34.9 %collective-permute-start = (bf16[192,2304]{1,0:T(8,128)(2,1)}, bf16[192,2304]{1,0:T(8,128)(2,1)}, u32[]{:S(2)}, u32[]{:S(2)}) collective-permute-start(bf16[192,2304]{1,0:T(8,128)(2,1)} %get-tuple-element.66.refs_0_), channel_id=1, source_target_pairs={{0,1},{1,2},{2,3},{3,0},{4,5},{5,6},{6,7},{7,4},{8,9},{9,10},{10,1... | collective-permute-start | bytes 2654216 | tf_op jit(solution)/shard_map/ppermute | solution.py:574
  517.5 123.3 %copy-start.8 = (bf16[192,2304]{1,0:T(8,128)(2,1)}, bf16[192,2304]{1,0:T(8,128)(2,1)S(1)}, u32[]{:S(2)}) copy-start(bf16[192,2304]{1,0:T(8,128)(2,1)S(1)} %collective-permute-done.16.refs_2_) | copy-start | bytes 2654212
  517.5 38.4 %collective-permute-start.2 = (bf16[192,2304]{1,0:T(8,128)(2,1)}, bf16[192,2304]{1,0:T(8,128)(2,1)}, u32[]{:S(2)}, u32[]{:S(2)}) collective-permute-start(bf16[192,2304]{1,0:T(8,128)(2,1)} %get-tuple-element.67.refs_1_), channel_id=1, source_target_pairs={{0,3},{1,0},{2,1},{3,2},{4,7},{5,4},{6,5},{7,6},{8,11},{9,8},{10,9... | collective-permute-start | bytes 2654216 | tf_op jit(solution)/shard_map/ppermute | solution.py:574
  520.7 120.5 %copy-start.9 = (bf16[192,2304]{1,0:T(8,128)(2,1)}, bf16[192,2304]{1,0:T(8,128)(2,1)S(1)}, u32[]{:S(2)}) copy-start(bf16[192,2304]{1,0:T(8,128)(2,1)S(1)} %collective-permute-done.18.refs_5_) | copy-start | bytes 2654212
  520.7 50.6 %collective-permute-start.8 = (bf16[192,2304]{1,0:T(8,128)(2,1)}, bf16[192,2304]{1,0:T(8,128)(2,1)}, u32[]{:S(2)}, u32[]{:S(2)}) collective-permute-start(bf16[192,2304]{1,0:T(8,128)(2,1)} %get-tuple-element.67.refs_1_), channel_id=1, source_target_pairs={{0,1},{1,2},{2,3},{3,0},{4,5},{5,6},{6,7},{7,4},{8,9},{9,10},{10,1... | collective-permute-start | bytes 2654216 | tf_op jit(solution)/shard_map/ppermute | solution.py:574
  533.3 19.6 %copy-start.10 = (bf16[192,2304]{1,0:T(8,128)(2,1)}, bf16[192,2304]{1,0:T(8,128)(2,1)S(1)}, u32[]{:S(2)}) copy-start(bf16[192,2304]{1,0:T(8,128)(2,1)S(1)} %collective-permute-done.22.refs_3_) | copy-start | bytes 2654212
  533.3 41.5 %collective-permute-start.9 = (bf16[192,2304]{1,0:T(8,128)(2,1)}, bf16[192,2304]{1,0:T(8,128)(2,1)S(1)}, u32[]{:S(2)}, u32[]{:S(2)}) collective-permute-start(bf16[192,2304]{1,0:T(8,128)(2,1)} %get-tuple-element.66.refs_0_), channel_id=1, source_target_pairs={{0,3},{1,0},{2,1},{3,2},{4,7},{5,4},{6,5},{7,6},{8,11},{9,8},{10,9... | collective-permute-start | bytes 2654216 | tf_op jit(solution)/shard_map/ppermute | solution.py:574
  536.9 16.0 %copy-start.11 = (bf16[192,2304]{1,0:T(8,128)(2,1)}, bf16[192,2304]{1,0:T(8,128)(2,1)S(1)}, u32[]{:S(2)}) copy-start(bf16[192,2304]{1,0:T(8,128)(2,1)S(1)} %collective-permute-done.23.refs_4_) | copy-start | bytes 2654212
  536.9 59.6 %collective-permute-start.24 = (bf16[768,768]{1,0:T(8,128)(2,1)S(1)}, bf16[768,768]{1,0:T(8,128)(2,1)S(1)}, u32[]{:S(2)}, u32[]{:S(2)}) collective-permute-start(bf16[768,768]{1,0:T(8,128)(2,1)S(1)} %copy-done), channel_id=1, source_target_pairs={{0,1},{1,2},{2,3},{3,0},{4,5},{5,6},{6,7},{7,4},{8,9},{9,10},{10,1... | collective-permute-start | bytes 3538952 | tf_op jit(solution)/shard_map/ppermute | solution.py:574
  552.4 47.8 %collective-permute-start.26 = (bf16[768,768]{1,0:T(8,128)(2,1)S(1)}, bf16[768,768]{1,0:T(8,128)(2,1)}, u32[]{:S(2)}, u32[]{:S(2)}) collective-permute-start(bf16[768,768]{1,0:T(8,128)(2,1)S(1)} %copy-done.1), channel_id=1, source_target_pairs={{0,3},{1,0},{2,1},{3,2},{4,7},{5,4},{6,5},{7,6},{8,11},{9,8},{10,9... | collective-permute-start | bytes 3538952 | tf_op jit(solution)/shard_map/ppermute | solution.py:574
  555.9 65.9 %collective-permute-start.28 = (bf16[768,768]{1,0:T(8,128)(2,1)S(1)}, bf16[768,768]{1,0:T(8,128)(2,1)S(1)}, u32[]{:S(2)}, u32[]{:S(2)}) collective-permute-start(bf16[768,768]{1,0:T(8,128)(2,1)S(1)} %copy-done.1), channel_id=1, source_target_pairs={{0,1},{1,2},{2,3},{3,0},{4,5},{5,6},{6,7},{7,4},{8,9},{9,10},{10,1... | collective-permute-start | bytes 3538952 | tf_op jit(solution)/shard_map/ppermute | solution.py:574
  571.3 54.0 %collective-permute-start.29 = (bf16[768,768]{1,0:T(8,128)(2,1)S(1)}, bf16[768,768]{1,0:T(8,128)(2,1)S(1)}, u32[]{:S(2)}, u32[]{:S(2)}) collective-permute-start(bf16[768,768]{1,0:T(8,128)(2,1)S(1)} %copy-done), channel_id=1, source_target_pairs={{0,3},{1,0},{2,1},{3,2},{4,7},{5,4},{6,5},{7,6},{8,11},{9,8},{10,9... | collective-permute-start | bytes 3538952 | tf_op jit(solution)/shard_map/ppermute | solution.py:574
  574.8 1.0 copy-start.15
  574.8 66.0 %collective-permute-start.17 = (bf16[192,2304]{1,0:T(8,128)(2,1)S(1)}, bf16[192,2304]{1,0:T(8,128)(2,1)S(1)}, u32[]{:S(2)}, u32[]{:S(2)}) collective-permute-start(bf16[192,2304]{1,0:T(8,128)(2,1)S(1)} %collective-permute-done.16.refs_2_), channel_id=1, source_target_pairs={{0,1},{1,2},{2,3},{3,0},{4,5},{5,6},{6,7},{7,4},{8,9},{9,10},{10,1... | collective-permute-start | bytes 2654216 | tf_op jit(solution)/shard_map/ppermute | solution.py:574
  596.5 54.2 %copy-start.2 = (bf16[768,768]{1,0:T(8,128)(2,1)}, bf16[768,768]{1,0:T(8,128)(2,1)S(1)}, u32[]{:S(2)}) copy-start(bf16[768,768]{1,0:T(8,128)(2,1)S(1)} %collective-permute-done.24.refs_2_) | copy-start | bytes 3538948
  596.5 47.8 %collective-permute-start.19 = (bf16[192,2304]{1,0:T(8,128)(2,1)S(1)}, bf16[192,2304]{1,0:T(8,128)(2,1)S(1)}, u32[]{:S(2)}, u32[]{:S(2)}) collective-permute-start(bf16[192,2304]{1,0:T(8,128)(2,1)S(1)} %collective-permute-done.18.refs_5_), channel_id=1, source_target_pairs={{0,3},{1,0},{2,1},{3,2},{4,7},{5,4},{6,5},{7,6},{8,11},{9,8},{10,9... | collective-permute-start | bytes 2654216 | tf_op jit(solution)/shard_map/ppermute | solution.py:574
  600.2 99.6 %collective-permute-start.25 = (bf16[768,768]{1,0:T(8,128)(2,1)S(1)}, bf16[768,768]{1,0:T(8,128)(2,1)}, u32[]{:S(2)}, u32[]{:S(2)}) collective-permute-start(bf16[768,768]{1,0:T(8,128)(2,1)S(1)} %collective-permute-done.24.refs_2_), channel_id=1, source_target_pairs={{0,1},{1,2},{2,3},{3,0},{4,5},{5,6},{6,7},{7,4},{8,9},{9,10},{10,1... | collective-permute-start | bytes 3538952 | tf_op jit(solution)/shard_map/ppermute | solution.py:574
  621.8 3.6 copy-start.4
  621.8 78.0 %collective-permute-start.27 = (bf16[768,768]{1,0:T(8,128)(2,1)}, bf16[768,768]{1,0:T(8,128)(2,1)S(1)}, u32[]{:S(2)}, u32[]{:S(2)}) collective-permute-start(bf16[768,768]{1,0:T(8,128)(2,1)} %collective-permute-done.26.refs_5_), channel_id=1, source_target_pairs={{0,3},{1,0},{2,1},{3,2},{4,7},{5,4},{6,5},{7,6},{8,11},{9,8},{10,9... | collective-permute-start | bytes 3538952 | tf_op jit(solution)/shard_map/ppermute | solution.py:574
  625.4 1.0 copy-start.5
  625.4 69.0 %collective-permute-start.1 = (bf16[192,2304]{1,0:T(8,128)(2,1)}, bf16[192,2304]{1,0:T(8,128)(2,1)S(1)}, u32[]{:S(2)}, u32[]{:S(2)}) collective-permute-start(bf16[192,2304]{1,0:T(8,128)(2,1)} %collective-permute-done.refs_2_), channel_id=1, source_target_pairs={{0,1},{1,2},{2,3},{3,0},{4,5},{5,6},{6,7},{7,4},{8,9},{9,10},{10,1... | collective-permute-start | bytes 2654216 | tf_op jit(solution)/shard_map/ppermute | solution.py:574
  640.8 3.6 copy-start.12
  640.8 53.6 %collective-permute-start.3 = (bf16[192,2304]{1,0:T(8,128)(2,1)}, bf16[192,2304]{1,0:T(8,128)(2,1)}, u32[]{:S(2)}, u32[]{:S(2)}) collective-permute-start(bf16[192,2304]{1,0:T(8,128)(2,1)} %collective-permute-done.2.refs_5_), channel_id=1, source_target_pairs={{0,3},{1,0},{2,1},{3,2},{4,7},{5,4},{6,5},{7,6},{8,11},{9,8},{10,9... | collective-permute-start | bytes 2654216 | tf_op jit(solution)/shard_map/ppermute | solution.py:574
  644.3 0.9 copy-start.13
  645.2 46.5 %collective-permute-start.15 = (bf16[192,768]{1,0:T(8,128)(2,1)}, bf16[192,768]{1,0:T(8,128)(2,1)S(1)}, u32[]{:S(2)}, u32[]{:S(2)}) collective-permute-start(bf16[192,768]{1,0:T(8,128)(2,1)} %collective-permute-done.14.refs_5_), channel_id=1, source_target_pairs={{0,3},{1,0},{2,1},{3,2},{4,7},{5,4},{6,5},{7,6},{8,11},{9,8},{10,9... | collective-permute-start | bytes 884744 | tf_op jit(solution)/shard_map/ppermute | solution.py:574
  691.7 0.7 copy-start.25
  694.3 0.9 copy-start.14
  699.8 1.0 copy-start.3
where the time goes:
time: 706 us; the launch traced here: 705 us
  Pallas kernels  506 us (72%)
  waiting for transfers between devices  169 us (24%)
  starting transfers between devices  23.8 us (3%)
    pallas_call x1, Pallas kernels, top(): pl.pallas_call(functools.partial(top_kernel, n, chunks, tiles, layer), gr...  189 us
    ppermute x30, waiting for transfers between devices, send(): return lax.ppermute(one, 'dp', way)  169 us
    pallas_call x1, Pallas kernels, bottom(): pl.pallas_call(functools.partial(bottom_kernel, n, chunks, tiles), grid=(...  149 us
    pallas_call x1, Pallas kernels, forward(): pl.pallas_call(functools.partial(forward_kernel, n, chunks, tiles), grid=...  75.7 us
    pallas_call x10, Pallas kernels, place(): pl.pallas_call(functools.partial(place_kernel, len(arrays)), grid_spec=pl...  54.1 us
    pallas_call x5, Pallas kernels, adam(): pl.pallas_call(body, grid_spec=pltpu.PrefetchScalarGridSpec(num_scalar_pr...  37.7 us
    ppermute x30, starting transfers between devices, send(): return lax.ppermute(one, 'dp', way)  23.8 us
  transfers between devices with their start and end apart: 30, of which 20 were waited for; matrix products, arithmetic and copies ran while one was open for 0% of the time, Pallas kernels for 7%

commit v1 on v0

--- a/solution.py
+++ b/solution.py
@@ -11,7 +11,8 @@
 F32, BF16 = jnp.float32, jnp.bfloat16
 STRIPE = 128
 VMEM_LIMIT = 60 << 20
-PIECES = ((0, 0, 1), (0, 1, 3), (2, 0, 2), (1, 0, 3), (1, 3, 1))
+EARLY = 0
+PIECES = ((0, 0, 1, False), (0, 1, 3, False), (2, 0, 2, True), (1, 0, 3, True), (1, 3, 1, False))
 
 
 def dot(a, b):
@@ -54,9 +55,27 @@
 
 def forward_kernel(n, chunks, tiles, *refs):
     x_first, x_next, x_before, dy, wg, wu, wd, *refs = refs
-    gate, up, a_t, h1, a1, a1_t, dy_t, act, normal, y = refs
+    moments, (gate, up, a_t, h1, a1, a1_t, dy_t, near_a, near_b), refs = refs[:6], refs[6:15], refs[15:]
+    act, normal, y, pack_a, pack_b, packed, own, send, recv = refs
     m = pl.program_id(0)
     width = n * STRIPE
+    right, _, left = neighbours(n)
+
+    def packing():
+        for k, ref in enumerate(moments[:4]):
+            for o, s in enumerate(stripes(n, chunks, EARLY)):
+                yield pltpu.make_async_copy(
+                    ref.at[1, :, s], pack_a.at[k, :, o * STRIPE : (o + 1) * STRIPE], packed.at[k * n + o]
+                )
+        for k, ref in enumerate(moments[4:]):
+            rows = slice(EARLY * STRIPE, (EARLY + 1) * STRIPE)
+            yield pltpu.make_async_copy(ref.at[1, rows, :], pack_b.at[k], packed.at[4 * n + k])
+
+    def copies():
+        for k, (part, near) in enumerate(((pack_a, near_a), (pack_b, near_b))):
+            yield remote(part, near.at[0], send.at[k], recv.at[k], right)
+            yield remote(part, near.at[1], send.at[2 + k], recv.at[2 + k], left)
+            yield pltpu.make_async_copy(part, near.at[2], own.at[k])
 
     def finish():
         h = (x_before[...].astype(F32) + y[...].astype(F32)).astype(BF16)
@@ -67,7 +86,18 @@
 
     @pl.when(m == 0)
     def _():
+        for copy in packing():
+            copy.start()
+        hail((right, left))
         normal[0] = normed(x_first[...])
+
+    @pl.when(m == 1)
+    def _():
+        pl.semaphore_wait(pltpu.get_barrier_semaphore(), 2)
+        for copy in packing():
+            copy.wait()
+        for copy in copies():
+            copy.start()
 
     @pl.when(m < tiles)
     def _():
@@ -90,36 +120,49 @@
         y[...] = dot(act[...], down).astype(BF16)
         normal[lax.rem(m + 1, 2)] = normed(x_next[...])
 
-    pl.when(m == tiles)(finish)
-
-
-def forward(n, chunks, x, dy, w_gate, w_up, w_down, tm=256):
+    @pl.when(m == tiles)
+    def _():
+        finish()
+        for copy in copies():
+            copy.wait()
+
+
+def forward(n, chunks, x, dy, w_gate, w_up, w_down, moments, tm=256):
     t, d = x.shape
     ff, tiles, width = w_gate.shape[2], t // tm, n * STRIPE
     here, before = lambda m: jnp.minimum(m, tiles - 1), lambda m: jnp.maximum(m - 1, 0)
     row = lambda at: pl.BlockSpec((tm, d), lambda m: (at(m), 0))
     col = lambda at: pl.BlockSpec((d, tm), lambda m: (0, at(m)))
     wide = pl.BlockSpec((chunks, tm, width), lambda m: (0, here(m), 0))
-    out = [jax.ShapeDtypeStruct((chunks, t, width), F32)] * 2 + [
-        jax.ShapeDtypeStruct(s, BF16) for s in ((d, t), (t, d), (t, d), (d, t), (d, t))
-    ]
+    pack_a, pack_b = (4, d // n, width), (2, STRIPE, d)
+    out = [jax.ShapeDtypeStruct((chunks, t, width), F32)] * 2
+    out += [jax.ShapeDtypeStruct(s, BF16) for s in ((d, t), (t, d), (t, d), (d, t), (d, t))]
+    out += [jax.ShapeDtypeStruct((3, *s), F32) for s in (pack_a, pack_b)]
+    whole = pl.BlockSpec(memory_space=pl.ANY)
     return pl.pallas_call(
         functools.partial(forward_kernel, n, chunks, tiles),
         grid=(tiles + 1,),
         in_specs=[once((tm, d), lambda m: (0, 0)), row(lambda m: jnp.minimum(m + 1, tiles - 1)), row(before), row(here)]
         + [once((1, d, ff), lambda m: (0, 0, 0))] * 2
-        + [once((1, ff, d), lambda m: (0, 0, 0))],
-        out_specs=[wide] * 2 + [col(here), row(before), row(before), col(before), col(here)],
+        + [once((1, ff, d), lambda m: (0, 0, 0))]
+        + [whole] * 6,
+        out_specs=[wide] * 2 + [col(here), row(before), row(before), col(before), col(here), whole, whole],
         out_shape=out,
         scratch_shapes=[
             pltpu.VMEM((tm, ff), BF16),
             pltpu.VMEM((2, tm, d), BF16),
             pltpu.VMEM((tm, d), BF16),
+            pltpu.VMEM(pack_a, F32),
+            pltpu.VMEM(pack_b, F32),
+            pltpu.SemaphoreType.DMA((4 * n + 2,)),
+            pltpu.SemaphoreType.DMA((2,)),
+            pltpu.SemaphoreType.DMA((4,)),
+            pltpu.SemaphoreType.DMA((4,)),
         ],
-        compiler_params=params(),
+        compiler_params=params(collective_id=2, has_side_effects=True),
         cost_estimate=cost(6 * t * d * ff, nbytes(*out)),
         name="forward",
-    )(x, x, x, dy, w_gate, w_up, w_down)
+    )(x, x, x, dy, w_gate, w_up, w_down, *moments)
 
 
 def neighbours(n):
@@ -127,11 +170,15 @@
     return lax.rem(me + 1, n), lax.rem(me + 2, n), lax.rem(me + n - 1, n)
 
 
-def greet(devices):
+def hail(devices):
     barrier = pltpu.get_barrier_semaphore()
     for device in devices:
         pl.semaphore_signal(barrier, inc=1, device_id={"dp": device}, device_id_type=pl.DeviceIdType.MESH)
-    pl.semaphore_wait(barrier, len(devices))
+
+
+def greet(devices):
+    hail(devices)
+    pl.semaphore_wait(pltpu.get_barrier_semaphore(), len(devices))
 
 
 def remote(src, dst, send, recv, device):
@@ -187,14 +234,15 @@
 def lay_out(n, raw, gacc, uacc, dacc):
     me = lax.axis_index("dp")
     rows = gacc.shape[0] // n
-    for o in range(n):
+
+    @pl.loop(0, n)
+    def _(o):
         turn = lax.rem(o - me + n, n)
-        raw[turn, :rows] = gacc[o * rows : (o + 1) * rows].astype(BF16)
-        raw[turn, rows : 2 * rows] = uacc[o * rows : (o + 1) * rows].astype(BF16)
+        mine, stripe = pl.ds(pl.multiple_of(o * rows, rows), rows), pl.ds(pl.multiple_of(o * STRIPE, STRIPE), STRIPE)
+        raw[turn, :rows] = gacc[mine].astype(BF16)
+        raw[turn, rows : 2 * rows] = uacc[mine].astype(BF16)
         for q in range(n):
-            raw[turn, 2 * rows :, q * STRIPE : (q + 1) * STRIPE] = dacc[
-                q * rows : (q + 1) * rows, o * STRIPE : (o + 1) * STRIPE
-            ].astype(BF16)
+            raw[turn, 2 * rows :, q * STRIPE : (q + 1) * STRIPE] = dacc[q * rows : (q + 1) * rows, stripe].astype(BF16)
 
 
 def backward_parts(g, u, dact):
@@ -225,9 +273,9 @@
 
 
 def top_kernel(n, chunks, tiles, layer, *refs):
-    a, a_t, dy, dy_t, h, wd, wg, wu, *refs = refs
-    dh, dh_t, g_out, last, squares_out, *refs = refs
-    gacc, uacc, dacc, da, raw, got, mid, squares, send, recv, local, wg_part, wu_part, w_sems = refs
+    a, a_t, dy, dy_t, h, wd, wg, wu, near_a, near_b, *refs = refs
+    dh, dh_t, g_out, last, squares_out, far_a, far_b, g_all, *refs = refs
+    gacc, uacc, dacc, da, raw, got, mid, squares, send, recv, local, wg_part, wu_part, w_sems, mine, e_send, e_recv = refs
     c, i = pl.program_id(0), pl.program_id(1)
     tm = a.shape[0]
     right, _, left = neighbours(n)
@@ -235,6 +283,23 @@
     slot, here, there = lax.rem(before, 2), lax.rem(c, 2), lax.rem(c + 1, 2)
     ring = Ring(n, raw, got.at[slot], mid, send.at[slot], recv.at[slot])
 
+    def moments():
+        for k, (near, far) in enumerate(((near_a, far_a), (near_b, far_b))):
+            half = far.shape[0] // 2
+            one, other = slice(0, half), slice(half, None)
+            yield remote(near.at[0, one], far.at[one], e_send.at[0, k], e_recv.at[0, k], right)
+            yield remote(near.at[1, other], far.at[other], e_send.at[1, k], e_recv.at[1, k], left)
+
+    def early():
+        yield remote(mine, g_all.at[0], e_send.at[2, 0], e_recv.at[2, 0], right)
+        yield remote(mine, g_all.at[1], e_send.at[2, 1], e_recv.at[2, 1], left)
+
+    def early_on():
+        half = mine.shape[0] // 2
+        one, other = pl.ds(0, half), pl.ds(half, half)
+        yield remote(g_all.at[0, one], g_all.at[2, one], e_send.at[3, 0], e_recv.at[3, 0], right)
+        yield remote(g_all.at[1, other], g_all.at[2, other], e_send.at[3, 1], e_recv.at[3, 1], left)
+
     def weights(c, slot):
         yield from fetch(chunks, layer, wg, wg_part.at[slot], w_sems.at[slot, 0], c)
         yield from fetch(chunks, layer, wu, wu_part.at[slot], w_sems.at[slot, 1], c)
@@ -246,11 +311,13 @@
             for copy in weights(c, here):
                 copy.start()
             greet((right, left))
+            for copy in moments():
+                copy.start()
             squares[...] = jnp.zeros_like(squares)
 
         @pl.when(c > 0)
         def _():
-            ring.begin()
+            ring.begin((0, 3))
 
         for copy in weights(c, here):
             copy.wait()
@@ -298,7 +365,33 @@
 
     pl.when(c < chunks - 1)(lambda: work(False))
     pl.when(c == chunks - 1)(lambda: work(True))
-    pl.when((c > 0) & (i == tiles // 2 - 1))(ring.go_on)
+    pl.when((c > 0) & (i == 0))(lambda: ring.begin((1, 4)))
+
+    @pl.when((c > 0) & (i == tiles // 2 - 1))
+    def _():
+        ring.go_on()
+
+        @pl.when(c == 1)
+        def _():
+            for copy in moments():
+                copy.wait()
+
+        @pl.when(c == EARLY + 2)
+        def _():
+            for copy in early():
+                copy.start()
+
+        @pl.when(c == EARLY + 3)
+        def _():
+            for copy in early():
+                copy.wait()
+            for copy in early_on():
+                copy.start()
+
+        @pl.when(c == EARLY + 4)
+        def _():
+            for copy in early_on():
+                copy.wait()
 
     @pl.when(i == tiles - 1)
     def _():
@@ -306,6 +399,10 @@
         def _():
             ring.end(g_out, squares)
             ring.sent(*range(6))
+
+        @pl.when(c == EARLY + 1)
+        def _():
+            mine[...] = g_out[0]
 
         lay_out(n, raw, gacc, uacc, dacc)
 
@@ -322,7 +419,7 @@
     return w_down.reshape(layers, n, ff // (n * STRIPE), STRIPE, d)
 
 
-def top(n, chunks, layer, a, a_t, dy, dy_t, h, w_gate, w_up, w_down, tm=1024):
+def top(n, chunks, layer, a, a_t, dy, dy_t, h, w_gate, w_up, w_down, near_a, near_b, tm=1024):
     t, d = a.shape
     width, tiles, block = n * STRIPE, t // tm, 3 * d // n
     row, col = pl.BlockSpec((tm, d), lambda c, i: (i, 0)), pl.BlockSpec((d, tm), lambda c, i: (0, i))
@@ -335,18 +432,22 @@
         jax.ShapeDtypeStruct((chunks - 1, block, width), BF16),
         jax.ShapeDtypeStruct((n, block, width), BF16),
         jax.ShapeDtypeStruct((8, width), F32),
+        jax.ShapeDtypeStruct(near_a.shape[1:], F32),
+        jax.ShapeDtypeStruct(near_b.shape[1:], F32),
+        jax.ShapeDtypeStruct((3, block, width), BF16),
     ]
     return pl.pallas_call(
         functools.partial(top_kernel, n, chunks, tiles, layer),
         grid=(chunks, tiles),
-        in_specs=[row, col, row, col, row_end, down] + [pl.BlockSpec(memory_space=pl.ANY)] * 2,
+        in_specs=[row, col, row, col, row_end, down] + [pl.BlockSpec(memory_space=pl.ANY)] * 4,
         out_specs=[
             row_end,
             col_end,
             pl.BlockSpec((1, block, width), lambda c, i: (jnp.maximum(c - 1, 0), 0, 0)),
             pl.BlockSpec(memory_space=pl.ANY),
             pl.BlockSpec((8, width), lambda c, i: (0, 0)),
-        ],
+        ]
+        + [pl.BlockSpec(memory_space=pl.ANY)] * 3,
         out_shape=shapes,
         scratch_shapes=[pltpu.VMEM((d, width), F32)] * 3
         + [
@@ -361,17 +462,20 @@
             pltpu.VMEM((2, d, width), BF16),
             pltpu.VMEM((2, d, width), BF16),
             pltpu.SemaphoreType.DMA((2, 2, n)),
+            pltpu.VMEM((block, width), BF16),
+            pltpu.SemaphoreType.DMA((4, 2)),
+            pltpu.SemaphoreType.DMA((4, 2)),
         ],
         compiler_params=pltpu.CompilerParams(vmem_limit_bytes=67043328, collective_id=0, has_side_effects=True),
         cost_estimate=cost(16 * t * d * width * chunks, chunks * nbytes(a, a_t, dy, dy_t)),
         name="top",
-    )(a, a_t, dy, dy_t, h, by_owner(n, w_down), w_gate, w_up)
+    )(a, a_t, dy, dy_t, h, by_owner(n, w_down), w_gate, w_up, near_a, near_b)
 
 
 def bottom_kernel(n, chunks, tiles, *refs):
     a_t, dy, dy_t, gate, up, *refs = refs
     wd, *refs = refs
-    first, squares_in, g_out, squares_out, gacc, uacc, dacc, raw, got, mid, squares, send, recv, local, others, to, fro = refs
+    first, squares_in, g_out, squares_out, gacc, uacc, dacc, raw, got, mid, squares, send, recv, local, all_squares, to, fro = refs
     c, i = pl.program_id(0), pl.program_id(1)
     right, opposite, left = neighbours(n)
 
@@ -424,14 +528,19 @@
         final = ring(c)
         final.end(g_out, squares)
         final.sent(*range(6))
+        me = lax.axis_index("dp")
+        all_squares[me] = squares[...]
         copies = [
-            remote(squares, others.at[k], to.at[k], fro.at[k], device) for k, device in enumerate((right, opposite, left))
+            remote(squares, all_squares.at[me], to.at[k], fro.at[k], device) for k, device in enumerate((right, opposite, left))
         ]
         for copy in copies:
             copy.start()
         for copy in copies:
             copy.wait()
-        squares_out[...] = squares[...] + (others[0] + others[1] + others[2])
+        total = all_squares[0]
+        for k in range(1, n):
+            total += all_squares[k]
+        squares_out[...] = total
 
 
 def bottom(n, chunks, layer, a_t, dy, dy_t, gate, up, w_down, first, squares, tm=1024):
@@ -462,7 +571,7 @@
             pltpu.SemaphoreType.DMA((chunks + 1, 6)),
             pltpu.SemaphoreType.DMA((chunks + 1, 6)),
             pltpu.SemaphoreType.DMA,
-            pltpu.VMEM((3, 8, width), F32),
+            pltpu.VMEM((n, 8, width), F32),
             pltpu.SemaphoreType.DMA((3,)),
             pltpu.SemaphoreType.DMA((3,)),
         ],
@@ -472,32 +581,48 @@
     )(a_t, dy, dy_t, gate, up, by_owner(n, w_down), first, squares)
 
 
+def clip(squares, count):
+    return jnp.minimum(1.0, 0.5 * lax.rsqrt(jnp.full((1, 1), jnp.sum(squares)) / count + 1e-30))
+
+
+def adamw(w, m, v, g):
+    m = 0.9 * m + 0.1 * g
+    v = 0.95 * v + 0.05 * g * g
+    old = w.astype(F32)
+    step = m * lax.rsqrt(v + 1e-8) + 0.1 * old
+    return (old - 0.02 * step).astype(BF16), m, v
+
+
+def upright(g):
+    return jnp.concatenate([g[:, q : q + STRIPE].T for q in range(0, g.shape[1], STRIPE)], 1)
+
+
 def adam_kernel(chunks, tall, count, squares, w, m, v, g_top, g_bottom, *refs):
     *w_out, m_out, v_out = refs
-    factor = jnp.minimum(1.0, 0.5 * lax.rsqrt(jnp.full((1, 1), jnp.sum(squares[...])) / count + 1e-30))
-
-    def work(layer, c, g):
-        at = pl.ds(pl.multiple_of(c * STRIPE, STRIPE), STRIPE)
-        i = (at, slice(None)) if tall else (slice(None), at)
-        g = g.astype(F32)
-        if tall:
-            g = jnp.concatenate([g[:, q : q + STRIPE].T for q in range(0, g.shape[1], STRIPE)], 1)
-        g = g * factor
-        m_new = 0.9 * m[layer, *i] + 0.1 * g
-        v_new = 0.95 * v[layer, *i] + 0.05 * g * g
-        old = w[layer, *i].astype(F32)
-        step = m_new * lax.rsqrt(v_new + 1e-8) + 0.1 * old
-        w_out[layer][i] = (old - 0.02 * step).astype(BF16)
-        m_out[layer, *i] = m_new
-        v_out[layer, *i] = v_new
-
-    @pl.loop(0, chunks - 1)
+    factor = clip(squares[...], count)
+
+    def work(layer, c, g, to):
+        def at(c):
+            rows = pl.ds(pl.multiple_of(c * STRIPE, STRIPE), STRIPE)
+            return (rows, slice(None)) if tall else (slice(None), rows)
+
+        g = upright(g.astype(F32)) if tall else g.astype(F32)
+        new, m_new, v_new = adamw(w[layer, *at(c)], m[layer, *at(c)], v[layer, *at(c)], g * factor)
+        if to is not None:
+            w_out[layer][at(to)] = new
+        m_out[layer, *at(c)] = m_new
+        v_out[layer, *at(c)] = v_new
+
+    work(0, EARLY, g_bottom[EARLY + 1], EARLY)
+    work(1, EARLY, g_top[EARLY], None)
+
+    @pl.loop(EARLY + 1, chunks - 1)
     def _(c):
-        work(0, c, g_bottom[c + 1])
-        work(1, c, g_top[c])
-
-    work(0, chunks - 1, g_bottom[chunks])
-    work(1, chunks - 1, g_bottom[0])
+        work(0, c, g_bottom[c + 1], c)
+        work(1, c, g_top[c], c - 1)
+
+    work(0, chunks - 1, g_bottom[chunks], chunks - 1)
+    work(1, chunks - 1, g_bottom[0], chunks - 2)
 
 
 def adam(me, squares, w, m, v, g_top, g_bottom, which, count, chunks, tall, first, blocks, begun):
@@ -505,7 +630,8 @@
     g_rows = g_top.shape[1] // 3
     g_width, width = (2 * STRIPE, 2 * g_rows) if tall else (STRIPE, STRIPE * chunks)
     block = pl.BlockSpec((layers, rows, width), lambda i, me: (0, 0, first + i))
-    out = [jax.ShapeDtypeStruct((rows, width * blocks), BF16)] * layers + [jax.ShapeDtypeStruct(m.shape, F32)] * 2
+    new = [(rows, width), (rows - STRIPE, width) if tall else (rows, width - STRIPE)]
+    out = [jax.ShapeDtypeStruct((r, c * blocks), BF16) for r, c in new] + [jax.ShapeDtypeStruct(m.shape, F32)] * 2
     fixed = list(begun)
 
     def body(me_ref, *refs):
@@ -520,7 +646,7 @@
             + [pl.BlockSpec((layers, rows, width), lambda i, me: (0, me[0], first + i)), block, block]
             + [pl.BlockSpec((g.shape[0], g_rows, g_width), lambda i, me: (0, which, first + i)) for g in (g_top, g_bottom)]
             + [pl.BlockSpec(memory_space=pl.ANY)] * len(fixed),
-            out_specs=[pl.BlockSpec((rows, width), lambda i, me: (0, i))] * layers + [block, block],
+            out_specs=[pl.BlockSpec(one, lambda i, me: (0, i)) for one in new] + [block, block],
         ),
         out_shape=out,
         input_output_aliases={7 + k: layers + k for k in range(len(fixed))},
@@ -531,51 +657,118 @@
     return outs[:layers], outs[layers:]
 
 
-def place_kernel(sources, me_ref, *refs):
-    pieces, out = refs[:sources], refs[-1]
-    k = pl.program_id(1)
-    for at, piece in enumerate(pieces):
-        pl.when(k == at)(lambda piece=piece: out.__setitem__(0, piece[...]))
-
-
-def place(me, shape, pieces, first, blocks, begun):
+def early_kernel(n, chunks, count, squares, *refs):
+    wg, wu, (wd, near_a, near_b, far_a, far_b, g_own, g_all), refs = refs[:n], refs[n : 2 * n], refs[2 * n : 2 * n + 7], refs[2 * n + 7 :]
+    outs, (across, down, sems) = refs[:3], refs[3:]
+    factor = clip(squares[...], count)
+    me = lax.axis_index("dp")
+    rows = near_a.shape[2]
+    held = ((near_a.at[2], near_b.at[2], g_own.at[0]), (near_a.at[1], near_b.at[1], g_all.at[1]))
+    held += ((far_a, far_b, g_all.at[2]), (near_a.at[0], near_b.at[0], g_all.at[0]))
+    for turn, (a, b, g) in enumerate(held):
+        o = lax.rem(me + turn, n)
+        at = pl.ds(pl.multiple_of(o * rows, rows), rows)
+        for k, w in enumerate((wg, wu)):
+            old = jnp.concatenate([one[0, at, :] for one in w], 1)
+            grad = g[k * rows : (k + 1) * rows, :].astype(F32) * factor
+            across[k, at, :] = adamw(old, a[2 * k], a[2 * k + 1], grad)[0]
+        grad = upright(g[2 * rows :, :].astype(F32)) * factor
+        down[o] = adamw(wd[0, o, 0], b[0], b[1], grad)[0]
+    copies = []
+    for o, s in enumerate(stripes(n, chunks, EARLY)):
+        for k in range(2):
+            copies.append((across.at[k, :, o * STRIPE : (o + 1) * STRIPE], outs[k].at[1, :, s]))
+        copies.append((down.at[o], outs[2].at[1, s, :]))
+    copies = [pltpu.make_async_copy(src, dst, sems.at[k]) for k, (src, dst) in enumerate(copies)]
+    for copy in copies:
+        copy.start()
+    for copy in copies:
+        copy.wait()
+
+
+def early_step(n, chunks, squares, weights, near_a, near_b, far_a, far_b, g_top, g_all, count):
+    w_gate, w_up, w_down = weights
+    d = w_gate.shape[1]
+    whole = lambda one: pl.BlockSpec(one.shape, lambda i: (0,) * one.ndim)
+    across = [pl.BlockSpec((1, d, STRIPE), lambda i, o=o: (1, 0, o * chunks + EARLY)) for o in range(n)]
+    down = pl.BlockSpec((1, n, 1, STRIPE, d), lambda i: (1, 0, EARLY, 0, 0))
+    own = pl.BlockSpec((1, *g_top.shape[1:]), lambda i: (EARLY, 0, 0))
+    arrays = (near_a, near_b, far_a, far_b)
+    return pl.pallas_call(
+        functools.partial(early_kernel, n, chunks, count),
+        grid=(1,),
+        in_specs=[whole(squares)] + across + across + [down] + [whole(one) for one in arrays] + [own, whole(g_all)],
+        out_specs=[pl.BlockSpec(memory_space=pl.ANY)] * 3,
+        out_shape=[jax.ShapeDtypeStruct(w.shape, BF16) for w in weights],
+        scratch_shapes=[
+            pltpu.VMEM((2, d, n * STRIPE), BF16),
+            pltpu.VMEM((n, STRIPE, d), BF16),
+            pltpu.SemaphoreType.DMA((3 * n,)),
+        ],
+        compiler_params=params(),
+        cost_estimate=cost(16 * 3 * d * n * STRIPE, nbytes(*arrays)),
+        name="early",
+    )(squares, *[w_gate] * n, *[w_up] * n, by_owner(n, w_down), *arrays, g_top, g_all)
+
+
+def place_kernel(n, pieces, regions, *refs):
+    arrays, out, sems = refs[: len(pieces)], refs[-2], refs[-1]
+    me = lax.axis_index("dp")
+    copies = []
+    for array, (layer, turn) in zip(arrays, pieces, strict=True):
+        o = lax.rem(me + turn, n)
+        for from_column, rows_before, columns, region in regions(layer):
+            rows = array.shape[0]
+            step = rows + rows_before
+            to = out.at[layer, pl.ds(pl.multiple_of(o * step + rows_before, 16), rows), region]
+            copies.append((array.at[:, from_column : from_column + columns], to))
+    copies = [pltpu.make_async_copy(src, dst, sems.at[k]) for k, (src, dst) in enumerate(copies)]
+    for copy in copies:
+        copy.start()
+    for copy in copies:
+        copy.wait()
+
+
+def place(n, chunks, whole, pieces, tall, first, blocks):
     arrays, where = zip(*pieces, strict=True)
-    rows, width = arrays[0].shape[0], arrays[0].shape[1] // blocks
-    n = shape[1] // rows
-
-    def at(j, k, me):
-        layer, turn = 0, 0
-        for i, (its_layer, its_turn) in enumerate(where):
-            layer, turn = jnp.where(k == i, its_layer, layer), jnp.where(k == i, its_turn, turn)
-        return layer, lax.rem(me[0] + turn, n), first + j
-
-    fixed = list(begun)
+    full = STRIPE * chunks
+
+    def regions(layer):
+        if tall:
+            columns = arrays[0].shape[1]
+            return [(0, layer * STRIPE, columns, slice(first * columns // blocks, (first + blocks) * columns // blocks))]
+        columns = full - layer * STRIPE
+        return [
+            (j * columns, 0, columns, slice((first + j) * full + layer * STRIPE, (first + j + 1) * full)) for j in range(blocks)
+        ]
+
     return pl.pallas_call(
-        functools.partial(place_kernel, len(arrays)),
-        grid_spec=pltpu.PrefetchScalarGridSpec(
-            num_scalar_prefetch=1,
-            grid=(blocks, len(arrays)),
-            in_specs=[pl.BlockSpec((rows, width), lambda j, k, me: (0, j))] * len(arrays)
-            + [pl.BlockSpec(memory_space=pl.ANY)] * len(fixed),
-            out_specs=pl.BlockSpec((1, rows, width), at),
-        ),
-        out_shape=jax.ShapeDtypeStruct(shape, arrays[0].dtype),
-        input_output_aliases={1 + len(arrays): 0} if fixed else {},
+        functools.partial(place_kernel, n, where, regions),
+        grid=(1,),
+        in_specs=[pl.BlockSpec(one.shape, lambda i: (0, 0)) for one in arrays] + [pl.BlockSpec(memory_space=pl.ANY)],
+        out_specs=pl.BlockSpec(memory_space=pl.ANY),
+        out_shape=jax.ShapeDtypeStruct(whole.shape, whole.dtype),
+        input_output_aliases={len(arrays): 0},
+        scratch_shapes=[pltpu.SemaphoreType.DMA((len(arrays) * blocks,))],
         compiler_params=params(),
         cost_estimate=cost(arrays[0].size, 4 * nbytes(*arrays)),
         name="place",
-    )(me, *arrays, *fixed)
-
-
-def send_around(n, own):
+    )(*arrays, whole)
+
+
+def send_around(n, own, swap):
     right, left = [(i, (i + 1) % n) for i in range(n)], [(i, (i - 1) % n) for i in range(n)]
 
     def send(one, way):
         return lax.ppermute(one, "dp", way)
 
-    l0, r1 = send(own[0], right), send(own[1], left)
-    l1, r0 = send(own[1], right), send(own[0], left)
-    return (l0, l1), (r0, r1), lambda: (send(l0, right), send(r1, left))
+    def in_order(a, b):
+        return (b, a) if swap else (a, b)
+
+    a, b = in_order(*own)
+    left_a, right_b = send(a, right), send(b, left)
+    left_b, right_a = send(b, right), send(a, left)
+    return in_order(left_a, left_b), in_order(right_a, right_b), lambda: in_order(send(left_a, right), send(right_b, left))
 
 
 def solution(mesh):
@@ -586,26 +779,29 @@
         chunks = w_gate.shape[2] // (n * STRIPE)
         me = lax.axis_index("dp").astype(jnp.int32).reshape(1)
 
-        gate, up, a0_t, h1, a1, a1_t, dy_t = forward(n, chunks, x, dy, w_gate, w_up, w_down)
-        dh, dh_t, g_top, last, squares = top(n, chunks, 1, a1, a1_t, dy, dy_t, h1, w_gate, w_up, w_down)
+        weights, moments = (w_gate, w_up, w_down), ((m_gate, v_gate), (m_up, v_up), (m_down, v_down))
+        *parts, near_a, near_b = forward(n, chunks, x, dy, *weights, sum(moments, ()))
+        gate, up, a0_t, h1, a1, a1_t, dy_t = parts
+        *parts, far_a, far_b, g_all = top(n, chunks, 1, a1, a1_t, dy, dy_t, h1, *weights, near_a, near_b)
+        dh, dh_t, g_top, last, squares = parts
         g_bottom, squares = bottom(n, chunks, 0, a0_t, dh, dh_t, gate, up, w_down, last, squares)
 
-        states = ((w_gate, m_gate, v_gate), (w_up, m_up, v_up), (w_down, m_down, v_down))
-        moments, whole, sent, count = [[], [], []], [[], [], []], [], 3 * w_gate.size
-        for which, first, blocks in PIECES:
-            own, moments[which] = adam(
-                me, squares, *states[which], g_top, g_bottom, which, count, chunks, which == 2, first, blocks, moments[which]
+        new, sent, count = [[], [], []], [], 3 * w_gate.size
+        for which, first, blocks, swap in PIECES:
+            own, new[which] = adam(
+                me, squares, weights[which], *moments[which], g_top, g_bottom, which, count, chunks, which == 2, first, blocks, new[which]
             )
             squares = lax.optimization_barrier((squares, *own))[0]
-            sent.append((own, *send_around(n, own)))
-        for k, (which, first, blocks) in enumerate(PIECES):
+            sent.append((own, *send_around(n, own, swap)))
+        whole = list(early_step(n, chunks, squares, weights, near_a, near_b, far_a, far_b, g_top, g_all, count))
+        for k, (which, first, blocks, swap) in enumerate(PIECES):
             own, left, right, _ = sent[k]
             near = [(one, (layer, turn)) for turn, pair in ((0, own), (n - 1, left), (1, right)) for layer, one in enumerate(pair)]
-            whole[which] = [place(me, states[which][0].shape, near, first, blocks, whole[which])]
-        for k, (which, first, blocks) in enumerate(PIECES):
+            whole[which] = place(n, chunks, whole[which], near, which == 2, first, blocks)
+        for k, (which, first, blocks, swap) in enumerate(PIECES):
             far = [(one, (layer, 2)) for layer, one in enumerate(sent[k][3]())]
-            whole[which] = [place(me, states[which][0].shape, far, first, blocks, whole[which])]
-        return (*(one[0] for one in whole), *(one[0] for one in moments), *(one[1] for one in moments))
+            whole[which] = place(n, chunks, whole[which], far, which == 2, first, blocks)
+        return (*whole, *(one[0] for one in new), *(one[1] for one in new))
 
     seq, part, rows = P(("rep", "dp"), None, None), P("rep", None, None), P("rep", "dp", None)
     state = P(None, "dp", None)

time: 706 us -> 683 us (0.967)
  waiting for transfers between devices: 169 us -> 149 us
  Pallas kernels: 506 us -> 497 us
  starting transfers between devices: 23.8 us -> 30.9 us
    ppermute x30, waiting for transfers between devices: 169 us -> 149 us  [send(): return lax.ppermute(one, 'dp', way)]
    pallas_call x10 -> x11, Pallas kernels: 54.1 us -> 43.7 us  [the longest x10 32.2 us: place(): pl.pallas_call(functools.partial(place_kernel, n, where, regions), grid=(...]
    ppermute x30, starting transfers between devices: 23.8 us -> 30.9 us  [send(): return lax.ppermute(one, 'dp', way)]
  transfers between devices with their start and end apart: 30 -> 30, of which waited for: 20 -> 16; matrix products, arithmetic and copies ran while one was open for 0% -> 0% of each run, Pallas kernels for 7% -> 6%
where the time goes in v1:
time: 683 us; the launch traced here: 682 us
  Pallas kernels  497 us (73%)
  waiting for transfers between devices  149 us (22%)
  starting transfers between devices  30.9 us (5%)
    pallas_call x1, Pallas kernels, top(): pl.pallas_call(functools.partial(top_kernel, n, chunks, tiles, layer), gr...  190 us
    pallas_call x1, Pallas kernels, bottom(): pl.pallas_call(functools.partial(bottom_kernel, n, chunks, tiles), grid=(...  149 us
    ppermute x30, waiting for transfers between devices, send(): return lax.ppermute(one, 'dp', way)  149 us
    pallas_call x1, Pallas kernels, forward(): pl.pallas_call(functools.partial(forward_kernel, n, chunks, tiles), grid=...  76.3 us
    pallas_call x5, Pallas kernels, adam(): pl.pallas_call(body, grid_spec=pltpu.PrefetchScalarGridSpec(num_scalar_pr...  37.3 us
    pallas_call x10, Pallas kernels, place(): pl.pallas_call(functools.partial(place_kernel, n, where, regions), grid=(...  32.2 us
    ppermute x30, starting transfers between devices, send(): return lax.ppermute(one, 'dp', way)  30.9 us
  transfers between devices with their start and end apart: 30, of which 16 were waited for; matrix products, arithmetic and copies ran while one was open for 0% of the time, Pallas kernels for 6%

profile of v1, /device:TPU:112, one launch (start us, length us, event | category | flops | bytes accessed | tf_op | source)
XLA Modules:
  0.0 682.3 jit_solution(5294323216752921350)
XLA Ops:
  0.6 76.3 %forward.1 = (f32[6,4096,512]{2,1,0:T(8,128)}, f32[6,4096,512]{2,1,0:T(8,128)}, bf16[768,4096]{1,0:T(8,128)(2,1)}, bf16[4096,768]{1,0:T(8,128)(2,1)}, bf16[4096,...) custom-call(bf16[4096,768]{1,0:T(8,128)(2,1)} %bitcast.7, ...), custom_call_target="tpu_custom_call" | custom-call | flops 57982058496 | bytes 139198464 | tf_op jit(solution)/shard_map/forward/pallas_call | solution.py:142
  77.0 190.0 %top.1 = (bf16[4096,768]{1,0:T(8,128)(2,1)}, bf16[768,4096]{1,0:T(8,128)(2,1)}, bf16[5,576,512]{2,1,0:T(8,128)(2,1)}, bf16[4,576,512]{2,1,0:T(8,128)(2,1)}, f32[...) custom-call(bf16[4096,768]{1,0:T(8,128)(2,1)} %get-tuple-element.57.refs_0_, ...), custom_call_target="tpu_custom_call" | custom-call | flops 154618822656 | bytes 150994944 | tf_op jit(solution)/shard_map/top/pallas_call | solution.py:439
  266.9 149.3 %bottom.1 = (bf16[7,576,512]{2,1,0:T(8,128)(2,1)}, f32[8,512]{1,0:T(8,128)}) custom-call(bf16[768,4096]{1,0:T(8,128)(2,1)} %get-tuple-element.56.refs_0_, bf16[4096,768]{1,0:T(8,128)(2,1)} %get-tuple-element.63.refs_1_, bf16[768,4096]{1,0:T(8,128)(2,1)} %get-tuple-element.64.refs_2_, f32[6,4096,512]{2,1,0:T(8,128)} %get-tuple-element.65.refs_3_, ...), custom_call_target="tpu_custom_call" | custom-call | flops 77309411328 | bytes 213909504 | tf_op jit(solution)/shard_map/bottom/pallas_call | solution.py:556
  416.3 4.4 adam.5
  420.7 9.3 %adam.6 = (bf16[192,2304]{1,0:T(8,128)(2,1)}, bf16[192,1920]{1,0:T(8,128)(2,1)}, f32[2,192,3072]{2,1,0:T(8,128)}, f32[2,192,3072]{2,1,0:T(8,128)}) custom-call(s32[1]{0:T(128)} %bitcast.me_ref, f32[8,512]{1,0:T(8,128)} %get-tuple-element.90.refs_0_.squares, bf16[2,768,3072]{2,1,0:T(8,128)(2,1)} %refs_3_.11, ...), custom_call_target="tpu_custom_call", output_to_operand_aliasing={{2}: (7, {}), {3}: (8, {})} | custom-call | flops 14155776 | bytes 19464192 | tf_op jit(solution)/shard_map/adam/pallas_call | solution.py:640
  430.0 9.5 %adam.7 = (bf16[768,768]{1,0:T(8,128)(2,1)}, bf16[640,768]{1,0:T(8,128)(2,1)}, f32[2,768,768]{2,1,0:T(8,128)}, f32[2,768,768]{2,1,0:T(8,128)}) custom-call(s32[1]{0:T(128)} %bitcast.me_ref, f32[8,512]{1,0:T(8,128)} %get-tuple-element.90.refs_0_.squares, bf16[2,3072,768]{2,1,0:T(8,128)(2,1)} %refs_1_.8, f32[2,768,768]{2,1,0:T(8,128)} %refs_2_.8, ...), custom_call_target="tpu_custom_call" | custom-call | flops 18874368 | bytes 25952256 | tf_op jit(solution)/shard_map/adam/pallas_call | solution.py:640
  439.5 9.3 %adam.8 = (bf16[192,2304]{1,0:T(8,128)(2,1)}, bf16[192,1920]{1,0:T(8,128)(2,1)}, f32[2,192,3072]{2,1,0:T(8,128)}, f32[2,192,3072]{2,1,0:T(8,128)}) custom-call(s32[1]{0:T(128)} %bitcast.me_ref, f32[8,512]{1,0:T(8,128)} %get-tuple-element.90.refs_0_.squares, bf16[2,768,3072]{2,1,0:T(8,128)(2,1)} %refs_7_.5, f32[2,192,3072]{2,1,0:T(8,128)} %refs_2_.10, ...), custom_call_target="tpu_custom_call" | custom-call | flops 14155776 | bytes 19464192 | tf_op jit(solution)/shard_map/adam/pallas_call | solution.py:640
  448.9 4.8 adam.9
  453.7 1.8 collective-permute-start.14
  455.4 0.2 collective-permute-start.20
  455.7 0.5 collective-permute-start.10
  456.2 1.6 collective-permute-start.12
  457.9 1.6 collective-permute-start.6
  459.5 2.5 collective-permute-done.14.refs_5_
  461.9 3.9 collective-permute-done.20.refs_3_
  465.8 0.0 collective-permute-start.4
  465.8 5.2 collective-permute-done.10.refs_3_
  471.0 0.0 collective-permute-start.21
  471.0 0.0 collective-permute-done.6.refs_5_
  471.0 0.2 collective-permute-start.11
  471.1 6.2 collective-permute-done.12.refs_2_
  477.4 0.0 collective-permute-start.23
  477.4 19.2 %collective-permute-done.4.refs_2_ = bf16[192,768]{1,0:T(8,128)(2,1)S(1)} collective-permute-done((bf16[192,768]{1,0:T(8,128)(2,1)S(1)}, bf16[192,768]{1,0:T(8,128)(2,1)S(1)}, u32[]{:S(2)}, u32[]{:S(2)}) %collective-permute-start.4) | collective-permute-done | bytes 294944 | tf_op jit(solution)/shard_map/ppermute | solution.py:763
  496.6 0.0 collective-permute-start.5
  496.6 3.2 collective-permute-start.15
  499.8 0.1 collective-permute-start.7
  499.9 6.2 collective-permute-done.15.refs_1_
  506.2 3.7 collective-permute-start.2
  509.9 1.6 collective-permute-done.7.refs_1_
  511.5 3.8 collective-permute-start.16
  515.3 1.6 collective-permute-start
  516.9 10.4 %collective-permute-done.2.refs_5_ = bf16[192,1920]{1,0:T(8,128)(2,1)} collective-permute-done((bf16[192,1920]{1,0:T(8,128)(2,1)S(1)}, bf16[192,1920]{1,0:T(8,128)(2,1)}, u32[]{:S(2)}, u32[]{:S(2)}) %collective-permute-start.2) | collective-permute-done | bytes 737312 | tf_op jit(solution)/shard_map/ppermute | solution.py:763
  527.2 3.8 collective-permute-start.9
  531.0 1.4 collective-permute-done.8.refs_3_
  532.5 2.0 collective-permute-start.24
  534.5 11.7 %collective-permute-done.16.refs_4_ = bf16[192,2304]{1,0:T(8,128)(2,1)S(1)} collective-permute-done((bf16[192,2304]{1,0:T(8,128)(2,1)S(1)}, bf16[192,2304]{1,0:T(8,128)(2,1)S(1)}, u32[]{:S(2)}, u32[]{:S(2)}) %collective-permute-start.16) | collective-permute-done | bytes 884768 | tf_op jit(solution)/shard_map/ppermute | solution.py:763
  546.2 5.3 collective-permute-done.22.refs_2_
  551.5 19.0 %collective-permute-done.refs_2_ = bf16[192,2304]{1,0:T(8,128)(2,1)} collective-permute-done((bf16[192,2304]{1,0:T(8,128)(2,1)S(1)}, bf16[192,2304]{1,0:T(8,128)(2,1)}, u32[]{:S(2)}, u32[]{:S(2)}) %collective-permute-start) | collective-permute-done | bytes 884768 | tf_op jit(solution)/shard_map/ppermute | solution.py:763
  570.5 2.0 collective-permute-start.29
  572.5 0.0 collective-permute-start.19
  572.5 19.0 %collective-permute-done.26.refs_3_ = bf16[640,768]{1,0:T(8,128)(2,1)} collective-permute-done((bf16[640,768]{1,0:T(8,128)(2,1)}, bf16[640,768]{1,0:T(8,128)(2,1)}, u32[]{:S(2)}, u32[]{:S(2)}) %collective-permute-start.26) | collective-permute-done | bytes 983072 | tf_op jit(solution)/shard_map/ppermute | solution.py:763
  591.6 2.0 collective-permute-start.17
  593.6 0.5 collective-permute-start.25
  594.1 17.5 %collective-permute-done.29.refs_5_ = bf16[640,768]{1,0:T(8,128)(2,1)S(1)} collective-permute-done((bf16[640,768]{1,0:T(8,128)(2,1)}, bf16[640,768]{1,0:T(8,128)(2,1)S(1)}, u32[]{:S(2)}, u32[]{:S(2)}) %collective-permute-start.29) | collective-permute-done | bytes 983072 | tf_op jit(solution)/shard_map/ppermute | solution.py:763
  611.6 5.1 collective-permute-done.28.refs_2_
  616.7 1.1 copy-done.3
  617.8 14.7 %collective-permute-done.19.refs_1_ = bf16[192,1920]{1,0:T(8,128)(2,1)S(1)} collective-permute-done((bf16[192,1920]{1,0:T(8,128)(2,1)S(1)}, bf16[192,1920]{1,0:T(8,128)(2,1)S(1)}, u32[]{:S(2)}, u32[]{:S(2)}) %collective-permute-start.19) | collective-permute-done | bytes 737312 | tf_op jit(solution)/shard_map/ppermute | solution.py:763
  632.5 2.0 collective-permute-start.3
  634.6 0.1 collective-permute-start.13
  634.7 0.8 copy-done.9
  635.5 11.5 %early.1 = (bf16[2,768,3072]{2,1,0:T(8,128)(2,1)}, bf16[2,768,3072]{2,1,0:T(8,128)(2,1)}, bf16[2,3072,768]{2,1,0:T(8,128)(2,1)}) custom-call(f32[8,512]{1,0:T(8,128)} %get-tuple-element.90.refs_0_.squares, bf16[2,768,3072]{2,1,0:T(8,128)(2,1)} %refs_3_.11, bf16[2,768,3072]{2,1,0:T(8,128)(2,1)} %refs_3_.11, bf16[2,768,3072]{2,1,0:T(8,128)(2,1)} %refs_3_.11, ...), custom_call_target="tpu_custom_call" | custom-call | flops 18874368 | bytes 9437184 | tf_op jit(solution)/shard_map/early/pallas_call | solution.py:697
  647.0 2.7 place.10.refs_6_
  649.7 4.7 place.14.refs_6_
  654.4 4.7 place.11.refs_2_
  659.1 2.7 place.15.refs_2_
  661.8 1.8 place.12.refs_2_
  663.6 5.7 place.18.refs_2_
  669.3 2.6 place.16.refs_2_
  672.0 0.7 copy-done.21
  672.7 1.8 place.17
  674.6 0.9 copy-done.10
  675.5 2.6 place.13
  678.1 1.1 copy-done.2
  679.2 2.9 place.19
  (69 shorter events, 0.1 us)
Async XLA Ops:
  448.8 17.0 %copy-start.16 = (bf16[192,768]{1,0:T(8,128)(2,1)S(1)}, bf16[192,768]{1,0:T(8,128)(2,1)}, u32[]{:S(2)}) copy-start(bf16[192,768]{1,0:T(8,128)(2,1)} %get-tuple-element.72.refs_0_) | copy-start | bytes 884740
  448.8 57.4 %copy-start.11 = (bf16[192,1920]{1,0:T(8,128)(2,1)S(1)}, bf16[192,1920]{1,0:T(8,128)(2,1)}, u32[]{:S(2)}) copy-start(bf16[192,1920]{1,0:T(8,128)(2,1)} %get-tuple-element.78.refs_1_) | copy-start | bytes 2211844
  448.8 62.6 %copy-start.6 = (bf16[192,2304]{1,0:T(8,128)(2,1)S(1)}, bf16[192,2304]{1,0:T(8,128)(2,1)}, u32[]{:S(2)}) copy-start(bf16[192,2304]{1,0:T(8,128)(2,1)} %get-tuple-element.83.refs_0_) | copy-start | bytes 2654212
  448.8 66.4 %copy-start.5 = (bf16[192,2304]{1,0:T(8,128)(2,1)S(1)}, bf16[192,2304]{1,0:T(8,128)(2,1)}, u32[]{:S(2)}) copy-start(bf16[192,2304]{1,0:T(8,128)(2,1)} %get-tuple-element.77.refs_0_) | copy-start | bytes 2654212
  448.9 83.6 %copy-start = (bf16[768,768]{1,0:T(8,128)(2,1)S(1)}, bf16[768,768]{1,0:T(8,128)(2,1)}, u32[]{:S(2)}) copy-start(bf16[768,768]{1,0:T(8,128)(2,1)} %get-tuple-element.80.refs_0_) | copy-start | bytes 3538948
  453.7 8.3 %collective-permute-start.14 = (bf16[192,640]{1,0:T(8,128)(2,1)}, bf16[192,640]{1,0:T(8,128)(2,1)S(1)}, u32[]{:S(2)}, u32[]{:S(2)}) collective-permute-start(bf16[192,640]{1,0:T(8,128)(2,1)} %get-tuple-element.89.refs_1_), channel_id=1, source_target_pairs={{0,3},{1,0},{2,1},{3,2},{4,7},{5,4},{6,5},{7,6},{8,11},{9,8},{10,9... | collective-permute-start | bytes 737288 | tf_op jit(solution)/shard_map/ppermute | solution.py:763
  455.4 10.4 %collective-permute-start.20 = (bf16[192,640]{1,0:T(8,128)(2,1)}, bf16[192,640]{1,0:T(8,128)(2,1)}, u32[]{:S(2)}, u32[]{:S(2)}) collective-permute-start(bf16[192,640]{1,0:T(8,128)(2,1)} %get-tuple-element.89.refs_1_), channel_id=1, source_target_pairs={{0,1},{1,2},{2,3},{3,0},{4,5},{5,6},{6,7},{7,4},{8,9},{9,10},{10,1... | collective-permute-start | bytes 737288 | tf_op jit(solution)/shard_map/ppermute | solution.py:763
  455.7 15.3 %collective-permute-start.10 = (bf16[192,640]{1,0:T(8,128)(2,1)}, bf16[192,640]{1,0:T(8,128)(2,1)S(1)}, u32[]{:S(2)}, u32[]{:S(2)}) collective-permute-start(bf16[192,640]{1,0:T(8,128)(2,1)} %get-tuple-element.73.refs_1_), channel_id=1, source_target_pairs={{0,1},{1,2},{2,3},{3,0},{4,5},{5,6},{6,7},{7,4},{8,9},{9,10},{10,1... | collective-permute-start | bytes 737288 | tf_op jit(solution)/shard_map/ppermute | solution.py:763
  456.2 21.2 %collective-permute-start.12 = (bf16[192,768]{1,0:T(8,128)(2,1)}, bf16[192,768]{1,0:T(8,128)(2,1)}, u32[]{:S(2)}, u32[]{:S(2)}) collective-permute-start(bf16[192,768]{1,0:T(8,128)(2,1)} %get-tuple-element.88.refs_0_), channel_id=1, source_target_pairs={{0,1},{1,2},{2,3},{3,0},{4,5},{5,6},{6,7},{7,4},{8,9},{9,10},{10,1... | collective-permute-start | bytes 884744 | tf_op jit(solution)/shard_map/ppermute | solution.py:763
  457.9 13.1 %collective-permute-start.6 = (bf16[192,640]{1,0:T(8,128)(2,1)}, bf16[192,640]{1,0:T(8,128)(2,1)S(1)}, u32[]{:S(2)}, u32[]{:S(2)}) collective-permute-start(bf16[192,640]{1,0:T(8,128)(2,1)} %get-tuple-element.73.refs_1_), channel_id=1, source_target_pairs={{0,3},{1,0},{2,1},{3,2},{4,7},{5,4},{6,5},{7,6},{8,11},{9,8},{10,9... | collective-permute-start | bytes 737288 | tf_op jit(solution)/shard_map/ppermute | solution.py:763
  461.9 47.9 %copy-start.22 = (bf16[192,640]{1,0:T(8,128)(2,1)}, bf16[192,640]{1,0:T(8,128)(2,1)S(1)}, u32[]{:S(2)}) copy-start(bf16[192,640]{1,0:T(8,128)(2,1)S(1)} %collective-permute-done.14.refs_5_) | copy-start | bytes 737284
  461.9 53.3 %collective-permute-start.18 = (bf16[192,1920]{1,0:T(8,128)(2,1)}, bf16[192,1920]{1,0:T(8,128)(2,1)S(1)}, u32[]{:S(2)}, u32[]{:S(2)}) collective-permute-start(bf16[192,1920]{1,0:T(8,128)(2,1)} %get-tuple-element.84.refs_1_), channel_id=1, source_target_pairs={{0,1},{1,2},{2,3},{3,0},{4,5},{5,6},{6,7},{7,4},{8,9},{9,10},{10,1... | collective-permute-start | bytes 2211848 | tf_op jit(solution)/shard_map/ppermute | solution.py:763
  465.8 30.8 %collective-permute-start.4 = (bf16[192,768]{1,0:T(8,128)(2,1)S(1)}, bf16[192,768]{1,0:T(8,128)(2,1)S(1)}, u32[]{:S(2)}, u32[]{:S(2)}) collective-permute-start(bf16[192,768]{1,0:T(8,128)(2,1)S(1)} %copy-done.16), channel_id=1, source_target_pairs={{0,1},{1,2},{2,3},{3,0},{4,5},{5,6},{6,7},{7,4},{8,9},{9,10},{10,1... | collective-permute-start | bytes 884744 | tf_op jit(solution)/shard_map/ppermute | solution.py:763
  471.0 6.4 copy-start.23
  471.0 25.6 %collective-permute-start.21 = (bf16[192,768]{1,0:T(8,128)(2,1)}, bf16[192,768]{1,0:T(8,128)(2,1)S(1)}, u32[]{:S(2)}, u32[]{:S(2)}) collective-permute-start(bf16[192,768]{1,0:T(8,128)(2,1)} %get-tuple-element.88.refs_0_), channel_id=1, source_target_pairs={{0,3},{1,0},{2,1},{3,2},{4,7},{5,4},{6,5},{7,6},{8,11},{9,8},{10,9... | collective-permute-start | bytes 884744 | tf_op jit(solution)/shard_map/ppermute | solution.py:763
  471.0 75.2 %copy-start.24 = (bf16[192,640]{1,0:T(8,128)(2,1)}, bf16[192,640]{1,0:T(8,128)(2,1)S(1)}, u32[]{:S(2)}) copy-start(bf16[192,640]{1,0:T(8,128)(2,1)S(1)} %collective-permute-done.6.refs_5_) | copy-start | bytes 737284
  471.0 28.9 %collective-permute-start.11 = (bf16[192,768]{1,0:T(8,128)(2,1)S(1)}, bf16[192,768]{1,0:T(8,128)(2,1)S(1)}, u32[]{:S(2)}, u32[]{:S(2)}) collective-permute-start(bf16[192,768]{1,0:T(8,128)(2,1)S(1)} %copy-done.16), channel_id=1, source_target_pairs={{0,3},{1,0},{2,1},{3,2},{4,7},{5,4},{6,5},{7,6},{8,11},{9,8},{10,9... | collective-permute-start | bytes 884744 | tf_op jit(solution)/shard_map/ppermute | solution.py:763
  477.4 37.9 %collective-permute-start.23 = (bf16[192,1920]{1,0:T(8,128)(2,1)}, bf16[192,1920]{1,0:T(8,128)(2,1)S(1)}, u32[]{:S(2)}, u32[]{:S(2)}) collective-permute-start(bf16[192,1920]{1,0:T(8,128)(2,1)} %get-tuple-element.84.refs_1_), channel_id=1, source_target_pairs={{0,3},{1,0},{2,1},{3,2},{4,7},{5,4},{6,5},{7,6},{8,11},{9,8},{10,9... | collective-permute-start | bytes 2211848 | tf_op jit(solution)/shard_map/ppermute | solution.py:763
  496.6 49.6 %copy-start.18 = (bf16[192,768]{1,0:T(8,128)(2,1)}, bf16[192,768]{1,0:T(8,128)(2,1)S(1)}, u32[]{:S(2)}) copy-start(bf16[192,768]{1,0:T(8,128)(2,1)S(1)} %collective-permute-done.4.refs_2_) | copy-start | bytes 884740
  496.6 14.9 %collective-permute-start.5 = (bf16[192,768]{1,0:T(8,128)(2,1)S(1)}, bf16[192,768]{1,0:T(8,128)(2,1)S(1)}, u32[]{:S(2)}, u32[]{:S(2)}) collective-permute-start(bf16[192,768]{1,0:T(8,128)(2,1)S(1)} %collective-permute-done.4.refs_2_), channel_id=1, source_target_pairs={{0,1},{1,2},{2,3},{3,0},{4,5},{5,6},{6,7},{7,4},{8,9},{9,10},{10,1... | collective-permute-start | bytes 884744 | tf_op jit(solution)/shard_map/ppermute | solution.py:763
  496.6 13.3 %copy-start.17 = (bf16[192,768]{1,0:T(8,128)(2,1)}, bf16[192,768]{1,0:T(8,128)(2,1)S(1)}, u32[]{:S(2)}) copy-start(bf16[192,768]{1,0:T(8,128)(2,1)S(1)} %collective-permute-done.21.refs_4_) | copy-start | bytes 884740
  496.6 9.6 %collective-permute-start.15 = (bf16[192,640]{1,0:T(8,128)(2,1)S(1)}, bf16[192,640]{1,0:T(8,128)(2,1)S(1)}, u32[]{:S(2)}, u32[]{:S(2)}) collective-permute-start(bf16[192,640]{1,0:T(8,128)(2,1)S(1)} %collective-permute-done.14.refs_5_), channel_id=1, source_target_pairs={{0,3},{1,0},{2,1},{3,2},{4,7},{5,4},{6,5},{7,6},{8,11},{9,8},{10,9... | collective-permute-start | bytes 737288 | tf_op jit(solution)/shard_map/ppermute | solution.py:763
  499.8 10.0 %copy-start.20 = (bf16[192,768]{1,0:T(8,128)(2,1)}, bf16[192,768]{1,0:T(8,128)(2,1)S(1)}, u32[]{:S(2)}) copy-start(bf16[192,768]{1,0:T(8,128)(2,1)S(1)} %collective-permute-done.11.refs_4_) | copy-start | bytes 884740
  499.8 11.6 %collective-permute-start.7 = (bf16[192,640]{1,0:T(8,128)(2,1)S(1)}, bf16[192,640]{1,0:T(8,128)(2,1)S(1)}, u32[]{:S(2)}, u32[]{:S(2)}) collective-permute-start(bf16[192,640]{1,0:T(8,128)(2,1)S(1)} %collective-permute-done.6.refs_5_), channel_id=1, source_target_pairs={{0,3},{1,0},{2,1},{3,2},{4,7},{5,4},{6,5},{7,6},{8,11},{9,8},{10,9... | collective-permute-start | bytes 737288 | tf_op jit(solution)/shard_map/ppermute | solution.py:763
  506.2 40.0 %copy-start.25 = (bf16[192,640]{1,0:T(8,128)(2,1)}, bf16[192,640]{1,0:T(8,128)(2,1)S(1)}, u32[]{:S(2)}) copy-start(bf16[192,640]{1,0:T(8,128)(2,1)S(1)} %collective-permute-done.15.refs_1_) | copy-start | bytes 737284
  506.2 21.1 %collective-permute-start.2 = (bf16[192,1920]{1,0:T(8,128)(2,1)S(1)}, bf16[192,1920]{1,0:T(8,128)(2,1)}, u32[]{:S(2)}, u32[]{:S(2)}) collective-permute-start(bf16[192,1920]{1,0:T(8,128)(2,1)S(1)} %copy-done.11), channel_id=1, source_target_pairs={{0,3},{1,0},{2,1},{3,2},{4,7},{5,4},{6,5},{7,6},{8,11},{9,8},{10,9... | collective-permute-start | bytes 2211848 | tf_op jit(solution)/shard_map/ppermute | solution.py:763
  511.4 19.6 %copy-start.26 = (bf16[192,640]{1,0:T(8,128)(2,1)}, bf16[192,640]{1,0:T(8,128)(2,1)S(1)}, u32[]{:S(2)}) copy-start(bf16[192,640]{1,0:T(8,128)(2,1)S(1)} %collective-permute-done.7.refs_1_) | copy-start | bytes 737284
  511.4 21.0 %collective-permute-start.8 = (bf16[192,1920]{1,0:T(8,128)(2,1)S(1)}, bf16[192,1920]{1,0:T(8,128)(2,1)S(1)}, u32[]{:S(2)}, u32[]{:S(2)}) collective-permute-start(bf16[192,1920]{1,0:T(8,128)(2,1)S(1)} %copy-done.11), channel_id=1, source_target_pairs={{0,1},{1,2},{2,3},{3,0},{4,5},{5,6},{6,7},{7,4},{8,9},{9,10},{10,1... | collective-permute-start | bytes 2211848 | tf_op jit(solution)/shard_map/ppermute | solution.py:763
  511.5 34.8 %copy-start.19 = (bf16[192,768]{1,0:T(8,128)(2,1)}, bf16[192,768]{1,0:T(8,128)(2,1)S(1)}, u32[]{:S(2)}) copy-start(bf16[192,768]{1,0:T(8,128)(2,1)S(1)} %collective-permute-done.5.refs_0_) | copy-start | bytes 884740
  511.5 34.7 %collective-permute-start.16 = (bf16[192,2304]{1,0:T(8,128)(2,1)S(1)}, bf16[192,2304]{1,0:T(8,128)(2,1)S(1)}, u32[]{:S(2)}, u32[]{:S(2)}) collective-permute-start(bf16[192,2304]{1,0:T(8,128)(2,1)S(1)} %copy-done.6), channel_id=1, source_target_pairs={{0,3},{1,0},{2,1},{3,2},{4,7},{5,4},{6,5},{7,6},{8,11},{9,8},{10,9... | collective-permute-start | bytes 2654216 | tf_op jit(solution)/shard_map/ppermute | solution.py:763
  515.2 120.2 %copy-start.12 = (bf16[192,1920]{1,0:T(8,128)(2,1)}, bf16[192,1920]{1,0:T(8,128)(2,1)S(1)}, u32[]{:S(2)}) copy-start(bf16[192,1920]{1,0:T(8,128)(2,1)S(1)} %collective-permute-done.18.refs_3_) | copy-start | bytes 2211844
  515.2 36.3 %collective-permute-start.22 = (bf16[192,2304]{1,0:T(8,128)(2,1)S(1)}, bf16[192,2304]{1,0:T(8,128)(2,1)}, u32[]{:S(2)}, u32[]{:S(2)}) collective-permute-start(bf16[192,2304]{1,0:T(8,128)(2,1)S(1)} %copy-done.6), channel_id=1, source_target_pairs={{0,1},{1,2},{2,3},{3,0},{4,5},{5,6},{6,7},{7,4},{8,9},{9,10},{10,1... | collective-permute-start | bytes 2654216 | tf_op jit(solution)/shard_map/ppermute | solution.py:763
  515.3 1.6 copy-start.13
  515.3 55.2 %collective-permute-start = (bf16[192,2304]{1,0:T(8,128)(2,1)S(1)}, bf16[192,2304]{1,0:T(8,128)(2,1)}, u32[]{:S(2)}, u32[]{:S(2)}) collective-permute-start(bf16[192,2304]{1,0:T(8,128)(2,1)S(1)} %copy-done.5), channel_id=1, source_target_pairs={{0,1},{1,2},{2,3},{3,0},{4,5},{5,6},{6,7},{7,4},{8,9},{9,10},{10,1... | collective-permute-start | bytes 2654216 | tf_op jit(solution)/shard_map/ppermute | solution.py:763
  527.2 45.3 %collective-permute-start.9 = (bf16[192,2304]{1,0:T(8,128)(2,1)S(1)}, bf16[192,2304]{1,0:T(8,128)(2,1)S(1)}, u32[]{:S(2)}, u32[]{:S(2)}) collective-permute-start(bf16[192,2304]{1,0:T(8,128)(2,1)S(1)} %copy-done.5), channel_id=1, source_target_pairs={{0,3},{1,0},{2,1},{3,2},{4,7},{5,4},{6,5},{7,6},{8,11},{9,8},{10,9... | collective-permute-start | bytes 2654216 | tf_op jit(solution)/shard_map/ppermute | solution.py:763
  532.5 40.1 %copy-start.14 = (bf16[192,1920]{1,0:T(8,128)(2,1)}, bf16[192,1920]{1,0:T(8,128)(2,1)S(1)}, u32[]{:S(2)}) copy-start(bf16[192,1920]{1,0:T(8,128)(2,1)S(1)} %collective-permute-done.8.refs_3_) | copy-start | bytes 2211844
  532.5 61.1 %collective-permute-start.24 = (bf16[768,768]{1,0:T(8,128)(2,1)S(1)}, bf16[768,768]{1,0:T(8,128)(2,1)S(1)}, u32[]{:S(2)}, u32[]{:S(2)}) collective-permute-start(bf16[768,768]{1,0:T(8,128)(2,1)S(1)} %copy-done), channel_id=1, source_target_pairs={{0,3},{1,0},{2,1},{3,2},{4,7},{5,4},{6,5},{7,6},{8,11},{9,8},{10,9... | collective-permute-start | bytes 3538952 | tf_op jit(solution)/shard_map/ppermute | solution.py:763
  546.2 86.3 %copy-start.7 = (bf16[192,2304]{1,0:T(8,128)(2,1)}, bf16[192,2304]{1,0:T(8,128)(2,1)S(1)}, u32[]{:S(2)}) copy-start(bf16[192,2304]{1,0:T(8,128)(2,1)S(1)} %collective-permute-done.16.refs_4_) | copy-start | bytes 2654212
  546.2 45.4 %collective-permute-start.26 = (bf16[640,768]{1,0:T(8,128)(2,1)}, bf16[640,768]{1,0:T(8,128)(2,1)}, u32[]{:S(2)}, u32[]{:S(2)}) collective-permute-start(bf16[640,768]{1,0:T(8,128)(2,1)} %get-tuple-element.81.refs_1_), channel_id=1, source_target_pairs={{0,1},{1,2},{2,3},{3,0},{4,5},{5,6},{6,7},{7,4},{8,9},{9,10},{10,1... | collective-permute-start | bytes 2949128 | tf_op jit(solution)/shard_map/ppermute | solution.py:763
  551.5 65.2 %collective-permute-start.28 = (bf16[768,768]{1,0:T(8,128)(2,1)S(1)}, bf16[768,768]{1,0:T(8,128)(2,1)S(1)}, u32[]{:S(2)}, u32[]{:S(2)}) collective-permute-start(bf16[768,768]{1,0:T(8,128)(2,1)S(1)} %copy-done), channel_id=1, source_target_pairs={{0,1},{1,2},{2,3},{3,0},{4,5},{5,6},{6,7},{7,4},{8,9},{9,10},{10,1... | collective-permute-start | bytes 3538952 | tf_op jit(solution)/shard_map/ppermute | solution.py:763
  570.5 41.1 %collective-permute-start.29 = (bf16[640,768]{1,0:T(8,128)(2,1)}, bf16[640,768]{1,0:T(8,128)(2,1)S(1)}, u32[]{:S(2)}, u32[]{:S(2)}) collective-permute-start(bf16[640,768]{1,0:T(8,128)(2,1)} %get-tuple-element.81.refs_1_), channel_id=1, source_target_pairs={{0,3},{1,0},{2,1},{3,2},{4,7},{5,4},{6,5},{7,6},{8,11},{9,8},{10,9... | collective-permute-start | bytes 2949128 | tf_op jit(solution)/shard_map/ppermute | solution.py:763
  572.5 62.0 %copy-start.8 = (bf16[192,2304]{1,0:T(8,128)(2,1)}, bf16[192,2304]{1,0:T(8,128)(2,1)S(1)}, u32[]{:S(2)}) copy-start(bf16[192,2304]{1,0:T(8,128)(2,1)S(1)} %collective-permute-done.9.refs_4_) | copy-start | bytes 2654212
  572.5 60.0 %collective-permute-start.19 = (bf16[192,1920]{1,0:T(8,128)(2,1)S(1)}, bf16[192,1920]{1,0:T(8,128)(2,1)S(1)}, u32[]{:S(2)}, u32[]{:S(2)}) collective-permute-start(bf16[192,1920]{1,0:T(8,128)(2,1)S(1)} %collective-permute-done.18.refs_3_), channel_id=1, source_target_pairs={{0,1},{1,2},{2,3},{3,0},{4,5},{5,6},{6,7},{7,4},{8,9},{9,10},{10,1... | collective-permute-start | bytes 2211848 | tf_op jit(solution)/shard_map/ppermute | solution.py:763
  591.6 43.0 %collective-permute-start.17 = (bf16[192,2304]{1,0:T(8,128)(2,1)S(1)}, bf16[192,2304]{1,0:T(8,128)(2,1)S(1)}, u32[]{:S(2)}, u32[]{:S(2)}) collective-permute-start(bf16[192,2304]{1,0:T(8,128)(2,1)S(1)} %collective-permute-done.16.refs_4_), channel_id=1, source_target_pairs={{0,3},{1,0},{2,1},{3,2},{4,7},{5,4},{6,5},{7,6},{8,11},{9,8},{10,9... | collective-permute-start | bytes 2654216 | tf_op jit(solution)/shard_map/ppermute | solution.py:763
  593.6 53.4 %copy-start.1 = (bf16[768,768]{1,0:T(8,128)(2,1)}, bf16[768,768]{1,0:T(8,128)(2,1)S(1)}, u32[]{:S(2)}) copy-start(bf16[768,768]{1,0:T(8,128)(2,1)S(1)} %collective-permute-done.24.refs_4_) | copy-start | bytes 3538948
  593.6 84.5 %collective-permute-start.25 = (bf16[768,768]{1,0:T(8,128)(2,1)S(1)}, bf16[768,768]{1,0:T(8,128)(2,1)S(1)}, u32[]{:S(2)}, u32[]{:S(2)}) collective-permute-start(bf16[768,768]{1,0:T(8,128)(2,1)S(1)} %collective-permute-done.24.refs_4_), channel_id=1, source_target_pairs={{0,3},{1,0},{2,1},{3,2},{4,7},{5,4},{6,5},{7,6},{8,11},{9,8},{10,9... | collective-permute-start | bytes 3538952 | tf_op jit(solution)/shard_map/ppermute | solution.py:763
  611.6 6.2 copy-start.4
  611.6 66.5 %collective-permute-start.27 = (bf16[640,768]{1,0:T(8,128)(2,1)}, bf16[640,768]{1,0:T(8,128)(2,1)}, u32[]{:S(2)}, u32[]{:S(2)}) collective-permute-start(bf16[640,768]{1,0:T(8,128)(2,1)} %collective-permute-done.26.refs_3_), channel_id=1, source_target_pairs={{0,1},{1,2},{2,3},{3,0},{4,5},{5,6},{6,7},{7,4},{8,9},{9,10},{10,1... | collective-permute-start | bytes 2949128 | tf_op jit(solution)/shard_map/ppermute | solution.py:763
  616.7 1.1 copy-start.3
  617.8 56.7 %collective-permute-start.1 = (bf16[192,2304]{1,0:T(8,128)(2,1)}, bf16[192,2304]{1,0:T(8,128)(2,1)S(1)}, u32[]{:S(2)}, u32[]{:S(2)}) collective-permute-start(bf16[192,2304]{1,0:T(8,128)(2,1)} %collective-permute-done.refs_2_), channel_id=1, source_target_pairs={{0,1},{1,2},{2,3},{3,0},{4,5},{5,6},{6,7},{7,4},{8,9},{9,10},{10,1... | collective-permute-start | bytes 2654216 | tf_op jit(solution)/shard_map/ppermute | solution.py:763
  632.5 2.9 copy-start.15
  632.5 42.0 %collective-permute-start.3 = (bf16[192,1920]{1,0:T(8,128)(2,1)}, bf16[192,1920]{1,0:T(8,128)(2,1)}, u32[]{:S(2)}, u32[]{:S(2)}) collective-permute-start(bf16[192,1920]{1,0:T(8,128)(2,1)} %collective-permute-done.2.refs_5_), channel_id=1, source_target_pairs={{0,3},{1,0},{2,1},{3,2},{4,7},{5,4},{6,5},{7,6},{8,11},{9,8},{10,9... | collective-permute-start | bytes 2211848 | tf_op jit(solution)/shard_map/ppermute | solution.py:763
  634.6 0.9 copy-start.9
  634.6 37.4 %collective-permute-start.13 = (bf16[192,768]{1,0:T(8,128)(2,1)}, bf16[192,768]{1,0:T(8,128)(2,1)S(1)}, u32[]{:S(2)}, u32[]{:S(2)}) collective-permute-start(bf16[192,768]{1,0:T(8,128)(2,1)} %collective-permute-done.12.refs_2_), channel_id=1, source_target_pairs={{0,1},{1,2},{2,3},{3,0},{4,5},{5,6},{6,7},{7,4},{8,9},{9,10},{10,1... | collective-permute-start | bytes 884744 | tf_op jit(solution)/shard_map/ppermute | solution.py:763
  671.9 0.7 copy-start.21
  674.5 1.0 copy-start.10
  678.1 1.1 copy-start.2

commit v2 on v1

--- a/solution.py
+++ b/solution.py
@@ -11,8 +11,8 @@
 F32, BF16 = jnp.float32, jnp.bfloat16
 STRIPE = 128
 VMEM_LIMIT = 60 << 20
-EARLY = 0
-PIECES = ((0, 0, 1, False), (0, 1, 3, False), (2, 0, 2, True), (1, 0, 3, True), (1, 3, 1, False))
+EARLY_DOWN = 2
+PIECES = ((0, 0, 1, False), (0, 1, 3, False), (2, 0, 2, True), (1, 0, 3, False), (1, 3, 1, False))
 
 
 def dot(a, b):
@@ -63,18 +63,19 @@
 
     def packing():
         for k, ref in enumerate(moments[:4]):
-            for o, s in enumerate(stripes(n, chunks, EARLY)):
+            for o, s in enumerate(stripes(n, chunks, 0)):
                 yield pltpu.make_async_copy(
                     ref.at[1, :, s], pack_a.at[k, :, o * STRIPE : (o + 1) * STRIPE], packed.at[k * n + o]
                 )
         for k, ref in enumerate(moments[4:]):
-            rows = slice(EARLY * STRIPE, (EARLY + 1) * STRIPE)
-            yield pltpu.make_async_copy(ref.at[1, rows, :], pack_b.at[k], packed.at[4 * n + k])
+            yield pltpu.make_async_copy(ref.at[1, : pack_b.shape[1], :], pack_b.at[k], packed.at[4 * n + k])
 
     def copies():
+        parts = ((pack_a, near_a, ()), (pack_b.at[0], near_b, (0,)), (pack_b.at[1, :STRIPE], near_b, (1, slice(0, STRIPE))))
+        for k, (part, near, where) in enumerate(parts):
+            yield remote(part, near.at[0, *where], send.at[k], recv.at[k], right)
+            yield remote(part, near.at[1, *where], send.at[3 + k], recv.at[3 + k], left)
         for k, (part, near) in enumerate(((pack_a, near_a), (pack_b, near_b))):
-            yield remote(part, near.at[0], send.at[k], recv.at[k], right)
-            yield remote(part, near.at[1], send.at[2 + k], recv.at[2 + k], left)
             yield pltpu.make_async_copy(part, near.at[2], own.at[k])
 
     def finish():
@@ -134,7 +135,7 @@
     row = lambda at: pl.BlockSpec((tm, d), lambda m: (at(m), 0))
     col = lambda at: pl.BlockSpec((d, tm), lambda m: (0, at(m)))
     wide = pl.BlockSpec((chunks, tm, width), lambda m: (0, here(m), 0))
-    pack_a, pack_b = (4, d // n, width), (2, STRIPE, d)
+    pack_a, pack_b = (4, d // n, width), (2, EARLY_DOWN * STRIPE, d)
     out = [jax.ShapeDtypeStruct((chunks, t, width), F32)] * 2
     out += [jax.ShapeDtypeStruct(s, BF16) for s in ((d, t), (t, d), (t, d), (d, t), (d, t))]
     out += [jax.ShapeDtypeStruct((3, *s), F32) for s in (pack_a, pack_b)]
@@ -156,8 +157,8 @@
             pltpu.VMEM(pack_b, F32),
             pltpu.SemaphoreType.DMA((4 * n + 2,)),
             pltpu.SemaphoreType.DMA((2,)),
-            pltpu.SemaphoreType.DMA((4,)),
-            pltpu.SemaphoreType.DMA((4,)),
+            pltpu.SemaphoreType.DMA((6,)),
+            pltpu.SemaphoreType.DMA((6,)),
         ],
         compiler_params=params(collective_id=2, has_side_effects=True),
         cost_estimate=cost(6 * t * d * ff, nbytes(*out)),
@@ -273,42 +274,67 @@
 
 
 def top_kernel(n, chunks, tiles, layer, *refs):
-    a, a_t, dy, dy_t, h, wd, wg, wu, near_a, near_b, *refs = refs
-    dh, dh_t, g_out, last, squares_out, far_a, far_b, g_all, *refs = refs
-    gacc, uacc, dacc, da, raw, got, mid, squares, send, recv, local, wg_part, wu_part, w_sems, mine, e_send, e_recv = refs
+    wholes, (h, wd, wg, wu, near_a, near_b), refs = refs[:4], refs[4:10], refs[10:]
+    dh, dh_t, g_out, last, squares_out, far_a, far_b, late, *refs = refs
+    alls, refs = refs[:2], refs[2:]
+    gacc, uacc, dacc, da, raw, got, mid, squares, send, recv, local, wg_part, wu_part, w_sems, *mines, e_send, e_recv = refs[:-5]
+    slots, loaded = refs[-5:-1], refs[-1]
     c, i = pl.program_id(0), pl.program_id(1)
-    tm = a.shape[0]
+    tm = h.shape[0]
     right, _, left = neighbours(n)
     before = jnp.maximum(c - 1, 0)
     slot, here, there = lax.rem(before, 2), lax.rem(c, 2), lax.rem(c + 1, 2)
     ring = Ring(n, raw, got.at[slot], mid, send.at[slot], recv.at[slot])
 
     def moments():
-        for k, (near, far) in enumerate(((near_a, far_a), (near_b, far_b))):
-            half = far.shape[0] // 2
-            one, other = slice(0, half), slice(half, None)
-            yield remote(near.at[0, one], far.at[one], e_send.at[0, k], e_recv.at[0, k], right)
-            yield remote(near.at[1, other], far.at[other], e_send.at[1, k], e_recv.at[1, k], left)
-
-    def early():
-        yield remote(mine, g_all.at[0], e_send.at[2, 0], e_recv.at[2, 0], right)
-        yield remote(mine, g_all.at[1], e_send.at[2, 1], e_recv.at[2, 1], left)
-
-    def early_on():
-        half = mine.shape[0] // 2
-        one, other = pl.ds(0, half), pl.ds(half, half)
-        yield remote(g_all.at[0, one], g_all.at[2, one], e_send.at[3, 0], e_recv.at[3, 0], right)
-        yield remote(g_all.at[1, other], g_all.at[2, other], e_send.at[3, 1], e_recv.at[3, 1], left)
+        half, rows = far_a.shape[0] // 2, 3 * STRIPE // 2
+        parts = (
+            (near_a, far_a, (slice(0, half),), 0),
+            (near_b, far_b, (0, slice(0, rows)), 0),
+            (near_a, far_a, (slice(half, None),), 1),
+            (near_b, far_b, (0, slice(rows, None)), 1),
+            (near_b, far_b, (1, slice(0, STRIPE)), 1),
+        )
+        for k, (near, far, where, side) in enumerate(parts):
+            yield remote(near.at[side, *where], far.at[*where], e_send.at[8, k], e_recv.at[8, k], (right, left)[side])
+
+    block = mines[0].shape[0]
+    across = 2 * block // 3
+    rounds = (
+        (near_b.at[2, 1, STRIPE:], late, 0, STRIPE, 1),
+        (mines[0].at[across:], alls[0], across, block - across, 2),
+        (mines[0].at[:across], alls[0], 0, across, 3),
+        (mines[1], alls[1], 0, block - across, 4),
+    )
+
+    def out(k):
+        mine, every, start, rows, _ = rounds[k]
+        for side in range(2):
+            to = every.at[side, pl.ds(start, rows)]
+            yield remote(mine, to, e_send.at[2 * k, side], e_recv.at[2 * k, side], (right, left)[side])
+
+    def on(k):
+        _, every, start, rows, _ = rounds[k]
+        half, at = rows // 2, 2 * k + 1
+        for side in range(2):
+            part = pl.ds(start + side * half, half)
+            yield remote(every.at[side, part], every.at[2, part], e_send.at[at, side], e_recv.at[at, side], (right, left)[side])
 
     def weights(c, slot):
         yield from fetch(chunks, layer, wg, wg_part.at[slot], w_sems.at[slot, 0], c)
         yield from fetch(chunks, layer, wu, wu_part.at[slot], w_sems.at[slot, 1], c)
 
+    def loads(i):
+        at, slot = pl.ds(pl.multiple_of(i * tm, tm), tm), lax.rem(i, 2)
+        for k, (whole, part) in enumerate(zip(wholes, slots, strict=True)):
+            source = whole.at[:, at] if k % 2 else whole.at[at]
+            yield pltpu.make_async_copy(source, part.at[slot], loaded.at[k, slot])
+
     @pl.when(i == 0)
     def _():
         @pl.when(c == 0)
         def _():
-            for copy in weights(c, here):
+            for copy in (*weights(c, here), *loads(i)):
                 copy.start()
             greet((right, left))
             for copy in moments():
@@ -327,6 +353,14 @@
             for copy in weights(c + 1, there):
                 copy.start()
 
+    @pl.when((c < chunks - 1) | (i < tiles - 1))
+    def _():
+        for load in loads(lax.rem(i + 1, tiles)):
+            load.start()
+
+    for load in loads(i):
+        load.wait()
+    a, a_t, dy, dy_t = (part.at[lax.rem(i, 2)] for part in slots)
     rows = pl.ds(pl.multiple_of(i * tm, tm), tm)
     pair = 2
 
@@ -371,27 +405,37 @@
     def _():
         ring.go_on()
 
-        @pl.when(c == 1)
-        def _():
-            for copy in moments():
-                copy.wait()
-
-        @pl.when(c == EARLY + 2)
-        def _():
-            for copy in early():
-                copy.start()
-
-        @pl.when(c == EARLY + 3)
-        def _():
-            for copy in early():
-                copy.wait()
-            for copy in early_on():
-                copy.start()
-
-        @pl.when(c == EARLY + 4)
-        def _():
-            for copy in early_on():
-                copy.wait()
+    @pl.when(i == tiles // 2)
+    def _():
+        for k, (*_, first) in enumerate(rounds):
+
+            @pl.when(c == first)
+            def _(k=k):
+                for copy in out(k):
+                    copy.start()
+
+            @pl.when(c == first + 1)
+            def _(k=k):
+                for copy in out(k):
+                    copy.wait()
+                for copy in on(k):
+                    copy.start()
+
+            if first + 2 < chunks:
+
+                @pl.when(c == first + 2)
+                def _(k=k):
+                    for copy in on(k):
+                        copy.wait()
+
+    @pl.when((c == chunks - 1) & (i == tiles - 1))
+    def _():
+        for copy in moments():
+            copy.wait()
+        for k, (*_, first) in enumerate(rounds):
+            if first + 2 >= chunks:
+                for copy in on(k):
+                    copy.wait()
 
     @pl.when(i == tiles - 1)
     def _():
@@ -400,9 +444,11 @@
             ring.end(g_out, squares)
             ring.sent(*range(6))
 
-        @pl.when(c == EARLY + 1)
-        def _():
-            mine[...] = g_out[0]
+        for k, mine in enumerate(mines):
+
+            @pl.when(c == k + 1)
+            def _(mine=mine):
+                mine[...] = g_out[0, g_out.shape[1] - mine.shape[0] :]
 
         lay_out(n, raw, gacc, uacc, dacc)
 
@@ -422,7 +468,7 @@
 def top(n, chunks, layer, a, a_t, dy, dy_t, h, w_gate, w_up, w_down, near_a, near_b, tm=1024):
     t, d = a.shape
     width, tiles, block = n * STRIPE, t // tm, 3 * d // n
-    row, col = pl.BlockSpec((tm, d), lambda c, i: (i, 0)), pl.BlockSpec((d, tm), lambda c, i: (0, i))
+    assert tiles % 2 == 0
     at_end = lambda c, i: jnp.where(c == chunks - 1, i, 0)
     row_end, col_end = pl.BlockSpec((tm, d), lambda c, i: (at_end(c, i), 0)), pl.BlockSpec((d, tm), lambda c, i: (0, at_end(c, i)))
     down = pl.BlockSpec((1, n, 1, STRIPE, d), lambda c, i: (layer, 0, c, 0, 0))
@@ -434,12 +480,14 @@
         jax.ShapeDtypeStruct((8, width), F32),
         jax.ShapeDtypeStruct(near_a.shape[1:], F32),
         jax.ShapeDtypeStruct(near_b.shape[1:], F32),
+        jax.ShapeDtypeStruct((3, STRIPE, d), F32),
         jax.ShapeDtypeStruct((3, block, width), BF16),
+        jax.ShapeDtypeStruct((3, block // 3, width), BF16),
     ]
     return pl.pallas_call(
         functools.partial(top_kernel, n, chunks, tiles, layer),
         grid=(chunks, tiles),
-        in_specs=[row, col, row, col, row_end, down] + [pl.BlockSpec(memory_space=pl.ANY)] * 4,
+        in_specs=[pl.BlockSpec(memory_space=pl.ANY)] * 4 + [row_end, down] + [pl.BlockSpec(memory_space=pl.ANY)] * 4,
         out_specs=[
             row_end,
             col_end,
@@ -447,7 +495,7 @@
             pl.BlockSpec(memory_space=pl.ANY),
             pl.BlockSpec((8, width), lambda c, i: (0, 0)),
         ]
-        + [pl.BlockSpec(memory_space=pl.ANY)] * 3,
+        + [pl.BlockSpec(memory_space=pl.ANY)] * 5,
         out_shape=shapes,
         scratch_shapes=[pltpu.VMEM((d, width), F32)] * 3
         + [
@@ -463,9 +511,12 @@
             pltpu.VMEM((2, d, width), BF16),
             pltpu.SemaphoreType.DMA((2, 2, n)),
             pltpu.VMEM((block, width), BF16),
-            pltpu.SemaphoreType.DMA((4, 2)),
-            pltpu.SemaphoreType.DMA((4, 2)),
-        ],
+            pltpu.VMEM((block // 3, width), BF16),
+            pltpu.SemaphoreType.DMA((9, 5)),
+            pltpu.SemaphoreType.DMA((9, 5)),
+        ]
+        + [pltpu.VMEM((2, *one), BF16) for one in ((tm, d), (d, tm)) * 2]
+        + [pltpu.SemaphoreType.DMA((4, 2))],
         compiler_params=pltpu.CompilerParams(vmem_limit_bytes=67043328, collective_id=0, has_side_effects=True),
         cost_estimate=cost(16 * t * d * width * chunks, chunks * nbytes(a, a_t, dy, dy_t)),
         name="top",
@@ -473,37 +524,55 @@
 
 
 def bottom_kernel(n, chunks, tiles, *refs):
-    a_t, dy, dy_t, gate, up, *refs = refs
-    wd, *refs = refs
-    first, squares_in, g_out, squares_out, gacc, uacc, dacc, raw, got, mid, squares, send, recv, local, all_squares, to, fro = refs
+    wholes, (wd, first, squares_in, g_out, squares_out), refs = refs[:5], refs[5:10], refs[10:]
+    gacc, uacc, dacc, raw, got, mid, squares, send, recv, local, all_squares, to, fro, *slots, loaded = refs
     c, i = pl.program_id(0), pl.program_id(1)
     right, opposite, left = neighbours(n)
+    tm = slots[0].shape[2]
+
+    def loads(c, i):
+        at, slot = pl.ds(pl.multiple_of(i * tm, tm), tm), lax.rem(i, 2)
+        tiles_at = ((slice(None), at), (at,), (slice(None), at), (c, at), (c, at))
+        for k, (whole, where, part) in enumerate(zip(wholes, tiles_at, slots, strict=True)):
+            yield pltpu.make_async_copy(whole.at[*where], part.at[slot], loaded.at[k, slot])
 
     def ring(k):
         slot = lax.rem(k, 2)
         return Ring(n, raw.at[slot], got.at[k], mid.at[slot], send.at[k], recv.at[k])
 
+    held = pltpu.make_async_copy(first, raw.at[0], local)
+
     @pl.when((c == 0) & (i == 0))
     def _():
-        copy = pltpu.make_async_copy(first, raw.at[0], local)
-        copy.start()
-        greet((right, opposite, left))
+        hail((right, opposite, left))
+        held.start()
+        for load in loads(c, i):
+            load.start()
         squares[...] = squares_in[...]
-        copy.wait()
-
-    @pl.when(i == 0)
+        pl.semaphore_wait(pltpu.get_barrier_semaphore(), 3)
+        Ring(n, first, got.at[0], mid.at[0], send.at[0], recv.at[0]).begin((0, 3))
+
+    @pl.when((c > 0) & (i == 0))
     def _():
         ring(c).begin((0, 3))
 
+    @pl.when((c < chunks - 1) | ((c == chunks - 1) & (i < tiles - 1)))
+    def _():
+        for load in loads(jnp.where(i == tiles - 1, c + 1, c), lax.rem(i + 1, tiles)):
+            load.start()
+
     @pl.when(c < chunks)
     def _():
+        for load in loads(c, i):
+            load.wait()
+        a_t, dy, dy_t, gate, up = (part.at[lax.rem(i, 2)] for part in slots)
         pair = 2
         parts = []
         for j in range(0, n, pair):
             w = wd[0, j : j + pair, 0].reshape(pair * STRIPE, wd.shape[4])
             parts.append((slice(j * STRIPE, (j + pair) * STRIPE), dot_nt(dy[...], w)))
         for to, dact in parts:
-            act, dg, du = backward_parts(gate[0, :, to], up[0, :, to], dact)
+            act, dg, du = backward_parts(gate[:, to], up[:, to], dact)
             for acc, left, right in ((gacc, a_t, dg), (uacc, a_t, du), (dacc, dy_t, act)):
                 acc[:, to] = jnp.where(i == 0, 0.0, acc[:, to]) + dot(left[...], right)
 
@@ -515,6 +584,7 @@
             before.end(g_out, squares)
             before.sent(*range(6))
 
+        pl.when(c == 0)(held.wait)
         ring(c).begin((1, 4))
 
     pl.when(i == tiles // 2)(lambda: ring(c).go_on())
@@ -546,17 +616,14 @@
 def bottom(n, chunks, layer, a_t, dy, dy_t, gate, up, w_down, first, squares, tm=1024):
     d, t = a_t.shape
     width, tiles, block = n * STRIPE, t // tm, 3 * d // n
-    tile = lambda c, i: jnp.where(c < chunks, i, tiles - 1)
-    chunk = lambda c: jnp.minimum(c, chunks - 1)
-    row, col = pl.BlockSpec((tm, d), lambda c, i: (tile(c, i), 0)), pl.BlockSpec((d, tm), lambda c, i: (0, tile(c, i)))
-    wide = pl.BlockSpec((1, tm, width), lambda c, i: (chunk(c), tile(c, i), 0))
+    assert tiles % 2 == 0
     small = pl.BlockSpec((8, width), lambda c, i: (0, 0))
-    down = pl.BlockSpec((1, n, 1, STRIPE, d), lambda c, i: (layer, 0, chunk(c), 0, 0))
+    down = pl.BlockSpec((1, n, 1, STRIPE, d), lambda c, i: (layer, 0, jnp.minimum(c, chunks - 1), 0, 0))
     done = lambda c, i: jnp.where((c == chunks) & (i == tiles - 1), chunks, jnp.maximum(c - 1, 0))
     return pl.pallas_call(
         functools.partial(bottom_kernel, n, chunks, tiles),
         grid=(chunks + 1, tiles),
-        in_specs=[col, row, col, wide, wide, down, pl.BlockSpec(memory_space=pl.ANY), small],
+        in_specs=[pl.BlockSpec(memory_space=pl.ANY)] * 5 + [down, pl.BlockSpec(memory_space=pl.ANY), small],
         out_specs=[pl.BlockSpec((1, block, width), lambda c, i: (done(c, i), 0, 0)), small],
         out_shape=[
             jax.ShapeDtypeStruct((chunks + 1, block, width), BF16),
@@ -574,7 +641,10 @@
             pltpu.VMEM((n, 8, width), F32),
             pltpu.SemaphoreType.DMA((3,)),
             pltpu.SemaphoreType.DMA((3,)),
-        ],
+        ]
+        + [pltpu.VMEM((2, *one), BF16) for one in ((d, tm), (tm, d), (d, tm))]
+        + [pltpu.VMEM((2, tm, width), F32)] * 2
+        + [pltpu.SemaphoreType.DMA((5, 2))],
         compiler_params=pltpu.CompilerParams(vmem_limit_bytes=VMEM_LIMIT, collective_id=1, has_side_effects=True),
         cost_estimate=cost(8 * t * d * width * chunks, nbytes(gate, up) + chunks * nbytes(a_t, dy, dy_t)),
         name="bottom",
@@ -613,16 +683,20 @@
         m_out[layer, *at(c)] = m_new
         v_out[layer, *at(c)] = v_new
 
-    work(0, EARLY, g_bottom[EARLY + 1], EARLY)
-    work(1, EARLY, g_top[EARLY], None)
-
-    @pl.loop(EARLY + 1, chunks - 1)
+    early = EARLY_DOWN if tall else 1
+
+    @pl.loop(0, early)
     def _(c):
         work(0, c, g_bottom[c + 1], c)
-        work(1, c, g_top[c], c - 1)
+        work(1, c, g_top[c], None)
+
+    @pl.loop(early, chunks - 1)
+    def _(c):
+        work(0, c, g_bottom[c + 1], c)
+        work(1, c, g_top[c], c - early)
 
     work(0, chunks - 1, g_bottom[chunks], chunks - 1)
-    work(1, chunks - 1, g_bottom[0], chunks - 2)
+    work(1, chunks - 1, g_bottom[0], chunks - 1 - early)
 
 
 def adam(me, squares, w, m, v, g_top, g_bottom, which, count, chunks, tall, first, blocks, begun):
@@ -630,7 +704,7 @@
     g_rows = g_top.shape[1] // 3
     g_width, width = (2 * STRIPE, 2 * g_rows) if tall else (STRIPE, STRIPE * chunks)
     block = pl.BlockSpec((layers, rows, width), lambda i, me: (0, 0, first + i))
-    new = [(rows, width), (rows - STRIPE, width) if tall else (rows, width - STRIPE)]
+    new = [(rows, width), (rows - EARLY_DOWN * STRIPE, width) if tall else (rows, width - STRIPE)]
     out = [jax.ShapeDtypeStruct((r, c * blocks), BF16) for r, c in new] + [jax.ShapeDtypeStruct(m.shape, F32)] * 2
     fixed = list(begun)
 
@@ -658,27 +732,51 @@
 
 
 def early_kernel(n, chunks, count, squares, *refs):
-    wg, wu, (wd, near_a, near_b, far_a, far_b, g_own, g_all), refs = refs[:n], refs[n : 2 * n], refs[2 * n : 2 * n + 7], refs[2 * n + 7 :]
-    outs, (across, down, sems) = refs[:3], refs[3:]
+    wg, wu, refs = refs[:n], refs[n : 2 * n], refs[2 * n :]
+    (wd, near_a, near_b, far_a, far_b, late, g_top, g_all, g_all_down), refs = refs[:9], refs[9:]
+    outs, (a, b, g, g_down, loaded, across, down, sems) = refs[:3], refs[3:]
+    rows = g_down.shape[1]
+    g_near, g_near_down = g_top.at[0], g_top.at[1, 2 * rows :, :]
+    loads = []
+    of_chunk = [pl.ds(k * STRIPE, STRIPE) for k in range(EARLY_DOWN)]
+    parts = [(a.at[turn], b.at[turn, 0], b.at[turn, 1, of_chunk[0]], b.at[turn, 1, of_chunk[1]], g.at[turn], g_down.at[turn]) for turn in range(n)]
+
+    def held(near_a, near_b, late, *sums):
+        return near_a, near_b.at[0], near_b.at[1, of_chunk[0]], late, *sums
+
+    sources = (
+        held(near_a.at[2], near_b.at[2], near_b.at[2, 1, of_chunk[1]], g_near, g_near_down),
+        held(near_a.at[1], near_b.at[1], late.at[1], g_all.at[1], g_all_down.at[1]),
+        held(far_a, far_b, late.at[2], g_all.at[2], g_all_down.at[2]),
+        held(near_a.at[0], near_b.at[0], late.at[0], g_all.at[0], g_all_down.at[0]),
+    )
+    for source, part in zip(sources, parts, strict=True):
+        loads += zip(source, part, strict=True)
+    loads = [pltpu.make_async_copy(src, dst, loaded.at[k]) for k, (src, dst) in enumerate(loads)]
+    for copy in loads:
+        copy.start()
     factor = clip(squares[...], count)
     me = lax.axis_index("dp")
-    rows = near_a.shape[2]
-    held = ((near_a.at[2], near_b.at[2], g_own.at[0]), (near_a.at[1], near_b.at[1], g_all.at[1]))
-    held += ((far_a, far_b, g_all.at[2]), (near_a.at[0], near_b.at[0], g_all.at[0]))
-    for turn, (a, b, g) in enumerate(held):
+    for copy in loads:
+        copy.wait()
+
+    @pl.loop(0, n)
+    def _(turn):
         o = lax.rem(me + turn, n)
         at = pl.ds(pl.multiple_of(o * rows, rows), rows)
         for k, w in enumerate((wg, wu)):
             old = jnp.concatenate([one[0, at, :] for one in w], 1)
-            grad = g[k * rows : (k + 1) * rows, :].astype(F32) * factor
-            across[k, at, :] = adamw(old, a[2 * k], a[2 * k + 1], grad)[0]
-        grad = upright(g[2 * rows :, :].astype(F32)) * factor
-        down[o] = adamw(wd[0, o, 0], b[0], b[1], grad)[0]
+            grad = g[turn, k * rows : (k + 1) * rows, :].astype(F32) * factor
+            across[k, at, :] = adamw(old, a[turn, 2 * k], a[turn, 2 * k + 1], grad)[0]
+        for k, part in enumerate((g[turn, 2 * rows :, :], g_down[turn])):
+            grad = upright(part.astype(F32)) * factor
+            down[o, of_chunk[k], :] = adamw(wd[0, o, k], b[turn, 0, of_chunk[k], :], b[turn, 1, of_chunk[k], :], grad)[0]
+
     copies = []
-    for o, s in enumerate(stripes(n, chunks, EARLY)):
+    for o, s in enumerate(stripes(n, chunks, 0)):
         for k in range(2):
             copies.append((across.at[k, :, o * STRIPE : (o + 1) * STRIPE], outs[k].at[1, :, s]))
-        copies.append((down.at[o], outs[2].at[1, s, :]))
+        copies.append((down.at[o], outs[2].at[1, s.start : s.start + down.shape[1], :]))
     copies = [pltpu.make_async_copy(src, dst, sems.at[k]) for k, (src, dst) in enumerate(copies)]
     for copy in copies:
         copy.start()
@@ -686,29 +784,33 @@
         copy.wait()
 
 
-def early_step(n, chunks, squares, weights, near_a, near_b, far_a, far_b, g_top, g_all, count):
+def early_step(n, chunks, squares, weights, near_a, near_b, far_a, far_b, late, g_top, g_all, g_all_down, count):
     w_gate, w_up, w_down = weights
     d = w_gate.shape[1]
     whole = lambda one: pl.BlockSpec(one.shape, lambda i: (0,) * one.ndim)
-    across = [pl.BlockSpec((1, d, STRIPE), lambda i, o=o: (1, 0, o * chunks + EARLY)) for o in range(n)]
-    down = pl.BlockSpec((1, n, 1, STRIPE, d), lambda i: (1, 0, EARLY, 0, 0))
-    own = pl.BlockSpec((1, *g_top.shape[1:]), lambda i: (EARLY, 0, 0))
-    arrays = (near_a, near_b, far_a, far_b)
+    across = [pl.BlockSpec((1, d, STRIPE), lambda i, o=o: (1, 0, o * chunks)) for o in range(n)]
+    down = pl.BlockSpec((1, n, EARLY_DOWN, STRIPE, d), lambda i: (1, 0, 0, 0, 0))
+    arrays = (near_a, near_b, far_a, far_b, late, g_top, g_all, g_all_down)
     return pl.pallas_call(
         functools.partial(early_kernel, n, chunks, count),
         grid=(1,),
-        in_specs=[whole(squares)] + across + across + [down] + [whole(one) for one in arrays] + [own, whole(g_all)],
+        in_specs=[whole(squares)] + across + across + [down] + [pl.BlockSpec(memory_space=pl.ANY)] * len(arrays),
         out_specs=[pl.BlockSpec(memory_space=pl.ANY)] * 3,
         out_shape=[jax.ShapeDtypeStruct(w.shape, BF16) for w in weights],
         scratch_shapes=[
+            pltpu.VMEM((n, *far_a.shape), F32),
+            pltpu.VMEM((n, *far_b.shape), F32),
+            pltpu.VMEM((n, *g_all.shape[1:]), BF16),
+            pltpu.VMEM((n, *g_all_down.shape[1:]), BF16),
+            pltpu.SemaphoreType.DMA((6 * n,)),
             pltpu.VMEM((2, d, n * STRIPE), BF16),
-            pltpu.VMEM((n, STRIPE, d), BF16),
+            pltpu.VMEM((n, EARLY_DOWN * STRIPE, d), BF16),
             pltpu.SemaphoreType.DMA((3 * n,)),
         ],
         compiler_params=params(),
         cost_estimate=cost(16 * 3 * d * n * STRIPE, nbytes(*arrays)),
         name="early",
-    )(squares, *[w_gate] * n, *[w_up] * n, by_owner(n, w_down), *arrays, g_top, g_all)
+    )(squares, *[w_gate] * n, *[w_up] * n, by_owner(n, w_down), *arrays)
 
 
 def place_kernel(n, pieces, regions, *refs):
@@ -736,7 +838,7 @@
     def regions(layer):
         if tall:
             columns = arrays[0].shape[1]
-            return [(0, layer * STRIPE, columns, slice(first * columns // blocks, (first + blocks) * columns // blocks))]
+            return [(0, layer * EARLY_DOWN * STRIPE, columns, slice(first * columns // blocks, (first + blocks) * columns // blocks))]
         columns = full - layer * STRIPE
         return [
             (j * columns, 0, columns, slice((first + j) * full + layer * STRIPE, (first + j + 1) * full)) for j in range(blocks)
@@ -782,7 +884,7 @@
         weights, moments = (w_gate, w_up, w_down), ((m_gate, v_gate), (m_up, v_up), (m_down, v_down))
         *parts, near_a, near_b = forward(n, chunks, x, dy, *weights, sum(moments, ()))
         gate, up, a0_t, h1, a1, a1_t, dy_t = parts
-        *parts, far_a, far_b, g_all = top(n, chunks, 1, a1, a1_t, dy, dy_t, h1, *weights, near_a, near_b)
+        *parts, far_a, far_b, late, g_all, g_all_down = top(n, chunks, 1, a1, a1_t, dy, dy_t, h1, *weights, near_a, near_b)
         dh, dh_t, g_top, last, squares = parts
         g_bottom, squares = bottom(n, chunks, 0, a0_t, dh, dh_t, gate, up, w_down, last, squares)
 
@@ -793,7 +895,7 @@
             )
             squares = lax.optimization_barrier((squares, *own))[0]
             sent.append((own, *send_around(n, own, swap)))
-        whole = list(early_step(n, chunks, squares, weights, near_a, near_b, far_a, far_b, g_top, g_all, count))
+        whole = list(early_step(n, chunks, squares, weights, near_a, near_b, far_a, far_b, late, g_top, g_all, g_all_down, count))
         for k, (which, first, blocks, swap) in enumerate(PIECES):
             own, left, right, _ = sent[k]
             near = [(one, (layer, turn)) for turn, pair in ((0, own), (n - 1, left), (1, right)) for layer, one in enumerate(pair)]

time: 683 us -> 676 us (0.990)
  waiting for transfers between devices: 149 us -> 135 us
    ppermute x30, waiting for transfers between devices: 149 us -> 135 us  [send(): return lax.ppermute(one, 'dp', way)]
  transfers between devices with their start and end apart: 30 -> 30, of which waited for: 16 -> 15; matrix products, arithmetic and copies ran while one was open for 0% -> 0% of each run, Pallas kernels for 6% -> 6%
where the time goes in v2:
time: 676 us
  Pallas kernels  499 us (74%)
  waiting for transfers between devices  135 us (20%)
  starting transfers between devices  36.9 us (5%)
    pallas_call x1, Pallas kernels, top(): pl.pallas_call(functools.partial(top_kernel, n, chunks, tiles, layer), gr...  189 us
    pallas_call x1, Pallas kernels, bottom(): pl.pallas_call(functools.partial(bottom_kernel, n, chunks, tiles), grid=(...  148 us
    ppermute x30, waiting for transfers between devices, send(): return lax.ppermute(one, 'dp', way)  135 us
    pallas_call x1, Pallas kernels, forward(): pl.pallas_call(functools.partial(forward_kernel, n, chunks, tiles), grid=...  77.4 us
    pallas_call x5, Pallas kernels, adam(): pl.pallas_call(body, grid_spec=pltpu.PrefetchScalarGridSpec(num_scalar_pr...  37.1 us
    ppermute x30, starting transfers between devices, send(): return lax.ppermute(one, 'dp', way)  36.9 us
    pallas_call x10, Pallas kernels, place(): pl.pallas_call(functools.partial(place_kernel, n, where, regions), grid=(...  31.8 us
    pallas_call x1, Pallas kernels, early_step(): pl.pallas_call(functools.partial(early_kernel, n, chunks, count), grid=(1...  14.9 us
  transfers between devices with their start and end apart: 30, of which 15 were waited for; matrix products, arithmetic and copies ran while one was open for 0% of the time, Pallas kernels for 6%

profile of v2, /device:TPU:112, one launch (start us, length us, event | category | flops | bytes accessed | tf_op | source)
XLA Modules:
  0.0 676.0 jit_solution(11821060125398994633)
XLA Ops:
  0.6 77.4 %forward.1 = (f32[6,4096,512]{2,1,0:T(8,128)}, f32[6,4096,512]{2,1,0:T(8,128)}, bf16[768,4096]{1,0:T(8,128)(2,1)}, bf16[4096,768]{1,0:T(8,128)(2,1)}, bf16[4096,...) custom-call(bf16[4096,768]{1,0:T(8,128)(2,1)} %bitcast.7, ...), custom_call_target="tpu_custom_call" | custom-call | flops 57982058496 | bytes 141557760 | tf_op jit(solution)/shard_map/forward/pallas_call | solution.py:143
  78.0 189.2 %top.1 = (bf16[4096,768]{1,0:T(8,128)(2,1)}, bf16[768,4096]{1,0:T(8,128)(2,1)}, bf16[5,576,512]{2,1,0:T(8,128)(2,1)}, bf16[4,576,512]{2,1,0:T(8,128)(2,1)}, f32[...) custom-call(bf16[4096,768]{1,0:T(8,128)(2,1)} %get-tuple-element.59., ...), custom_call_target="tpu_custom_call" | custom-call | flops 154618822656 | bytes 150994944 | tf_op jit(solution)/shard_map/top/pallas_call | solution.py:487
  267.2 148.3 %bottom.1 = (bf16[7,576,512]{2,1,0:T(8,128)(2,1)}, f32[8,512]{1,0:T(8,128)}) custom-call(bf16[768,4096]{1,0:T(8,128)(2,1)} %get-tuple-element.58.refs_0_, bf16[4096,768]{1,0:T(8,128)(2,1)} %get-tuple-element.65.refs_1_, bf16[768,4096]{1,0:T(8,128)(2,1)} %get-tuple-element.66.refs_2_, f32[6,4096,512]{2,1,0:T(8,128)} %get-tuple-element.67.refs_3_, ...), custom_call_target="tpu_custom_call" | custom-call | flops 77309411328 | bytes 213909504 | tf_op jit(solution)/shard_map/bottom/pallas_call | solution.py:623
  415.5 4.4 adam.5
  419.9 9.3 %adam.6 = (bf16[192,2304]{1,0:T(8,128)(2,1)}, bf16[192,1920]{1,0:T(8,128)(2,1)}, f32[2,192,3072]{2,1,0:T(8,128)}, f32[2,192,3072]{2,1,0:T(8,128)}) custom-call(s32[1]{0:T(128)} %bitcast.me_ref, f32[8,512]{1,0:T(8,128)} %get-tuple-element.92.refs_0_.squares, bf16[2,768,3072]{2,1,0:T(8,128)(2,1)} %refs_3_.11, ...), custom_call_target="tpu_custom_call", output_to_operand_aliasing={{2}: (7, {}), {3}: (8, {})} | custom-call | flops 14155776 | bytes 19464192 | tf_op jit(solution)/shard_map/adam/pallas_call | solution.py:714
  429.2 9.6 %adam.7 = (bf16[768,768]{1,0:T(8,128)(2,1)}, bf16[512,768]{1,0:T(8,128)(2,1)}, f32[2,768,768]{2,1,0:T(8,128)}, f32[2,768,768]{2,1,0:T(8,128)}) custom-call(s32[1]{0:T(128)} %bitcast.me_ref, f32[8,512]{1,0:T(8,128)} %get-tuple-element.92.refs_0_.squares, bf16[2,3072,768]{2,1,0:T(8,128)(2,1)} %refs_1_.8, f32[2,768,768]{2,1,0:T(8,128)} %refs_2_.8, ...), custom_call_target="tpu_custom_call" | custom-call | flops 18874368 | bytes 25952256 | tf_op jit(solution)/shard_map/adam/pallas_call | solution.py:714
  438.7 9.3 %adam.8 = (bf16[192,2304]{1,0:T(8,128)(2,1)}, bf16[192,1920]{1,0:T(8,128)(2,1)}, f32[2,192,3072]{2,1,0:T(8,128)}, f32[2,192,3072]{2,1,0:T(8,128)}) custom-call(s32[1]{0:T(128)} %bitcast.me_ref, f32[8,512]{1,0:T(8,128)} %get-tuple-element.92.refs_0_.squares, bf16[2,768,3072]{2,1,0:T(8,128)(2,1)} %refs_7_.5, f32[2,192,3072]{2,1,0:T(8,128)} %refs_2_.10, ...), custom_call_target="tpu_custom_call" | custom-call | flops 14155776 | bytes 19464192 | tf_op jit(solution)/shard_map/adam/pallas_call | solution.py:714
  448.1 4.5 adam.9
  452.6 1.7 collective-permute-start.14
  454.3 0.3 collective-permute-start.20
  454.6 0.5 collective-permute-start.10
  455.1 2.8 collective-permute-start.6
  457.9 3.8 collective-permute-done.14.refs_5_
  461.6 2.9 collective-permute-start.21
  464.6 0.1 collective-permute-start.11
  464.7 5.2 collective-permute-done.10.refs_3_
  469.8 0.0 collective-permute-done.6.refs_5_
  469.9 2.0 collective-permute-start.4
  471.9 4.4 collective-permute-done.12.refs_2_
  476.3 0.0 collective-permute-start.22
  476.3 0.0 collective-permute-done.21.refs_4_
  476.3 3.2 collective-permute-start.15
  479.5 0.0 collective-permute-done.11.refs_4_
  479.5 2.9 collective-permute-start.7
  482.5 0.0 collective-permute-start.5
  482.5 18.1 %collective-permute-done.15.refs_1_ = bf16[192,640]{1,0:T(8,128)(2,1)S(1)} collective-permute-done((bf16[192,640]{1,0:T(8,128)(2,1)S(1)}, bf16[192,640]{1,0:T(8,128)(2,1)S(1)}, u32[]{:S(2)}, u32[]{:S(2)}) %collective-permute-start.15) | collective-permute-done | bytes 245792 | tf_op jit(solution)/shard_map/ppermute | solution.py:865
  500.6 2.9 collective-permute-start.2
  503.5 2.3 collective-permute-done.7.refs_1_
  505.9 1.5 collective-permute-start.26
  507.4 1.9 collective-permute-start.29
  509.3 1.1 collective-permute-start.16
  510.4 11.3 %collective-permute-done.2.refs_5_ = bf16[192,1920]{1,0:T(8,128)(2,1)} collective-permute-done((bf16[192,1920]{1,0:T(8,128)(2,1)S(1)}, bf16[192,1920]{1,0:T(8,128)(2,1)}, u32[]{:S(2)}, u32[]{:S(2)}) %collective-permute-start.2) | collective-permute-done | bytes 737312 | tf_op jit(solution)/shard_map/ppermute | solution.py:865
  521.8 2.9 collective-permute-start.23
  524.7 1.7 collective-permute-done.8.refs_3_
  526.4 1.7 collective-permute-start.24
  528.2 15.2 %collective-permute-done.26.refs_3_ = bf16[512,768]{1,0:T(8,128)(2,1)} collective-permute-done((bf16[512,768]{1,0:T(8,128)(2,1)S(1)}, bf16[512,768]{1,0:T(8,128)(2,1)}, u32[]{:S(2)}, u32[]{:S(2)}) %collective-permute-start.26) | collective-permute-done | bytes 786464 | tf_op jit(solution)/shard_map/ppermute | solution.py:865
  543.4 0.6 collective-permute-start.28
  544.1 18.2 %collective-permute-done.16.refs_2_ = bf16[192,2304]{1,0:T(8,128)(2,1)S(1)} collective-permute-done((bf16[192,2304]{1,0:T(8,128)(2,1)S(1)}, bf16[192,2304]{1,0:T(8,128)(2,1)S(1)}, u32[]{:S(2)}, u32[]{:S(2)}) %collective-permute-start.16) | collective-permute-done | bytes 884768 | tf_op jit(solution)/shard_map/ppermute | solution.py:865
  562.3 1.7 collective-permute-start.9
  564.0 0.1 collective-permute-start.19
  564.1 17.2 %collective-permute-done.refs_2_ = bf16[192,2304]{1,0:T(8,128)(2,1)} collective-permute-done((bf16[192,2304]{1,0:T(8,128)(2,1)}, bf16[192,2304]{1,0:T(8,128)(2,1)}, u32[]{:S(2)}, u32[]{:S(2)}) %collective-permute-start) | collective-permute-done | bytes 884768 | tf_op jit(solution)/shard_map/ppermute | solution.py:865
  581.3 1.4 collective-permute-done.24.refs_4_
  582.8 2.9 collective-permute-start.25
  585.7 16.0 %collective-permute-done.9.refs_4_ = bf16[192,2304]{1,0:T(8,128)(2,1)S(1)} collective-permute-done((bf16[192,2304]{1,0:T(8,128)(2,1)}, bf16[192,2304]{1,0:T(8,128)(2,1)S(1)}, u32[]{:S(2)}, u32[]{:S(2)}) %collective-permute-start.9) | collective-permute-done | bytes 884768 | tf_op jit(solution)/shard_map/ppermute | solution.py:865
  601.7 4.8 collective-permute-done.28.refs_2_
  606.5 1.1 copy-done.3
  607.6 10.0 %collective-permute-done.19.refs_1_ = bf16[192,1920]{1,0:T(8,128)(2,1)S(1)} collective-permute-done((bf16[192,1920]{1,0:T(8,128)(2,1)S(1)}, bf16[192,1920]{1,0:T(8,128)(2,1)S(1)}, u32[]{:S(2)}, u32[]{:S(2)}) %collective-permute-start.19) | collective-permute-done | bytes 737312 | tf_op jit(solution)/shard_map/ppermute | solution.py:865
  617.5 2.9 collective-permute-start.3
  620.5 5.0 collective-permute-done.17.refs_0_
  625.5 0.9 copy-done.7
  626.4 14.9 %early.1 = (bf16[2,768,3072]{2,1,0:T(8,128)(2,1)}, bf16[2,768,3072]{2,1,0:T(8,128)(2,1)}, bf16[2,3072,768]{2,1,0:T(8,128)(2,1)}) custom-call(f32[8,512]{1,0:T(8,128)} %get-tuple-element.92.refs_0_.squares, bf16[2,768,3072]{2,1,0:T(8,128)(2,1)} %refs_3_.11, bf16[2,768,3072]{2,1,0:T(8,128)(2,1)} %refs_3_.11, bf16[2,768,3072]{2,1,0:T(8,128)(2,1)} %refs_3_.11, ...), custom_call_target="tpu_custom_call" | custom-call | flops 18874368 | bytes 19070976 | tf_op jit(solution)/shard_map/early/pallas_call | solution.py:794
  641.3 2.7 place.10.refs_6_
  644.0 4.7 place.14.refs_6_
  648.7 4.7 place.11.refs_2_
  653.5 2.7 place.15.refs_2_
  656.1 1.8 place.12.refs_2_
  658.0 5.3 place.18.refs_2_
  663.3 2.6 place.16.refs_2_
  665.9 0.7 copy-done.21
  666.7 1.8 place.17
  668.5 2.6 place.13
  671.1 0.9 copy-done.10
  672.0 1.1 copy-done.2
  673.1 2.8 place.19
  (71 shorter events, 0.2 us)
Async XLA Ops:
  448.0 16.6 %copy-start.16 = (bf16[192,768]{1,0:T(8,128)(2,1)S(1)}, bf16[192,768]{1,0:T(8,128)(2,1)}, u32[]{:S(2)}) copy-start(bf16[192,768]{1,0:T(8,128)(2,1)} %get-tuple-element.74.refs_0_) | copy-start | bytes 884740
  448.0 52.6 %copy-start.11 = (bf16[192,1920]{1,0:T(8,128)(2,1)S(1)}, bf16[192,1920]{1,0:T(8,128)(2,1)}, u32[]{:S(2)}) copy-start(bf16[192,1920]{1,0:T(8,128)(2,1)} %get-tuple-element.80.refs_1_) | copy-start | bytes 2211844
  448.0 57.8 %copy-start.9 = (bf16[512,768]{1,0:T(8,128)(2,1)S(1)}, bf16[512,768]{1,0:T(8,128)(2,1)}, u32[]{:S(2)}) copy-start(bf16[512,768]{1,0:T(8,128)(2,1)} %get-tuple-element.83.refs_1_) | copy-start | bytes 2359300
  448.0 61.3 %copy-start.4 = (bf16[192,2304]{1,0:T(8,128)(2,1)S(1)}, bf16[192,2304]{1,0:T(8,128)(2,1)}, u32[]{:S(2)}) copy-start(bf16[192,2304]{1,0:T(8,128)(2,1)} %get-tuple-element.85.refs_0_) | copy-start | bytes 2654212
  448.1 78.4 %copy-start = (bf16[768,768]{1,0:T(8,128)(2,1)S(1)}, bf16[768,768]{1,0:T(8,128)(2,1)}, u32[]{:S(2)}) copy-start(bf16[768,768]{1,0:T(8,128)(2,1)} %get-tuple-element.82.refs_0_) | copy-start | bytes 3538948
  452.6 9.0 %collective-permute-start.14 = (bf16[192,640]{1,0:T(8,128)(2,1)}, bf16[192,640]{1,0:T(8,128)(2,1)S(1)}, u32[]{:S(2)}, u32[]{:S(2)}) collective-permute-start(bf16[192,640]{1,0:T(8,128)(2,1)} %get-tuple-element.91.refs_1_), channel_id=1, source_target_pairs={{0,3},{1,0},{2,1},{3,2},{4,7},{5,4},{6,5},{7,6},{8,11},{9,8},{10,9... | collective-permute-start | bytes 737288 | tf_op jit(solution)/shard_map/ppermute | solution.py:865
  454.3 10.3 %collective-permute-start.20 = (bf16[192,640]{1,0:T(8,128)(2,1)}, bf16[192,640]{1,0:T(8,128)(2,1)S(1)}, u32[]{:S(2)}, u32[]{:S(2)}) collective-permute-start(bf16[192,640]{1,0:T(8,128)(2,1)} %get-tuple-element.91.refs_1_), channel_id=1, source_target_pairs={{0,1},{1,2},{2,3},{3,0},{4,5},{5,6},{6,7},{7,4},{8,9},{9,10},{10,1... | collective-permute-start | bytes 737288 | tf_op jit(solution)/shard_map/ppermute | solution.py:865
  454.6 15.2 %collective-permute-start.10 = (bf16[192,640]{1,0:T(8,128)(2,1)}, bf16[192,640]{1,0:T(8,128)(2,1)S(1)}, u32[]{:S(2)}, u32[]{:S(2)}) collective-permute-start(bf16[192,640]{1,0:T(8,128)(2,1)} %get-tuple-element.75.refs_1_), channel_id=1, source_target_pairs={{0,1},{1,2},{2,3},{3,0},{4,5},{5,6},{6,7},{7,4},{8,9},{9,10},{10,1... | collective-permute-start | bytes 737288 | tf_op jit(solution)/shard_map/ppermute | solution.py:865
  455.1 14.7 %collective-permute-start.6 = (bf16[192,640]{1,0:T(8,128)(2,1)}, bf16[192,640]{1,0:T(8,128)(2,1)S(1)}, u32[]{:S(2)}, u32[]{:S(2)}) collective-permute-start(bf16[192,640]{1,0:T(8,128)(2,1)} %get-tuple-element.75.refs_1_), channel_id=1, source_target_pairs={{0,3},{1,0},{2,1},{3,2},{4,7},{5,4},{6,5},{7,6},{8,11},{9,8},{10,9... | collective-permute-start | bytes 737288 | tf_op jit(solution)/shard_map/ppermute | solution.py:865
  457.9 18.4 %collective-permute-start.12 = (bf16[192,768]{1,0:T(8,128)(2,1)}, bf16[192,768]{1,0:T(8,128)(2,1)}, u32[]{:S(2)}, u32[]{:S(2)}) collective-permute-start(bf16[192,768]{1,0:T(8,128)(2,1)} %get-tuple-element.90.refs_0_), channel_id=1, source_target_pairs={{0,1},{1,2},{2,3},{3,0},{4,5},{5,6},{6,7},{7,4},{8,9},{9,10},{10,1... | collective-permute-start | bytes 884744 | tf_op jit(solution)/shard_map/ppermute | solution.py:865
  461.6 82.4 %copy-start.22 = (bf16[192,640]{1,0:T(8,128)(2,1)}, bf16[192,640]{1,0:T(8,128)(2,1)S(1)}, u32[]{:S(2)}) copy-start(bf16[192,640]{1,0:T(8,128)(2,1)S(1)} %collective-permute-done.14.refs_5_) | copy-start | bytes 737284
  461.6 14.6 %collective-permute-start.21 = (bf16[192,768]{1,0:T(8,128)(2,1)}, bf16[192,768]{1,0:T(8,128)(2,1)S(1)}, u32[]{:S(2)}, u32[]{:S(2)}) collective-permute-start(bf16[192,768]{1,0:T(8,128)(2,1)} %get-tuple-element.90.refs_0_), channel_id=1, source_target_pairs={{0,3},{1,0},{2,1},{3,2},{4,7},{5,4},{6,5},{7,6},{8,11},{9,8},{10,9... | collective-permute-start | bytes 884744 | tf_op jit(solution)/shard_map/ppermute | solution.py:865
  464.6 7.3 %copy-start.23 = (bf16[192,640]{1,0:T(8,128)(2,1)}, bf16[192,640]{1,0:T(8,128)(2,1)S(1)}, u32[]{:S(2)}) copy-start(bf16[192,640]{1,0:T(8,128)(2,1)S(1)} %collective-permute-done.20.refs_3_) | copy-start | bytes 737284
  464.6 15.0 %collective-permute-start.11 = (bf16[192,768]{1,0:T(8,128)(2,1)S(1)}, bf16[192,768]{1,0:T(8,128)(2,1)S(1)}, u32[]{:S(2)}, u32[]{:S(2)}) collective-permute-start(bf16[192,768]{1,0:T(8,128)(2,1)S(1)} %copy-done.16), channel_id=1, source_target_pairs={{0,3},{1,0},{2,1},{3,2},{4,7},{5,4},{6,5},{7,6},{8,11},{9,8},{10,9... | collective-permute-start | bytes 884744 | tf_op jit(solution)/shard_map/ppermute | solution.py:865
  469.8 2.0 copy-start.24
  469.8 37.6 %collective-permute-start.18 = (bf16[192,1920]{1,0:T(8,128)(2,1)}, bf16[192,1920]{1,0:T(8,128)(2,1)S(1)}, u32[]{:S(2)}, u32[]{:S(2)}) collective-permute-start(bf16[192,1920]{1,0:T(8,128)(2,1)} %get-tuple-element.86.refs_1_), channel_id=1, source_target_pairs={{0,3},{1,0},{2,1},{3,2},{4,7},{5,4},{6,5},{7,6},{8,11},{9,8},{10,9... | collective-permute-start | bytes 2211848 | tf_op jit(solution)/shard_map/ppermute | solution.py:865
  469.8 74.2 %copy-start.25 = (bf16[192,640]{1,0:T(8,128)(2,1)}, bf16[192,640]{1,0:T(8,128)(2,1)S(1)}, u32[]{:S(2)}) copy-start(bf16[192,640]{1,0:T(8,128)(2,1)S(1)} %collective-permute-done.6.refs_5_) | copy-start | bytes 737284
  469.9 12.6 %collective-permute-start.4 = (bf16[192,768]{1,0:T(8,128)(2,1)S(1)}, bf16[192,768]{1,0:T(8,128)(2,1)S(1)}, u32[]{:S(2)}, u32[]{:S(2)}) collective-permute-start(bf16[192,768]{1,0:T(8,128)(2,1)S(1)} %copy-done.16), channel_id=1, source_target_pairs={{0,1},{1,2},{2,3},{3,0},{4,5},{5,6},{6,7},{7,4},{8,9},{9,10},{10,1... | collective-permute-start | bytes 884744 | tf_op jit(solution)/shard_map/ppermute | solution.py:865
  476.3 33.1 %collective-permute-start.22 = (bf16[192,1920]{1,0:T(8,128)(2,1)}, bf16[192,1920]{1,0:T(8,128)(2,1)S(1)}, u32[]{:S(2)}, u32[]{:S(2)}) collective-permute-start(bf16[192,1920]{1,0:T(8,128)(2,1)} %get-tuple-element.86.refs_1_), channel_id=1, source_target_pairs={{0,1},{1,2},{2,3},{3,0},{4,5},{5,6},{6,7},{7,4},{8,9},{9,10},{10,1... | collective-permute-start | bytes 2211848 | tf_op jit(solution)/shard_map/ppermute | solution.py:865
  476.3 67.1 %copy-start.17 = (bf16[192,768]{1,0:T(8,128)(2,1)}, bf16[192,768]{1,0:T(8,128)(2,1)S(1)}, u32[]{:S(2)}) copy-start(bf16[192,768]{1,0:T(8,128)(2,1)S(1)} %collective-permute-done.21.refs_4_) | copy-start | bytes 884740
  476.3 24.3 %collective-permute-start.15 = (bf16[192,640]{1,0:T(8,128)(2,1)S(1)}, bf16[192,640]{1,0:T(8,128)(2,1)S(1)}, u32[]{:S(2)}, u32[]{:S(2)}) collective-permute-start(bf16[192,640]{1,0:T(8,128)(2,1)S(1)} %collective-permute-done.14.refs_5_), channel_id=1, source_target_pairs={{0,3},{1,0},{2,1},{3,2},{4,7},{5,4},{6,5},{7,6},{8,11},{9,8},{10,9... | collective-permute-start | bytes 737288 | tf_op jit(solution)/shard_map/ppermute | solution.py:865
  479.5 29.8 %copy-start.18 = (bf16[192,768]{1,0:T(8,128)(2,1)}, bf16[192,768]{1,0:T(8,128)(2,1)S(1)}, u32[]{:S(2)}) copy-start(bf16[192,768]{1,0:T(8,128)(2,1)S(1)} %collective-permute-done.11.refs_4_) | copy-start | bytes 884740
  479.5 26.3 %collective-permute-start.7 = (bf16[192,640]{1,0:T(8,128)(2,1)S(1)}, bf16[192,640]{1,0:T(8,128)(2,1)S(1)}, u32[]{:S(2)}, u32[]{:S(2)}) collective-permute-start(bf16[192,640]{1,0:T(8,128)(2,1)S(1)} %collective-permute-done.6.refs_5_), channel_id=1, source_target_pairs={{0,3},{1,0},{2,1},{3,2},{4,7},{5,4},{6,5},{7,6},{8,11},{9,8},{10,9... | collective-permute-start | bytes 737288 | tf_op jit(solution)/shard_map/ppermute | solution.py:865
  482.5 61.6 %copy-start.19 = (bf16[192,768]{1,0:T(8,128)(2,1)}, bf16[192,768]{1,0:T(8,128)(2,1)S(1)}, u32[]{:S(2)}) copy-start(bf16[192,768]{1,0:T(8,128)(2,1)S(1)} %collective-permute-done.4.refs_2_) | copy-start | bytes 884740
  482.5 23.4 %collective-permute-start.5 = (bf16[192,768]{1,0:T(8,128)(2,1)S(1)}, bf16[192,768]{1,0:T(8,128)(2,1)S(1)}, u32[]{:S(2)}, u32[]{:S(2)}) collective-permute-start(bf16[192,768]{1,0:T(8,128)(2,1)S(1)} %collective-permute-done.4.refs_2_), channel_id=1, source_target_pairs={{0,1},{1,2},{2,3},{3,0},{4,5},{5,6},{6,7},{7,4},{8,9},{9,10},{10,1... | collective-permute-start | bytes 884744 | tf_op jit(solution)/shard_map/ppermute | solution.py:865
  500.6 43.5 %copy-start.26 = (bf16[192,640]{1,0:T(8,128)(2,1)}, bf16[192,640]{1,0:T(8,128)(2,1)S(1)}, u32[]{:S(2)}) copy-start(bf16[192,640]{1,0:T(8,128)(2,1)S(1)} %collective-permute-done.15.refs_1_) | copy-start | bytes 737284
  500.6 21.2 %collective-permute-start.2 = (bf16[192,1920]{1,0:T(8,128)(2,1)S(1)}, bf16[192,1920]{1,0:T(8,128)(2,1)}, u32[]{:S(2)}, u32[]{:S(2)}) collective-permute-start(bf16[192,1920]{1,0:T(8,128)(2,1)S(1)} %copy-done.11), channel_id=1, source_target_pairs={{0,3},{1,0},{2,1},{3,2},{4,7},{5,4},{6,5},{7,6},{8,11},{9,8},{10,9... | collective-permute-start | bytes 2211848 | tf_op jit(solution)/shard_map/ppermute | solution.py:865
  505.9 3.5 copy-start.27
  505.9 20.6 %collective-permute-start.8 = (bf16[192,1920]{1,0:T(8,128)(2,1)S(1)}, bf16[192,1920]{1,0:T(8,128)(2,1)S(1)}, u32[]{:S(2)}, u32[]{:S(2)}) collective-permute-start(bf16[192,1920]{1,0:T(8,128)(2,1)S(1)} %copy-done.11), channel_id=1, source_target_pairs={{0,1},{1,2},{2,3},{3,0},{4,5},{5,6},{6,7},{7,4},{8,9},{9,10},{10,1... | collective-permute-start | bytes 2211848 | tf_op jit(solution)/shard_map/ppermute | solution.py:865
  505.9 18.8 %copy-start.20 = (bf16[192,768]{1,0:T(8,128)(2,1)}, bf16[192,768]{1,0:T(8,128)(2,1)S(1)}, u32[]{:S(2)}) copy-start(bf16[192,768]{1,0:T(8,128)(2,1)S(1)} %collective-permute-done.5.refs_0_) | copy-start | bytes 884740
  505.9 37.5 %collective-permute-start.26 = (bf16[512,768]{1,0:T(8,128)(2,1)S(1)}, bf16[512,768]{1,0:T(8,128)(2,1)}, u32[]{:S(2)}, u32[]{:S(2)}) collective-permute-start(bf16[512,768]{1,0:T(8,128)(2,1)S(1)} %copy-done.9), channel_id=1, source_target_pairs={{0,1},{1,2},{2,3},{3,0},{4,5},{5,6},{6,7},{7,4},{8,9},{9,10},{10,1... | collective-permute-start | bytes 2359304 | tf_op jit(solution)/shard_map/ppermute | solution.py:865
  507.4 118.9 %copy-start.12 = (bf16[192,1920]{1,0:T(8,128)(2,1)}, bf16[192,1920]{1,0:T(8,128)(2,1)S(1)}, u32[]{:S(2)}) copy-start(bf16[192,1920]{1,0:T(8,128)(2,1)S(1)} %collective-permute-done.18.refs_5_) | copy-start | bytes 2211844
  507.4 36.0 %collective-permute-start.29 = (bf16[512,768]{1,0:T(8,128)(2,1)S(1)}, bf16[512,768]{1,0:T(8,128)(2,1)}, u32[]{:S(2)}, u32[]{:S(2)}) collective-permute-start(bf16[512,768]{1,0:T(8,128)(2,1)S(1)} %copy-done.9), channel_id=1, source_target_pairs={{0,3},{1,0},{2,1},{3,2},{4,7},{5,4},{6,5},{7,6},{8,11},{9,8},{10,9... | collective-permute-start | bytes 2359304 | tf_op jit(solution)/shard_map/ppermute | solution.py:865
  509.3 34.1 %copy-start.13 = (bf16[192,1920]{1,0:T(8,128)(2,1)}, bf16[192,1920]{1,0:T(8,128)(2,1)S(1)}, u32[]{:S(2)}) copy-start(bf16[192,1920]{1,0:T(8,128)(2,1)S(1)} %collective-permute-done.22.refs_3_) | copy-start | bytes 2211844
  509.3 52.9 %collective-permute-start.16 = (bf16[192,2304]{1,0:T(8,128)(2,1)S(1)}, bf16[192,2304]{1,0:T(8,128)(2,1)S(1)}, u32[]{:S(2)}, u32[]{:S(2)}) collective-permute-start(bf16[192,2304]{1,0:T(8,128)(2,1)S(1)} %copy-done.4), channel_id=1, source_target_pairs={{0,1},{1,2},{2,3},{3,0},{4,5},{5,6},{6,7},{7,4},{8,9},{9,10},{10,1... | collective-permute-start | bytes 2654216 | tf_op jit(solution)/shard_map/ppermute | solution.py:865
  521.8 42.2 %collective-permute-start.23 = (bf16[192,2304]{1,0:T(8,128)(2,1)S(1)}, bf16[192,2304]{1,0:T(8,128)(2,1)S(1)}, u32[]{:S(2)}, u32[]{:S(2)}) collective-permute-start(bf16[192,2304]{1,0:T(8,128)(2,1)S(1)} %copy-done.4), channel_id=1, source_target_pairs={{0,3},{1,0},{2,1},{3,2},{4,7},{5,4},{6,5},{7,6},{8,11},{9,8},{10,9... | collective-permute-start | bytes 2654216 | tf_op jit(solution)/shard_map/ppermute | solution.py:865
  526.4 37.6 %copy-start.14 = (bf16[192,1920]{1,0:T(8,128)(2,1)}, bf16[192,1920]{1,0:T(8,128)(2,1)S(1)}, u32[]{:S(2)}) copy-start(bf16[192,1920]{1,0:T(8,128)(2,1)S(1)} %collective-permute-done.8.refs_3_) | copy-start | bytes 2211844
  526.4 56.3 %collective-permute-start.24 = (bf16[768,768]{1,0:T(8,128)(2,1)S(1)}, bf16[768,768]{1,0:T(8,128)(2,1)S(1)}, u32[]{:S(2)}, u32[]{:S(2)}) collective-permute-start(bf16[768,768]{1,0:T(8,128)(2,1)S(1)} %copy-done), channel_id=1, source_target_pairs={{0,3},{1,0},{2,1},{3,2},{4,7},{5,4},{6,5},{7,6},{8,11},{9,8},{10,9... | collective-permute-start | bytes 3538952 | tf_op jit(solution)/shard_map/ppermute | solution.py:865
  543.4 37.9 %collective-permute-start = (bf16[192,2304]{1,0:T(8,128)(2,1)}, bf16[192,2304]{1,0:T(8,128)(2,1)}, u32[]{:S(2)}, u32[]{:S(2)}) collective-permute-start(bf16[192,2304]{1,0:T(8,128)(2,1)} %get-tuple-element.79.refs_0_), channel_id=1, source_target_pairs={{0,1},{1,2},{2,3},{3,0},{4,5},{5,6},{6,7},{7,4},{8,9},{9,10},{10,1... | collective-permute-start | bytes 2654216 | tf_op jit(solution)/shard_map/ppermute | solution.py:865
  543.4 63.1 %collective-permute-start.28 = (bf16[768,768]{1,0:T(8,128)(2,1)S(1)}, bf16[768,768]{1,0:T(8,128)(2,1)S(1)}, u32[]{:S(2)}, u32[]{:S(2)}) collective-permute-start(bf16[768,768]{1,0:T(8,128)(2,1)S(1)} %copy-done), channel_id=1, source_target_pairs={{0,1},{1,2},{2,3},{3,0},{4,5},{5,6},{6,7},{7,4},{8,9},{9,10},{10,1... | collective-permute-start | bytes 3538952 | tf_op jit(solution)/shard_map/ppermute | solution.py:865
  562.2 45.3 %copy-start.5 = (bf16[192,2304]{1,0:T(8,128)(2,1)}, bf16[192,2304]{1,0:T(8,128)(2,1)S(1)}, u32[]{:S(2)}) copy-start(bf16[192,2304]{1,0:T(8,128)(2,1)S(1)} %collective-permute-done.16.refs_2_) | copy-start | bytes 2654212
  562.3 39.5 %collective-permute-start.9 = (bf16[192,2304]{1,0:T(8,128)(2,1)}, bf16[192,2304]{1,0:T(8,128)(2,1)S(1)}, u32[]{:S(2)}, u32[]{:S(2)}) collective-permute-start(bf16[192,2304]{1,0:T(8,128)(2,1)} %get-tuple-element.79.refs_0_), channel_id=1, source_target_pairs={{0,3},{1,0},{2,1},{3,2},{4,7},{5,4},{6,5},{7,6},{8,11},{9,8},{10,9... | collective-permute-start | bytes 2654216 | tf_op jit(solution)/shard_map/ppermute | solution.py:865
  564.0 61.5 %copy-start.6 = (bf16[192,2304]{1,0:T(8,128)(2,1)}, bf16[192,2304]{1,0:T(8,128)(2,1)S(1)}, u32[]{:S(2)}) copy-start(bf16[192,2304]{1,0:T(8,128)(2,1)S(1)} %collective-permute-done.23.refs_4_) | copy-start | bytes 2654212
  564.0 53.5 %collective-permute-start.19 = (bf16[192,1920]{1,0:T(8,128)(2,1)S(1)}, bf16[192,1920]{1,0:T(8,128)(2,1)S(1)}, u32[]{:S(2)}, u32[]{:S(2)}) collective-permute-start(bf16[192,1920]{1,0:T(8,128)(2,1)S(1)} %collective-permute-done.18.refs_5_), channel_id=1, source_target_pairs={{0,3},{1,0},{2,1},{3,2},{4,7},{5,4},{6,5},{7,6},{8,11},{9,8},{10,9... | collective-permute-start | bytes 2211848 | tf_op jit(solution)/shard_map/ppermute | solution.py:865
  581.3 44.1 %collective-permute-start.17 = (bf16[192,2304]{1,0:T(8,128)(2,1)S(1)}, bf16[192,2304]{1,0:T(8,128)(2,1)S(1)}, u32[]{:S(2)}, u32[]{:S(2)}) collective-permute-start(bf16[192,2304]{1,0:T(8,128)(2,1)S(1)} %collective-permute-done.16.refs_2_), channel_id=1, source_target_pairs={{0,1},{1,2},{2,3},{3,0},{4,5},{5,6},{6,7},{7,4},{8,9},{9,10},{10,1... | collective-permute-start | bytes 2654216 | tf_op jit(solution)/shard_map/ppermute | solution.py:865
  582.8 58.6 %copy-start.1 = (bf16[768,768]{1,0:T(8,128)(2,1)}, bf16[768,768]{1,0:T(8,128)(2,1)S(1)}, u32[]{:S(2)}) copy-start(bf16[768,768]{1,0:T(8,128)(2,1)S(1)} %collective-permute-done.24.refs_4_) | copy-start | bytes 3538948
  582.8 88.4 %collective-permute-start.25 = (bf16[768,768]{1,0:T(8,128)(2,1)S(1)}, bf16[768,768]{1,0:T(8,128)(2,1)S(1)}, u32[]{:S(2)}, u32[]{:S(2)}) collective-permute-start(bf16[768,768]{1,0:T(8,128)(2,1)S(1)} %collective-permute-done.24.refs_4_), channel_id=1, source_target_pairs={{0,3},{1,0},{2,1},{3,2},{4,7},{5,4},{6,5},{7,6},{8,11},{9,8},{10,9... | collective-permute-start | bytes 3538952 | tf_op jit(solution)/shard_map/ppermute | solution.py:865
  601.7 24.6 %copy-start.8 = (bf16[192,2304]{1,0:T(8,128)(2,1)}, bf16[192,2304]{1,0:T(8,128)(2,1)S(1)}, u32[]{:S(2)}) copy-start(bf16[192,2304]{1,0:T(8,128)(2,1)S(1)} %collective-permute-done.9.refs_4_) | copy-start | bytes 2654212
  601.7 66.8 %collective-permute-start.1 = (bf16[192,2304]{1,0:T(8,128)(2,1)}, bf16[192,2304]{1,0:T(8,128)(2,1)}, u32[]{:S(2)}, u32[]{:S(2)}) collective-permute-start(bf16[192,2304]{1,0:T(8,128)(2,1)} %collective-permute-done.refs_2_), channel_id=1, source_target_pairs={{0,1},{1,2},{2,3},{3,0},{4,5},{5,6},{6,7},{7,4},{8,9},{9,10},{10,1... | collective-permute-start | bytes 2654216 | tf_op jit(solution)/shard_map/ppermute | solution.py:865
  606.5 1.1 copy-start.3
  607.5 63.6 %collective-permute-start.27 = (bf16[512,768]{1,0:T(8,128)(2,1)}, bf16[512,768]{1,0:T(8,128)(2,1)S(1)}, u32[]{:S(2)}, u32[]{:S(2)}) collective-permute-start(bf16[512,768]{1,0:T(8,128)(2,1)} %collective-permute-done.26.refs_3_), channel_id=1, source_target_pairs={{0,1},{1,2},{2,3},{3,0},{4,5},{5,6},{6,7},{7,4},{8,9},{9,10},{10,1... | collective-permute-start | bytes 2359304 | tf_op jit(solution)/shard_map/ppermute | solution.py:865
  617.5 8.8 %copy-start.15 = (bf16[192,1920]{1,0:T(8,128)(2,1)}, bf16[192,1920]{1,0:T(8,128)(2,1)S(1)}, u32[]{:S(2)}) copy-start(bf16[192,1920]{1,0:T(8,128)(2,1)S(1)} %collective-permute-done.19.refs_1_) | copy-start | bytes 2211844
  617.5 51.0 %collective-permute-start.3 = (bf16[192,1920]{1,0:T(8,128)(2,1)}, bf16[192,1920]{1,0:T(8,128)(2,1)}, u32[]{:S(2)}, u32[]{:S(2)}) collective-permute-start(bf16[192,1920]{1,0:T(8,128)(2,1)} %collective-permute-done.2.refs_5_), channel_id=1, source_target_pairs={{0,3},{1,0},{2,1},{3,2},{4,7},{5,4},{6,5},{7,6},{8,11},{9,8},{10,9... | collective-permute-start | bytes 2211848 | tf_op jit(solution)/shard_map/ppermute | solution.py:865
  625.5 0.9 copy-start.7
  625.5 40.5 %collective-permute-start.13 = (bf16[192,768]{1,0:T(8,128)(2,1)}, bf16[192,768]{1,0:T(8,128)(2,1)S(1)}, u32[]{:S(2)}, u32[]{:S(2)}) collective-permute-start(bf16[192,768]{1,0:T(8,128)(2,1)} %collective-permute-done.12.refs_2_), channel_id=1, source_target_pairs={{0,1},{1,2},{2,3},{3,0},{4,5},{5,6},{6,7},{7,4},{8,9},{9,10},{10,1... | collective-permute-start | bytes 884744 | tf_op jit(solution)/shard_map/ppermute | solution.py:865
  665.9 0.7 copy-start.21
  671.1 0.9 copy-start.10
  672.0 1.1 copy-start.2

commit v3 on v2

--- a/solution.py
+++ b/solution.py
@@ -11,8 +11,8 @@
 F32, BF16 = jnp.float32, jnp.bfloat16
 STRIPE = 128
 VMEM_LIMIT = 60 << 20
-EARLY_DOWN = 2
-PIECES = ((0, 0, 1, False), (0, 1, 3, False), (2, 0, 2, True), (1, 0, 3, False), (1, 3, 1, False))
+EARLY = 2
+PIECES = ((0, 0, 1, False), (0, 1, 3, True), (2, 0, 2, False), (1, 0, 3, True), (1, 3, 1, False))
 
 
 def dot(a, b):
@@ -62,20 +62,20 @@
     right, _, left = neighbours(n)
 
     def packing():
+        each = pack_a.shape[2] // n
         for k, ref in enumerate(moments[:4]):
-            for o, s in enumerate(stripes(n, chunks, 0)):
-                yield pltpu.make_async_copy(
-                    ref.at[1, :, s], pack_a.at[k, :, o * STRIPE : (o + 1) * STRIPE], packed.at[k * n + o]
-                )
+            for o in range(n):
+                part = pack_a.at[k, :, o * each : (o + 1) * each]
+                start = o * chunks * STRIPE
+                yield pltpu.make_async_copy(ref.at[1, :, start : start + each], part, packed.at[k * n + o])
         for k, ref in enumerate(moments[4:]):
             yield pltpu.make_async_copy(ref.at[1, : pack_b.shape[1], :], pack_b.at[k], packed.at[4 * n + k])
 
     def copies():
-        parts = ((pack_a, near_a, ()), (pack_b.at[0], near_b, (0,)), (pack_b.at[1, :STRIPE], near_b, (1, slice(0, STRIPE))))
-        for k, (part, near, where) in enumerate(parts):
-            yield remote(part, near.at[0, *where], send.at[k], recv.at[k], right)
-            yield remote(part, near.at[1, *where], send.at[3 + k], recv.at[3 + k], left)
-        for k, (part, near) in enumerate(((pack_a, near_a), (pack_b, near_b))):
+        _, (half_a, half_b), _ = share()
+        for k, (part, near, half) in enumerate(((pack_a, near_a, half_a), (pack_b, near_b, half_b))):
+            yield remote(part.at[half], near.at[0, half], send.at[k], recv.at[k], right)
+            yield remote(part.at[half], near.at[1, half], send.at[2 + k], recv.at[2 + k], left)
             yield pltpu.make_async_copy(part, near.at[2], own.at[k])
 
     def finish():
@@ -135,7 +135,7 @@
     row = lambda at: pl.BlockSpec((tm, d), lambda m: (at(m), 0))
     col = lambda at: pl.BlockSpec((d, tm), lambda m: (0, at(m)))
     wide = pl.BlockSpec((chunks, tm, width), lambda m: (0, here(m), 0))
-    pack_a, pack_b = (4, d // n, width), (2, EARLY_DOWN * STRIPE, d)
+    pack_a, pack_b = (4, d // n, EARLY * width), (2, EARLY * STRIPE, d)
     out = [jax.ShapeDtypeStruct((chunks, t, width), F32)] * 2
     out += [jax.ShapeDtypeStruct(s, BF16) for s in ((d, t), (t, d), (t, d), (d, t), (d, t))]
     out += [jax.ShapeDtypeStruct((3, *s), F32) for s in (pack_a, pack_b)]
@@ -157,8 +157,8 @@
             pltpu.VMEM(pack_b, F32),
             pltpu.SemaphoreType.DMA((4 * n + 2,)),
             pltpu.SemaphoreType.DMA((2,)),
-            pltpu.SemaphoreType.DMA((6,)),
-            pltpu.SemaphoreType.DMA((6,)),
+            pltpu.SemaphoreType.DMA((4,)),
+            pltpu.SemaphoreType.DMA((4,)),
         ],
         compiler_params=params(collective_id=2, has_side_effects=True),
         cost_estimate=cost(6 * t * d * ff, nbytes(*out)),
@@ -177,15 +177,17 @@
         pl.semaphore_signal(barrier, inc=1, device_id={"dp": device}, device_id_type=pl.DeviceIdType.MESH)
 
 
-def greet(devices):
-    hail(devices)
-    pl.semaphore_wait(pltpu.get_barrier_semaphore(), len(devices))
-
-
-def remote(src, dst, send, recv, device):
+def remote(src, dst, send, recv, device, axis="dp"):
     return pltpu.make_async_remote_copy(
-        src_ref=src, dst_ref=dst, send_sem=send, recv_sem=recv, device_id={"dp": device}, device_id_type=pl.DeviceIdType.MESH
+        src_ref=src, dst_ref=dst, send_sem=send, recv_sem=recv, device_id={axis: device}, device_id_type=pl.DeviceIdType.MESH
     )
+
+
+def share():
+    rep = lax.axis_index("rep")
+    core = lax.rem(rep, 2)
+    halves = [(pl.ds(2 * one, 2), pl.ds(one, 1)) for one in (core, 1 - core)]
+    return rep + 1 - 2 * core, *halves
 
 
 class Ring:
@@ -275,7 +277,7 @@
 
 def top_kernel(n, chunks, tiles, layer, *refs):
     wholes, (h, wd, wg, wu, near_a, near_b), refs = refs[:4], refs[4:10], refs[10:]
-    dh, dh_t, g_out, last, squares_out, far_a, far_b, late, *refs = refs
+    dh, dh_t, g_out, last, squares_out, other_a, other_b, far_a, far_b, *refs = refs
     alls, refs = refs[:2], refs[2:]
     gacc, uacc, dacc, da, raw, got, mid, squares, send, recv, local, wg_part, wu_part, w_sems, *mines, e_send, e_recv = refs[:-5]
     slots, loaded = refs[-5:-1], refs[-1]
@@ -286,36 +288,37 @@
     slot, here, there = lax.rem(before, 2), lax.rem(c, 2), lax.rem(c + 1, 2)
     ring = Ring(n, raw, got.at[slot], mid, send.at[slot], recv.at[slot])
 
+    other, (half_a, half_b), _ = share()
+
     def moments():
-        half, rows = far_a.shape[0] // 2, 3 * STRIPE // 2
-        parts = (
-            (near_a, far_a, (slice(0, half),), 0),
-            (near_b, far_b, (0, slice(0, rows)), 0),
-            (near_a, far_a, (slice(half, None),), 1),
-            (near_b, far_b, (0, slice(rows, None)), 1),
-            (near_b, far_b, (1, slice(0, STRIPE)), 1),
-        )
-        for k, (near, far, where, side) in enumerate(parts):
-            yield remote(near.at[side, *where], far.at[*where], e_send.at[8, k], e_recv.at[8, k], (right, left)[side])
+        kind, rows = half_a.start, far_b.shape[1] // 2
+        for side in range(2):
+            part, way = pl.ds(side * rows, rows), (right, left)[side]
+            yield remote(near_a.at[side, kind + side], far_a.at[kind + side], e_send.at[6, side], e_recv.at[6, side], way)
+            yield remote(near_b.at[side, half_b, part], far_b.at[half_b, part], e_send.at[7, side], e_recv.at[7, side], way)
+
+    def exchange(far):
+        pairs = [(near_a.at[side, half_a], other_a.at[side]) for side in range(2)]
+        pairs += [(near_b.at[side, half_b], other_b.at[side]) for side in range(2)]
+        if far:
+            pairs = [(far_a.at[half_a], far_a.at[half_a]), (far_b.at[half_b], far_b.at[half_b])]
+        for k, (src, dst) in enumerate(pairs):
+            yield remote(src, dst, e_send.at[8 + far, k], e_recv.at[8 + far, k], other, "rep")
 
     block = mines[0].shape[0]
     across = 2 * block // 3
-    rounds = (
-        (near_b.at[2, 1, STRIPE:], late, 0, STRIPE, 1),
-        (mines[0].at[across:], alls[0], across, block - across, 2),
-        (mines[0].at[:across], alls[0], 0, across, 3),
-        (mines[1], alls[1], 0, block - across, 4),
-    )
+    rounds = ((0, 0, block, 2), (1, across, block - across, 3), (1, 0, across, 4))
 
     def out(k):
-        mine, every, start, rows, _ = rounds[k]
+        early, start, rows, _ = rounds[k]
+        part = pl.ds(start, rows)
         for side in range(2):
-            to = every.at[side, pl.ds(start, rows)]
-            yield remote(mine, to, e_send.at[2 * k, side], e_recv.at[2 * k, side], (right, left)[side])
+            to = alls[early].at[side, part]
+            yield remote(mines[early].at[part], to, e_send.at[2 * k, side], e_recv.at[2 * k, side], (right, left)[side])
 
     def on(k):
-        _, every, start, rows, _ = rounds[k]
-        half, at = rows // 2, 2 * k + 1
+        early, start, rows, _ = rounds[k]
+        every, half, at = alls[early], rows // 2, 2 * k + 1
         for side in range(2):
             part = pl.ds(start + side * half, half)
             yield remote(every.at[side, part], every.at[2, part], e_send.at[at, side], e_recv.at[at, side], (right, left)[side])
@@ -336,8 +339,11 @@
         def _():
             for copy in (*weights(c, here), *loads(i)):
                 copy.start()
-            greet((right, left))
-            for copy in moments():
+            barrier = pltpu.get_barrier_semaphore()
+            pl.semaphore_signal(barrier, inc=1, device_id={"rep": other}, device_id_type=pl.DeviceIdType.MESH)
+            hail((right, left))
+            pl.semaphore_wait(barrier, 3)
+            for copy in (*moments(), *exchange(False)):
                 copy.start()
             squares[...] = jnp.zeros_like(squares)
 
@@ -407,6 +413,18 @@
 
     @pl.when(i == tiles // 2)
     def _():
+        @pl.when(c == 1)
+        def _():
+            for copy in moments():
+                copy.wait()
+            for copy in exchange(True):
+                copy.start()
+
+        @pl.when(c == 2)
+        def _():
+            for copy in (*exchange(False), *exchange(True)):
+                copy.wait()
+
         for k, (*_, first) in enumerate(rounds):
 
             @pl.when(c == first)
@@ -430,8 +448,6 @@
 
     @pl.when((c == chunks - 1) & (i == tiles - 1))
     def _():
-        for copy in moments():
-            copy.wait()
         for k, (*_, first) in enumerate(rounds):
             if first + 2 >= chunks:
                 for copy in on(k):
@@ -448,7 +464,7 @@
 
             @pl.when(c == k + 1)
             def _(mine=mine):
-                mine[...] = g_out[0, g_out.shape[1] - mine.shape[0] :]
+                mine[...] = g_out[0]
 
         lay_out(n, raw, gacc, uacc, dacc)
 
@@ -478,11 +494,9 @@
         jax.ShapeDtypeStruct((chunks - 1, block, width), BF16),
         jax.ShapeDtypeStruct((n, block, width), BF16),
         jax.ShapeDtypeStruct((8, width), F32),
-        jax.ShapeDtypeStruct(near_a.shape[1:], F32),
-        jax.ShapeDtypeStruct(near_b.shape[1:], F32),
-        jax.ShapeDtypeStruct((3, STRIPE, d), F32),
-        jax.ShapeDtypeStruct((3, block, width), BF16),
-        jax.ShapeDtypeStruct((3, block // 3, width), BF16),
+        *(jax.ShapeDtypeStruct((2, one.shape[1] // 2, *one.shape[2:]), F32) for one in (near_a, near_b)),
+        *(jax.ShapeDtypeStruct(one.shape[1:], F32) for one in (near_a, near_b)),
+        *[jax.ShapeDtypeStruct((3, block, width), BF16)] * EARLY,
     ]
     return pl.pallas_call(
         functools.partial(top_kernel, n, chunks, tiles, layer),
@@ -495,7 +509,7 @@
             pl.BlockSpec(memory_space=pl.ANY),
             pl.BlockSpec((8, width), lambda c, i: (0, 0)),
         ]
-        + [pl.BlockSpec(memory_space=pl.ANY)] * 5,
+        + [pl.BlockSpec(memory_space=pl.ANY)] * (4 + EARLY),
         out_shape=shapes,
         scratch_shapes=[pltpu.VMEM((d, width), F32)] * 3
         + [
@@ -510,10 +524,9 @@
             pltpu.VMEM((2, d, width), BF16),
             pltpu.VMEM((2, d, width), BF16),
             pltpu.SemaphoreType.DMA((2, 2, n)),
-            pltpu.VMEM((block, width), BF16),
-            pltpu.VMEM((block // 3, width), BF16),
-            pltpu.SemaphoreType.DMA((9, 5)),
-            pltpu.SemaphoreType.DMA((9, 5)),
+            *[pltpu.VMEM((block, width), BF16)] * EARLY,
+            pltpu.SemaphoreType.DMA((10, 4)),
+            pltpu.SemaphoreType.DMA((10, 4)),
         ]
         + [pltpu.VMEM((2, *one), BF16) for one in ((tm, d), (d, tm)) * 2]
         + [pltpu.SemaphoreType.DMA((4, 2))],
@@ -683,20 +696,18 @@
         m_out[layer, *at(c)] = m_new
         v_out[layer, *at(c)] = v_new
 
-    early = EARLY_DOWN if tall else 1
-
-    @pl.loop(0, early)
+    @pl.loop(0, EARLY)
     def _(c):
         work(0, c, g_bottom[c + 1], c)
         work(1, c, g_top[c], None)
 
-    @pl.loop(early, chunks - 1)
+    @pl.loop(EARLY, chunks - 1)
     def _(c):
         work(0, c, g_bottom[c + 1], c)
-        work(1, c, g_top[c], c - early)
+        work(1, c, g_top[c], c - EARLY)
 
     work(0, chunks - 1, g_bottom[chunks], chunks - 1)
-    work(1, chunks - 1, g_bottom[0], chunks - 1 - early)
+    work(1, chunks - 1, g_bottom[0], chunks - 1 - EARLY)
 
 
 def adam(me, squares, w, m, v, g_top, g_bottom, which, count, chunks, tall, first, blocks, begun):
@@ -704,7 +715,8 @@
     g_rows = g_top.shape[1] // 3
     g_width, width = (2 * STRIPE, 2 * g_rows) if tall else (STRIPE, STRIPE * chunks)
     block = pl.BlockSpec((layers, rows, width), lambda i, me: (0, 0, first + i))
-    new = [(rows, width), (rows - EARLY_DOWN * STRIPE, width) if tall else (rows, width - STRIPE)]
+    rest = EARLY * STRIPE
+    new = [(rows, width), (rows - rest, width) if tall else (rows, width - rest)]
     out = [jax.ShapeDtypeStruct((r, c * blocks), BF16) for r, c in new] + [jax.ShapeDtypeStruct(m.shape, F32)] * 2
     fixed = list(begun)
 
@@ -731,27 +743,18 @@
     return outs[:layers], outs[layers:]
 
 
-def early_kernel(n, chunks, count, squares, *refs):
-    wg, wu, refs = refs[:n], refs[n : 2 * n], refs[2 * n :]
-    (wd, near_a, near_b, far_a, far_b, late, g_top, g_all, g_all_down), refs = refs[:9], refs[9:]
-    outs, (a, b, g, g_down, loaded, across, down, sems) = refs[:3], refs[3:]
-    rows = g_down.shape[1]
-    g_near, g_near_down = g_top.at[0], g_top.at[1, 2 * rows :, :]
+def early_kernel(n, count, squares, *refs):
+    wg, wu, (wd, near_a, near_b, other_a, other_b, far_a, far_b, g_top), refs = refs[:n], refs[n : 2 * n], refs[2 * n : 2 * n + 8], refs[2 * n + 8 :]
+    alls, outs, (a, b, g, loaded, across, down, sems) = refs[:EARLY], refs[EARLY : EARLY + 3], refs[EARLY + 3 :]
+    rows, each = a.shape[2], EARLY * STRIPE
+    _, mine, others = share()
     loads = []
-    of_chunk = [pl.ds(k * STRIPE, STRIPE) for k in range(EARLY_DOWN)]
-    parts = [(a.at[turn], b.at[turn, 0], b.at[turn, 1, of_chunk[0]], b.at[turn, 1, of_chunk[1]], g.at[turn], g_down.at[turn]) for turn in range(n)]
-
-    def held(near_a, near_b, late, *sums):
-        return near_a, near_b.at[0], near_b.at[1, of_chunk[0]], late, *sums
-
-    sources = (
-        held(near_a.at[2], near_b.at[2], near_b.at[2, 1, of_chunk[1]], g_near, g_near_down),
-        held(near_a.at[1], near_b.at[1], late.at[1], g_all.at[1], g_all_down.at[1]),
-        held(far_a, far_b, late.at[2], g_all.at[2], g_all_down.at[2]),
-        held(near_a.at[0], near_b.at[0], late.at[0], g_all.at[0], g_all_down.at[0]),
-    )
-    for source, part in zip(sources, parts, strict=True):
-        loads += zip(source, part, strict=True)
+    for k, (part, near, other, far) in enumerate(((a, near_a, other_a, far_a), (b, near_b, other_b, far_b))):
+        loads += [(near.at[2], part.at[0]), (far, part.at[2])]
+        for turn, side in ((1, 1), (3, 0)):
+            loads += [(near.at[side, mine[k]], part.at[turn, mine[k]]), (other.at[side], part.at[turn, others[k]])]
+    for k, every in enumerate(alls):
+        loads += [(source, g.at[turn, k]) for turn, source in enumerate((g_top.at[k], every.at[1], every.at[2], every.at[0]))]
     loads = [pltpu.make_async_copy(src, dst, loaded.at[k]) for k, (src, dst) in enumerate(loads)]
     for copy in loads:
         copy.start()
@@ -765,18 +768,20 @@
         o = lax.rem(me + turn, n)
         at = pl.ds(pl.multiple_of(o * rows, rows), rows)
         for k, w in enumerate((wg, wu)):
-            old = jnp.concatenate([one[0, at, :] for one in w], 1)
-            grad = g[turn, k * rows : (k + 1) * rows, :].astype(F32) * factor
-            across[k, at, :] = adamw(old, a[turn, 2 * k], a[turn, 2 * k + 1], grad)[0]
-        for k, part in enumerate((g[turn, 2 * rows :, :], g_down[turn])):
-            grad = upright(part.astype(F32)) * factor
-            down[o, of_chunk[k], :] = adamw(wd[0, o, k], b[turn, 0, of_chunk[k], :], b[turn, 1, of_chunk[k], :], grad)[0]
-
-    copies = []
-    for o, s in enumerate(stripes(n, chunks, 0)):
+            for j in range(n):
+                to = slice(j * each, (j + 1) * each)
+                grad = jnp.concatenate([g[turn, e, k * rows : (k + 1) * rows, j * STRIPE : (j + 1) * STRIPE] for e in range(EARLY)], 1)
+                across[k, at, to] = adamw(w[j][0, at, :], a[turn, 2 * k, :, to], a[turn, 2 * k + 1, :, to], grad.astype(F32) * factor)[0]
+        for e in range(EARLY):
+            part = slice(e * STRIPE, (e + 1) * STRIPE)
+            grad = upright(g[turn, e, 2 * rows :, :].astype(F32)) * factor
+            down[o, part, :] = adamw(wd[0, o, e], b[turn, 0, part, :], b[turn, 1, part, :], grad)[0]
+
+    copies, whole = [], outs[0].shape[2] // n
+    for o in range(n):
         for k in range(2):
-            copies.append((across.at[k, :, o * STRIPE : (o + 1) * STRIPE], outs[k].at[1, :, s]))
-        copies.append((down.at[o], outs[2].at[1, s.start : s.start + down.shape[1], :]))
+            copies.append((across.at[k, :, o * each : (o + 1) * each], outs[k].at[1, :, o * whole : o * whole + each]))
+        copies.append((down.at[o], outs[2].at[1, o * whole : o * whole + each, :]))
     copies = [pltpu.make_async_copy(src, dst, sems.at[k]) for k, (src, dst) in enumerate(copies)]
     for copy in copies:
         copy.start()
@@ -784,31 +789,30 @@
         copy.wait()
 
 
-def early_step(n, chunks, squares, weights, near_a, near_b, far_a, far_b, late, g_top, g_all, g_all_down, count):
+def early_step(n, chunks, squares, weights, moments, g_top, alls, count):
     w_gate, w_up, w_down = weights
-    d = w_gate.shape[1]
-    whole = lambda one: pl.BlockSpec(one.shape, lambda i: (0,) * one.ndim)
-    across = [pl.BlockSpec((1, d, STRIPE), lambda i, o=o: (1, 0, o * chunks)) for o in range(n)]
-    down = pl.BlockSpec((1, n, EARLY_DOWN, STRIPE, d), lambda i: (1, 0, 0, 0, 0))
-    arrays = (near_a, near_b, far_a, far_b, late, g_top, g_all, g_all_down)
+    d, each = w_gate.shape[1], EARLY * STRIPE
+    assert chunks % EARLY == 0
+    across = [pl.BlockSpec((1, d, each), lambda i, o=o: (1, 0, o * (chunks // EARLY))) for o in range(n)]
+    down = pl.BlockSpec((1, n, EARLY, STRIPE, d), lambda i: (1, 0, 0, 0, 0))
+    arrays = (*moments, g_top, *alls)
+    held = [(n, *one.shape) for one in moments[-2:]]
     return pl.pallas_call(
-        functools.partial(early_kernel, n, chunks, count),
+        functools.partial(early_kernel, n, count),
         grid=(1,),
-        in_specs=[whole(squares)] + across + across + [down] + [pl.BlockSpec(memory_space=pl.ANY)] * len(arrays),
+        in_specs=[pl.BlockSpec(squares.shape, lambda i: (0, 0))] + across + across + [down] + [pl.BlockSpec(memory_space=pl.ANY)] * len(arrays),
         out_specs=[pl.BlockSpec(memory_space=pl.ANY)] * 3,
         out_shape=[jax.ShapeDtypeStruct(w.shape, BF16) for w in weights],
         scratch_shapes=[
-            pltpu.VMEM((n, *far_a.shape), F32),
-            pltpu.VMEM((n, *far_b.shape), F32),
-            pltpu.VMEM((n, *g_all.shape[1:]), BF16),
-            pltpu.VMEM((n, *g_all_down.shape[1:]), BF16),
-            pltpu.SemaphoreType.DMA((6 * n,)),
-            pltpu.VMEM((2, d, n * STRIPE), BF16),
-            pltpu.VMEM((n, EARLY_DOWN * STRIPE, d), BF16),
+            *(pltpu.VMEM(one, F32) for one in held),
+            pltpu.VMEM((n, EARLY, *g_top.shape[1:]), BF16),
+            pltpu.SemaphoreType.DMA((12 + n * EARLY,)),
+            pltpu.VMEM((2, d, n * each), BF16),
+            pltpu.VMEM((n, each, d), BF16),
             pltpu.SemaphoreType.DMA((3 * n,)),
         ],
         compiler_params=params(),
-        cost_estimate=cost(16 * 3 * d * n * STRIPE, nbytes(*arrays)),
+        cost_estimate=cost(16 * 3 * d * n * each, nbytes(*moments)),
         name="early",
     )(squares, *[w_gate] * n, *[w_up] * n, by_owner(n, w_down), *arrays)
 
@@ -838,11 +842,10 @@
     def regions(layer):
         if tall:
             columns = arrays[0].shape[1]
-            return [(0, layer * EARLY_DOWN * STRIPE, columns, slice(first * columns // blocks, (first + blocks) * columns // blocks))]
-        columns = full - layer * STRIPE
-        return [
-            (j * columns, 0, columns, slice((first + j) * full + layer * STRIPE, (first + j + 1) * full)) for j in range(blocks)
-        ]
+            return [(0, layer * EARLY * STRIPE, columns, slice(first * columns // blocks, (first + blocks) * columns // blocks))]
+        there = layer * EARLY * STRIPE
+        columns = full - there
+        return [(j * columns, 0, columns, slice((first + j) * full + there, (first + j + 1) * full)) for j in range(blocks)]
 
     return pl.pallas_call(
         functools.partial(place_kernel, n, where, regions),
@@ -884,8 +887,8 @@
         weights, moments = (w_gate, w_up, w_down), ((m_gate, v_gate), (m_up, v_up), (m_down, v_down))
         *parts, near_a, near_b = forward(n, chunks, x, dy, *weights, sum(moments, ()))
         gate, up, a0_t, h1, a1, a1_t, dy_t = parts
-        *parts, far_a, far_b, late, g_all, g_all_down = top(n, chunks, 1, a1, a1_t, dy, dy_t, h1, *weights, near_a, near_b)
-        dh, dh_t, g_top, last, squares = parts
+        parts = top(n, chunks, 1, a1, a1_t, dy, dy_t, h1, *weights, near_a, near_b)
+        (dh, dh_t, g_top, last, squares), early, alls = parts[:5], parts[5:9], parts[9:]
         g_bottom, squares = bottom(n, chunks, 0, a0_t, dh, dh_t, gate, up, w_down, last, squares)
 
         new, sent, count = [[], [], []], [], 3 * w_gate.size
@@ -895,7 +898,7 @@
             )
             squares = lax.optimization_barrier((squares, *own))[0]
             sent.append((own, *send_around(n, own, swap)))
-        whole = list(early_step(n, chunks, squares, weights, near_a, near_b, far_a, far_b, late, g_top, g_all, g_all_down, count))
+        whole = list(early_step(n, chunks, squares, weights, (near_a, near_b, *early), g_top, alls, count))
         for k, (which, first, blocks, swap) in enumerate(PIECES):
             own, left, right, _ = sent[k]
             near = [(one, (layer, turn)) for turn, pair in ((0, own), (n - 1, left), (1, right)) for layer, one in enumerate(pair)]

time: 676 us -> 665 us (0.984)
  waiting for transfers between devices: 135 us -> 122 us
    ppermute x30, waiting for transfers between devices: 135 us -> 122 us  [send(): return lax.ppermute(one, 'dp', way)]
  transfers between devices with their start and end apart: 30 -> 30, of which waited for: 15 -> 15; matrix products, arithmetic and copies ran while one was open for 0% -> 0% of each run, Pallas kernels for 6% -> 7%
where the time goes in v3:
time: 665 us
  Pallas kernels  502 us (75%)
  waiting for transfers between devices  122 us (18%)
  starting transfers between devices  35.3 us (5%)
    pallas_call x1, Pallas kernels, top(): pl.pallas_call(functools.partial(top_kernel, n, chunks, tiles, layer), gr...  191 us
    pallas_call x1, Pallas kernels, bottom(): pl.pallas_call(functools.partial(bottom_kernel, n, chunks, tiles), grid=(...  147 us
    ppermute x30, waiting for transfers between devices, send(): return lax.ppermute(one, 'dp', way)  122 us
    pallas_call x1, Pallas kernels, forward(): pl.pallas_call(functools.partial(forward_kernel, n, chunks, tiles), grid=...  76.4 us
    pallas_call x5, Pallas kernels, adam(): pl.pallas_call(body, grid_spec=pltpu.PrefetchScalarGridSpec(num_scalar_pr...  36.6 us
    ppermute x30, starting transfers between devices, send(): return lax.ppermute(one, 'dp', way)  35.3 us
    pallas_call x10, Pallas kernels, place(): pl.pallas_call(functools.partial(place_kernel, n, where, regions), grid=(...  30.7 us
    pallas_call x1, Pallas kernels, early_step(): pl.pallas_call(functools.partial(early_kernel, n, count), grid=(1,), in_s...  20.3 us
  transfers between devices with their start and end apart: 30, of which 15 were waited for; matrix products, arithmetic and copies ran while one was open for 0% of the time, Pallas kernels for 7%

profile of v3, /device:TPU:112, one launch (start us, length us, event | category | flops | bytes accessed | tf_op | source)
XLA Modules:
  0.0 664.6 jit_solution(1609740256166129437)
XLA Ops:
  0.6 76.4 %forward.1 = (f32[6,4096,512]{2,1,0:T(8,128)}, f32[6,4096,512]{2,1,0:T(8,128)}, bf16[768,4096]{1,0:T(8,128)(2,1)}, bf16[4096,768]{1,0:T(8,128)(2,1)}, bf16[4096,...) custom-call(bf16[4096,768]{1,0:T(8,128)(2,1)} %bitcast.7, ...), custom_call_target="tpu_custom_call" | custom-call | flops 57982058496 | bytes 146276352 | tf_op jit(solution)/shard_map/forward/pallas_call | solution.py:143
  77.0 191.0 %top.1 = (bf16[4096,768]{1,0:T(8,128)(2,1)}, bf16[768,4096]{1,0:T(8,128)(2,1)}, bf16[5,576,512]{2,1,0:T(8,128)(2,1)}, bf16[4,576,512]{2,1,0:T(8,128)(2,1)}, f32[...) custom-call(bf16[4096,768]{1,0:T(8,128)(2,1)} %get-tuple-element.60., ...), custom_call_target="tpu_custom_call" | custom-call | flops 154618822656 | bytes 150994944 | tf_op jit(solution)/shard_map/top/pallas_call | solution.py:501
  268.0 147.1 %bottom.1 = (bf16[7,576,512]{2,1,0:T(8,128)(2,1)}, f32[8,512]{1,0:T(8,128)}) custom-call(bf16[768,4096]{1,0:T(8,128)(2,1)} %get-tuple-element.59.refs_0_, bf16[4096,768]{1,0:T(8,128)(2,1)} %get-tuple-element.66.refs_1_, bf16[768,4096]{1,0:T(8,128)(2,1)} %get-tuple-element.67.refs_2_, f32[6,4096,512]{2,1,0:T(8,128)} %get-tuple-element.68.refs_3_, ...), custom_call_target="tpu_custom_call" | custom-call | flops 77309411328 | bytes 213909504 | tf_op jit(solution)/shard_map/bottom/pallas_call | solution.py:636
  415.1 4.3 adam.5
  419.5 9.2 %adam.6 = (bf16[192,2304]{1,0:T(8,128)(2,1)}, bf16[192,1536]{1,0:T(8,128)(2,1)}, f32[2,192,3072]{2,1,0:T(8,128)}, f32[2,192,3072]{2,1,0:T(8,128)}) custom-call(s32[1]{0:T(128)} %bitcast.me_ref, f32[8,512]{1,0:T(8,128)} %get-tuple-element.93.refs_0_.squares, bf16[2,768,3072]{2,1,0:T(8,128)(2,1)} %refs_3_.11, ...), custom_call_target="tpu_custom_call", output_to_operand_aliasing={{2}: (7, {}), {3}: (8, {})} | custom-call | flops 14155776 | bytes 19464192 | tf_op jit(solution)/shard_map/adam/pallas_call | solution.py:726
  428.6 9.5 %adam.7 = (bf16[768,768]{1,0:T(8,128)(2,1)}, bf16[512,768]{1,0:T(8,128)(2,1)}, f32[2,768,768]{2,1,0:T(8,128)}, f32[2,768,768]{2,1,0:T(8,128)}) custom-call(s32[1]{0:T(128)} %bitcast.me_ref, f32[8,512]{1,0:T(8,128)} %get-tuple-element.93.refs_0_.squares, bf16[2,3072,768]{2,1,0:T(8,128)(2,1)} %refs_1_.8, f32[2,768,768]{2,1,0:T(8,128)} %refs_2_.8, ...), custom_call_target="tpu_custom_call" | custom-call | flops 18874368 | bytes 25952256 | tf_op jit(solution)/shard_map/adam/pallas_call | solution.py:726
  438.2 9.2 %adam.8 = (bf16[192,2304]{1,0:T(8,128)(2,1)}, bf16[192,1536]{1,0:T(8,128)(2,1)}, f32[2,192,3072]{2,1,0:T(8,128)}, f32[2,192,3072]{2,1,0:T(8,128)}) custom-call(s32[1]{0:T(128)} %bitcast.me_ref, f32[8,512]{1,0:T(8,128)} %get-tuple-element.93.refs_0_.squares, bf16[2,768,3072]{2,1,0:T(8,128)(2,1)} %refs_7_.5, f32[2,192,3072]{2,1,0:T(8,128)} %refs_2_.10, ...), custom_call_target="tpu_custom_call" | custom-call | flops 14155776 | bytes 19464192 | tf_op jit(solution)/shard_map/adam/pallas_call | solution.py:726
  447.4 4.5 adam.9
  451.8 1.8 collective-permute-start.14
  453.6 0.2 collective-permute-start.20
  453.9 0.6 collective-permute-start.12
  454.4 1.6 collective-permute-start.10
  456.0 1.6 collective-permute-start.6
  457.7 1.2 collective-permute-done.14.refs_5_
  458.8 3.6 collective-permute-start.21
  462.4 0.5 collective-permute-done.20.refs_3_
  462.9 0.0 collective-permute-start.11
  462.9 7.7 %collective-permute-done.10.refs_3_ = bf16[192,512]{1,0:T(8,128)(2,1)} collective-permute-done((bf16[192,512]{1,0:T(8,128)(2,1)}, bf16[192,512]{1,0:T(8,128)(2,1)}, u32[]{:S(2)}, u32[]{:S(2)}) %collective-permute-start.10) | collective-permute-done | bytes 196640 | tf_op jit(solution)/shard_map/ppermute | solution.py:868
  470.7 0.0 collective-permute-start.18
  470.7 0.0 collective-permute-done.6.refs_5_
  470.7 0.1 collective-permute-start.4
  470.8 0.0 collective-permute-done.12.refs_2_
  470.8 3.2 collective-permute-start.23
  474.0 1.9 collective-permute-start.15
  476.0 1.0 collective-permute-done.11.refs_4_
  476.9 3.1 collective-permute-start.7
  480.0 10.7 %collective-permute-done.4.refs_2_ = bf16[192,768]{1,0:T(8,128)(2,1)S(1)} collective-permute-done((bf16[192,768]{1,0:T(8,128)(2,1)}, bf16[192,768]{1,0:T(8,128)(2,1)S(1)}, u32[]{:S(2)}, u32[]{:S(2)}) %collective-permute-start.4) | collective-permute-done | bytes 294944 | tf_op jit(solution)/shard_map/ppermute | solution.py:868
  490.8 3.0 collective-permute-done.15.refs_1_
  493.8 3.1 collective-permute-start.9
  496.9 1.1 collective-permute-done.7.refs_1_
  498.0 3.1 collective-permute-start.26
  501.2 3.3 collective-permute-start.16
  504.5 3.1 collective-permute-done.2.refs_3_
  507.6 3.0 collective-permute-done.9.refs_5_
  510.6 0.7 collective-permute-start.24
  511.3 19.5 %collective-permute-done.5.refs_0_ = bf16[192,768]{1,0:T(8,128)(2,1)} collective-permute-done((bf16[192,768]{1,0:T(8,128)(2,1)S(1)}, bf16[192,768]{1,0:T(8,128)(2,1)}, u32[]{:S(2)}, u32[]{:S(2)}) %collective-permute-start.5) | collective-permute-done | bytes 294944 | tf_op jit(solution)/shard_map/ppermute | solution.py:868
  530.8 3.2 collective-permute-start
  534.0 0.1 collective-permute-start.29
  534.2 12.3 %collective-permute-done.16.refs_4_ = bf16[192,2304]{1,0:T(8,128)(2,1)S(1)} collective-permute-done((bf16[192,2304]{1,0:T(8,128)(2,1)S(1)}, bf16[192,2304]{1,0:T(8,128)(2,1)S(1)}, u32[]{:S(2)}, u32[]{:S(2)}) %collective-permute-start.16) | collective-permute-done | bytes 884768 | tf_op jit(solution)/shard_map/ppermute | solution.py:868
  546.4 0.7 collective-permute-start.8
  547.1 27.8 %collective-permute-done.22.refs_2_ = bf16[192,2304]{1,0:T(8,128)(2,1)S(1)} collective-permute-done((bf16[192,2304]{1,0:T(8,128)(2,1)S(1)}, bf16[192,2304]{1,0:T(8,128)(2,1)S(1)}, u32[]{:S(2)}, u32[]{:S(2)}) %collective-permute-start.22) | collective-permute-done | bytes 884768 | tf_op jit(solution)/shard_map/ppermute | solution.py:868
  574.9 2.0 collective-permute-start.19
  577.0 0.1 collective-permute-start.25
  577.1 16.8 %collective-permute-done.8.refs_2_ = bf16[192,2304]{1,0:T(8,128)(2,1)S(1)} collective-permute-done((bf16[192,2304]{1,0:T(8,128)(2,1)}, bf16[192,2304]{1,0:T(8,128)(2,1)S(1)}, u32[]{:S(2)}, u32[]{:S(2)}) %collective-permute-start.8) | collective-permute-done | bytes 884768 | tf_op jit(solution)/shard_map/ppermute | solution.py:868
  593.9 1.1 copy-done.3
  595.0 0.4 collective-permute-start.27
  595.4 11.1 %collective-permute-done.19.refs_1_ = bf16[192,1536]{1,0:T(8,128)(2,1)S(1)} collective-permute-done((bf16[192,1536]{1,0:T(8,128)(2,1)S(1)}, bf16[192,1536]{1,0:T(8,128)(2,1)S(1)}, u32[]{:S(2)}, u32[]{:S(2)}) %collective-permute-start.19) | collective-permute-done | bytes 589856 | tf_op jit(solution)/shard_map/ppermute | solution.py:868
  606.5 3.1 collective-permute-done.17.refs_0_
  609.6 0.7 collective-permute-start.13
  610.3 0.2 copy-done.7
  610.5 20.3 %early.1 = (bf16[2,768,3072]{2,1,0:T(8,128)(2,1)}, bf16[2,768,3072]{2,1,0:T(8,128)(2,1)}, bf16[2,3072,768]{2,1,0:T(8,128)(2,1)}) custom-call(f32[8,512]{1,0:T(8,128)} %get-tuple-element.93.refs_0_.squares, bf16[2,768,3072]{2,1,0:T(8,128)(2,1)} %refs_3_.11, bf16[2,768,3072]{2,1,0:T(8,128)(2,1)} %refs_3_.11, bf16[2,768,3072]{2,1,0:T(8,128)(2,1)} %refs_3_.11, ...), custom_call_target="tpu_custom_call" | custom-call | flops 37748736 | bytes 23592960 | tf_op jit(solution)/shard_map/early/pallas_call | solution.py:800
  630.9 2.5 place.10.refs_6_
  633.5 4.4 place.14.refs_6_
  637.9 4.4 place.11.refs_2_
  642.4 2.5 place.15.refs_2_
  644.9 1.8 place.12.refs_2_
  646.7 5.3 place.18.refs_2_
  652.1 2.5 place.16.refs_2_
  654.6 0.7 copy-done.20
  655.3 1.8 place.17
  657.1 2.5 place.13
  659.7 0.9 copy-done.10
  660.5 1.1 copy-done.2
  661.6 2.8 place.19
  (65 shorter events, 0.1 us)
Async XLA Ops:
  447.3 23.3 %copy-start.12 = (bf16[192,1536]{1,0:T(8,128)(2,1)S(1)}, bf16[192,1536]{1,0:T(8,128)(2,1)}, u32[]{:S(2)}) copy-start(bf16[192,1536]{1,0:T(8,128)(2,1)} %get-tuple-element.87.refs_1_) | copy-start | bytes 1769476
  447.3 43.4 %copy-start.11 = (bf16[192,1536]{1,0:T(8,128)(2,1)S(1)}, bf16[192,1536]{1,0:T(8,128)(2,1)}, u32[]{:S(2)}) copy-start(bf16[192,1536]{1,0:T(8,128)(2,1)} %get-tuple-element.81.refs_1_) | copy-start | bytes 1769476
  447.3 50.6 %copy-start.9 = (bf16[512,768]{1,0:T(8,128)(2,1)S(1)}, bf16[512,768]{1,0:T(8,128)(2,1)}, u32[]{:S(2)}) copy-start(bf16[512,768]{1,0:T(8,128)(2,1)} %get-tuple-element.84.refs_1_) | copy-start | bytes 2359300
  447.4 53.8 %copy-start.4 = (bf16[192,2304]{1,0:T(8,128)(2,1)S(1)}, bf16[192,2304]{1,0:T(8,128)(2,1)}, u32[]{:S(2)}) copy-start(bf16[192,2304]{1,0:T(8,128)(2,1)} %get-tuple-element.86.refs_0_) | copy-start | bytes 2654212
  447.4 63.3 %copy-start = (bf16[768,768]{1,0:T(8,128)(2,1)S(1)}, bf16[768,768]{1,0:T(8,128)(2,1)}, u32[]{:S(2)}) copy-start(bf16[768,768]{1,0:T(8,128)(2,1)} %get-tuple-element.83.refs_0_) | copy-start | bytes 3538948
  451.8 7.0 %collective-permute-start.14 = (bf16[192,512]{1,0:T(8,128)(2,1)}, bf16[192,512]{1,0:T(8,128)(2,1)S(1)}, u32[]{:S(2)}, u32[]{:S(2)}) collective-permute-start(bf16[192,512]{1,0:T(8,128)(2,1)} %get-tuple-element.92.refs_1_), channel_id=1, source_target_pairs={{0,3},{1,0},{2,1},{3,2},{4,7},{5,4},{6,5},{7,6},{8,11},{9,8},{10,9... | collective-permute-start | bytes 589832 | tf_op jit(solution)/shard_map/ppermute | solution.py:868
  453.6 9.3 %collective-permute-start.20 = (bf16[192,512]{1,0:T(8,128)(2,1)}, bf16[192,512]{1,0:T(8,128)(2,1)}, u32[]{:S(2)}, u32[]{:S(2)}) collective-permute-start(bf16[192,512]{1,0:T(8,128)(2,1)} %get-tuple-element.92.refs_1_), channel_id=1, source_target_pairs={{0,1},{1,2},{2,3},{3,0},{4,5},{5,6},{6,7},{7,4},{8,9},{9,10},{10,1... | collective-permute-start | bytes 589832 | tf_op jit(solution)/shard_map/ppermute | solution.py:868
  453.9 16.9 %collective-permute-start.12 = (bf16[192,768]{1,0:T(8,128)(2,1)}, bf16[192,768]{1,0:T(8,128)(2,1)}, u32[]{:S(2)}, u32[]{:S(2)}) collective-permute-start(bf16[192,768]{1,0:T(8,128)(2,1)} %get-tuple-element.91.refs_0_), channel_id=1, source_target_pairs={{0,1},{1,2},{2,3},{3,0},{4,5},{5,6},{6,7},{7,4},{8,9},{9,10},{10,1... | collective-permute-start | bytes 884744 | tf_op jit(solution)/shard_map/ppermute | solution.py:868
  454.4 16.2 %collective-permute-start.10 = (bf16[192,512]{1,0:T(8,128)(2,1)}, bf16[192,512]{1,0:T(8,128)(2,1)}, u32[]{:S(2)}, u32[]{:S(2)}) collective-permute-start(bf16[192,512]{1,0:T(8,128)(2,1)} %get-tuple-element.76.refs_1_), channel_id=1, source_target_pairs={{0,1},{1,2},{2,3},{3,0},{4,5},{5,6},{6,7},{7,4},{8,9},{9,10},{10,1... | collective-permute-start | bytes 589832 | tf_op jit(solution)/shard_map/ppermute | solution.py:868
  456.0 14.6 %collective-permute-start.6 = (bf16[192,512]{1,0:T(8,128)(2,1)}, bf16[192,512]{1,0:T(8,128)(2,1)S(1)}, u32[]{:S(2)}, u32[]{:S(2)}) collective-permute-start(bf16[192,512]{1,0:T(8,128)(2,1)} %get-tuple-element.76.refs_1_), channel_id=1, source_target_pairs={{0,3},{1,0},{2,1},{3,2},{4,7},{5,4},{6,5},{7,6},{8,11},{9,8},{10,9... | collective-permute-start | bytes 589832 | tf_op jit(solution)/shard_map/ppermute | solution.py:868
  458.8 42.3 %copy-start.21 = (bf16[192,512]{1,0:T(8,128)(2,1)}, bf16[192,512]{1,0:T(8,128)(2,1)S(1)}, u32[]{:S(2)}) copy-start(bf16[192,512]{1,0:T(8,128)(2,1)S(1)} %collective-permute-done.14.refs_5_) | copy-start | bytes 589828
  458.8 15.2 %collective-permute-start.21 = (bf16[192,768]{1,0:T(8,128)(2,1)}, bf16[192,768]{1,0:T(8,128)(2,1)S(1)}, u32[]{:S(2)}, u32[]{:S(2)}) collective-permute-start(bf16[192,768]{1,0:T(8,128)(2,1)} %get-tuple-element.91.refs_0_), channel_id=1, source_target_pairs={{0,3},{1,0},{2,1},{3,2},{4,7},{5,4},{6,5},{7,6},{8,11},{9,8},{10,9... | collective-permute-start | bytes 884744 | tf_op jit(solution)/shard_map/ppermute | solution.py:868
  462.9 14.0 %collective-permute-start.11 = (bf16[192,768]{1,0:T(8,128)(2,1)}, bf16[192,768]{1,0:T(8,128)(2,1)S(1)}, u32[]{:S(2)}, u32[]{:S(2)}) collective-permute-start(bf16[192,768]{1,0:T(8,128)(2,1)} %get-tuple-element.75.refs_0_), channel_id=1, source_target_pairs={{0,3},{1,0},{2,1},{3,2},{4,7},{5,4},{6,5},{7,6},{8,11},{9,8},{10,9... | collective-permute-start | bytes 884744 | tf_op jit(solution)/shard_map/ppermute | solution.py:868
  470.7 30.4 %collective-permute-start.18 = (bf16[192,1536]{1,0:T(8,128)(2,1)S(1)}, bf16[192,1536]{1,0:T(8,128)(2,1)S(1)}, u32[]{:S(2)}, u32[]{:S(2)}) collective-permute-start(bf16[192,1536]{1,0:T(8,128)(2,1)S(1)} %copy-done.12), channel_id=1, source_target_pairs={{0,1},{1,2},{2,3},{3,0},{4,5},{5,6},{6,7},{7,4},{8,9},{9,10},{10,1... | collective-permute-start | bytes 1769480 | tf_op jit(solution)/shard_map/ppermute | solution.py:868
  470.7 40.6 %copy-start.23 = (bf16[192,512]{1,0:T(8,128)(2,1)}, bf16[192,512]{1,0:T(8,128)(2,1)S(1)}, u32[]{:S(2)}) copy-start(bf16[192,512]{1,0:T(8,128)(2,1)S(1)} %collective-permute-done.6.refs_5_) | copy-start | bytes 589828
  470.7 20.1 %collective-permute-start.4 = (bf16[192,768]{1,0:T(8,128)(2,1)}, bf16[192,768]{1,0:T(8,128)(2,1)S(1)}, u32[]{:S(2)}, u32[]{:S(2)}) collective-permute-start(bf16[192,768]{1,0:T(8,128)(2,1)} %get-tuple-element.75.refs_0_), channel_id=1, source_target_pairs={{0,1},{1,2},{2,3},{3,0},{4,5},{5,6},{6,7},{7,4},{8,9},{9,10},{10,1... | collective-permute-start | bytes 884744 | tf_op jit(solution)/shard_map/ppermute | solution.py:868
  470.8 30.4 %collective-permute-start.23 = (bf16[192,1536]{1,0:T(8,128)(2,1)S(1)}, bf16[192,1536]{1,0:T(8,128)(2,1)S(1)}, u32[]{:S(2)}, u32[]{:S(2)}) collective-permute-start(bf16[192,1536]{1,0:T(8,128)(2,1)S(1)} %copy-done.12), channel_id=1, source_target_pairs={{0,3},{1,0},{2,1},{3,2},{4,7},{5,4},{6,5},{7,6},{8,11},{9,8},{10,9... | collective-permute-start | bytes 1769480 | tf_op jit(solution)/shard_map/ppermute | solution.py:868
  474.0 27.1 %copy-start.17 = (bf16[192,768]{1,0:T(8,128)(2,1)}, bf16[192,768]{1,0:T(8,128)(2,1)S(1)}, u32[]{:S(2)}) copy-start(bf16[192,768]{1,0:T(8,128)(2,1)S(1)} %collective-permute-done.21.refs_4_) | copy-start | bytes 884740
  474.0 19.8 %collective-permute-start.15 = (bf16[192,512]{1,0:T(8,128)(2,1)S(1)}, bf16[192,512]{1,0:T(8,128)(2,1)S(1)}, u32[]{:S(2)}, u32[]{:S(2)}) collective-permute-start(bf16[192,512]{1,0:T(8,128)(2,1)S(1)} %collective-permute-done.14.refs_5_), channel_id=1, source_target_pairs={{0,3},{1,0},{2,1},{3,2},{4,7},{5,4},{6,5},{7,6},{8,11},{9,8},{10,9... | collective-permute-start | bytes 589832 | tf_op jit(solution)/shard_map/ppermute | solution.py:868
  476.9 24.2 %copy-start.18 = (bf16[192,768]{1,0:T(8,128)(2,1)}, bf16[192,768]{1,0:T(8,128)(2,1)S(1)}, u32[]{:S(2)}) copy-start(bf16[192,768]{1,0:T(8,128)(2,1)S(1)} %collective-permute-done.11.refs_4_) | copy-start | bytes 884740
  476.9 21.1 %collective-permute-start.7 = (bf16[192,512]{1,0:T(8,128)(2,1)S(1)}, bf16[192,512]{1,0:T(8,128)(2,1)S(1)}, u32[]{:S(2)}, u32[]{:S(2)}) collective-permute-start(bf16[192,512]{1,0:T(8,128)(2,1)S(1)} %collective-permute-done.6.refs_5_), channel_id=1, source_target_pairs={{0,3},{1,0},{2,1},{3,2},{4,7},{5,4},{6,5},{7,6},{8,11},{9,8},{10,9... | collective-permute-start | bytes 589832 | tf_op jit(solution)/shard_map/ppermute | solution.py:868
  490.8 20.6 %copy-start.19 = (bf16[192,768]{1,0:T(8,128)(2,1)}, bf16[192,768]{1,0:T(8,128)(2,1)S(1)}, u32[]{:S(2)}) copy-start(bf16[192,768]{1,0:T(8,128)(2,1)S(1)} %collective-permute-done.4.refs_2_) | copy-start | bytes 884740
  490.8 16.9 %collective-permute-start.2 = (bf16[192,1536]{1,0:T(8,128)(2,1)S(1)}, bf16[192,1536]{1,0:T(8,128)(2,1)}, u32[]{:S(2)}, u32[]{:S(2)}) collective-permute-start(bf16[192,1536]{1,0:T(8,128)(2,1)S(1)} %copy-done.11), channel_id=1, source_target_pairs={{0,1},{1,2},{2,3},{3,0},{4,5},{5,6},{6,7},{7,4},{8,9},{9,10},{10,1... | collective-permute-start | bytes 1769480 | tf_op jit(solution)/shard_map/ppermute | solution.py:868
  493.8 17.6 %copy-start.22 = (bf16[192,512]{1,0:T(8,128)(2,1)}, bf16[192,512]{1,0:T(8,128)(2,1)S(1)}, u32[]{:S(2)}) copy-start(bf16[192,512]{1,0:T(8,128)(2,1)S(1)} %collective-permute-done.15.refs_1_) | copy-start | bytes 589828
  493.8 16.9 %collective-permute-start.9 = (bf16[192,1536]{1,0:T(8,128)(2,1)S(1)}, bf16[192,1536]{1,0:T(8,128)(2,1)S(1)}, u32[]{:S(2)}, u32[]{:S(2)}) collective-permute-start(bf16[192,1536]{1,0:T(8,128)(2,1)S(1)} %copy-done.11), channel_id=1, source_target_pairs={{0,3},{1,0},{2,1},{3,2},{4,7},{5,4},{6,5},{7,6},{8,11},{9,8},{10,9... | collective-permute-start | bytes 1769480 | tf_op jit(solution)/shard_map/ppermute | solution.py:868
  498.0 13.3 %copy-start.24 = (bf16[192,512]{1,0:T(8,128)(2,1)}, bf16[192,512]{1,0:T(8,128)(2,1)S(1)}, u32[]{:S(2)}) copy-start(bf16[192,512]{1,0:T(8,128)(2,1)S(1)} %collective-permute-done.7.refs_1_) | copy-start | bytes 589828
  498.0 32.8 %collective-permute-start.26 = (bf16[512,768]{1,0:T(8,128)(2,1)S(1)}, bf16[512,768]{1,0:T(8,128)(2,1)}, u32[]{:S(2)}, u32[]{:S(2)}) collective-permute-start(bf16[512,768]{1,0:T(8,128)(2,1)S(1)} %copy-done.9), channel_id=1, source_target_pairs={{0,3},{1,0},{2,1},{3,2},{4,7},{5,4},{6,5},{7,6},{8,11},{9,8},{10,9... | collective-permute-start | bytes 2359304 | tf_op jit(solution)/shard_map/ppermute | solution.py:868
  501.1 109.4 %copy-start.13 = (bf16[192,1536]{1,0:T(8,128)(2,1)}, bf16[192,1536]{1,0:T(8,128)(2,1)S(1)}, u32[]{:S(2)}) copy-start(bf16[192,1536]{1,0:T(8,128)(2,1)S(1)} %collective-permute-done.18.refs_3_) | copy-start | bytes 1769476
  501.1 32.9 %collective-permute-start.28 = (bf16[512,768]{1,0:T(8,128)(2,1)S(1)}, bf16[512,768]{1,0:T(8,128)(2,1)}, u32[]{:S(2)}, u32[]{:S(2)}) collective-permute-start(bf16[512,768]{1,0:T(8,128)(2,1)S(1)} %copy-done.9), channel_id=1, source_target_pairs={{0,1},{1,2},{2,3},{3,0},{4,5},{5,6},{6,7},{7,4},{8,9},{9,10},{10,1... | collective-permute-start | bytes 2359304 | tf_op jit(solution)/shard_map/ppermute | solution.py:868
  501.2 32.9 %copy-start.14 = (bf16[192,1536]{1,0:T(8,128)(2,1)}, bf16[192,1536]{1,0:T(8,128)(2,1)S(1)}, u32[]{:S(2)}) copy-start(bf16[192,1536]{1,0:T(8,128)(2,1)S(1)} %collective-permute-done.23.refs_5_) | copy-start | bytes 1769476
  501.2 45.2 %collective-permute-start.16 = (bf16[192,2304]{1,0:T(8,128)(2,1)S(1)}, bf16[192,2304]{1,0:T(8,128)(2,1)S(1)}, u32[]{:S(2)}, u32[]{:S(2)}) collective-permute-start(bf16[192,2304]{1,0:T(8,128)(2,1)S(1)} %copy-done.4), channel_id=1, source_target_pairs={{0,3},{1,0},{2,1},{3,2},{4,7},{5,4},{6,5},{7,6},{8,11},{9,8},{10,9... | collective-permute-start | bytes 2654216 | tf_op jit(solution)/shard_map/ppermute | solution.py:868
  507.6 23.2 %collective-permute-start.5 = (bf16[192,768]{1,0:T(8,128)(2,1)S(1)}, bf16[192,768]{1,0:T(8,128)(2,1)}, u32[]{:S(2)}, u32[]{:S(2)}) collective-permute-start(bf16[192,768]{1,0:T(8,128)(2,1)S(1)} %collective-permute-done.4.refs_2_), channel_id=1, source_target_pairs={{0,1},{1,2},{2,3},{3,0},{4,5},{5,6},{6,7},{7,4},{8,9},{9,10},{10,1... | collective-permute-start | bytes 884744 | tf_op jit(solution)/shard_map/ppermute | solution.py:868
  510.6 23.4 %copy-start.15 = (bf16[192,1536]{1,0:T(8,128)(2,1)}, bf16[192,1536]{1,0:T(8,128)(2,1)S(1)}, u32[]{:S(2)}) copy-start(bf16[192,1536]{1,0:T(8,128)(2,1)S(1)} %collective-permute-done.9.refs_5_) | copy-start | bytes 1769476
  510.6 66.3 %collective-permute-start.24 = (bf16[768,768]{1,0:T(8,128)(2,1)S(1)}, bf16[768,768]{1,0:T(8,128)(2,1)S(1)}, u32[]{:S(2)}, u32[]{:S(2)}) collective-permute-start(bf16[768,768]{1,0:T(8,128)(2,1)S(1)} %copy-done), channel_id=1, source_target_pairs={{0,1},{1,2},{2,3},{3,0},{4,5},{5,6},{6,7},{7,4},{8,9},{9,10},{10,1... | collective-permute-start | bytes 3538952 | tf_op jit(solution)/shard_map/ppermute | solution.py:868
  530.8 44.1 %collective-permute-start.22 = (bf16[192,2304]{1,0:T(8,128)(2,1)S(1)}, bf16[192,2304]{1,0:T(8,128)(2,1)S(1)}, u32[]{:S(2)}, u32[]{:S(2)}) collective-permute-start(bf16[192,2304]{1,0:T(8,128)(2,1)S(1)} %copy-done.4), channel_id=1, source_target_pairs={{0,1},{1,2},{2,3},{3,0},{4,5},{5,6},{6,7},{7,4},{8,9},{9,10},{10,1... | collective-permute-start | bytes 2654216 | tf_op jit(solution)/shard_map/ppermute | solution.py:868
  530.8 44.1 %collective-permute-start = (bf16[192,2304]{1,0:T(8,128)(2,1)}, bf16[192,2304]{1,0:T(8,128)(2,1)}, u32[]{:S(2)}, u32[]{:S(2)}) collective-permute-start(bf16[192,2304]{1,0:T(8,128)(2,1)} %get-tuple-element.80.refs_0_), channel_id=1, source_target_pairs={{0,3},{1,0},{2,1},{3,2},{4,7},{5,4},{6,5},{7,6},{8,11},{9,8},{10,9... | collective-permute-start | bytes 2654216 | tf_op jit(solution)/shard_map/ppermute | solution.py:868
  534.0 59.8 %collective-permute-start.29 = (bf16[768,768]{1,0:T(8,128)(2,1)S(1)}, bf16[768,768]{1,0:T(8,128)(2,1)S(1)}, u32[]{:S(2)}, u32[]{:S(2)}) collective-permute-start(bf16[768,768]{1,0:T(8,128)(2,1)S(1)} %copy-done), channel_id=1, source_target_pairs={{0,3},{1,0},{2,1},{3,2},{4,7},{5,4},{6,5},{7,6},{8,11},{9,8},{10,9... | collective-permute-start | bytes 3538952 | tf_op jit(solution)/shard_map/ppermute | solution.py:868
  546.4 49.0 %copy-start.5 = (bf16[192,2304]{1,0:T(8,128)(2,1)}, bf16[192,2304]{1,0:T(8,128)(2,1)S(1)}, u32[]{:S(2)}) copy-start(bf16[192,2304]{1,0:T(8,128)(2,1)S(1)} %collective-permute-done.16.refs_4_) | copy-start | bytes 2654212
  546.4 47.4 %collective-permute-start.8 = (bf16[192,2304]{1,0:T(8,128)(2,1)}, bf16[192,2304]{1,0:T(8,128)(2,1)S(1)}, u32[]{:S(2)}, u32[]{:S(2)}) collective-permute-start(bf16[192,2304]{1,0:T(8,128)(2,1)} %get-tuple-element.80.refs_0_), channel_id=1, source_target_pairs={{0,1},{1,2},{2,3},{3,0},{4,5},{5,6},{6,7},{7,4},{8,9},{9,10},{10,1... | collective-permute-start | bytes 2654216 | tf_op jit(solution)/shard_map/ppermute | solution.py:868
  574.9 34.7 %copy-start.6 = (bf16[192,2304]{1,0:T(8,128)(2,1)}, bf16[192,2304]{1,0:T(8,128)(2,1)S(1)}, u32[]{:S(2)}) copy-start(bf16[192,2304]{1,0:T(8,128)(2,1)S(1)} %collective-permute-done.22.refs_2_) | copy-start | bytes 2654212
  574.9 34.7 %collective-permute-start.17 = (bf16[192,2304]{1,0:T(8,128)(2,1)S(1)}, bf16[192,2304]{1,0:T(8,128)(2,1)S(1)}, u32[]{:S(2)}, u32[]{:S(2)}) collective-permute-start(bf16[192,2304]{1,0:T(8,128)(2,1)S(1)} %collective-permute-done.16.refs_4_), channel_id=1, source_target_pairs={{0,3},{1,0},{2,1},{3,2},{4,7},{5,4},{6,5},{7,6},{8,11},{9,8},{10,9... | collective-permute-start | bytes 2654216 | tf_op jit(solution)/shard_map/ppermute | solution.py:868
  574.9 31.6 %collective-permute-start.19 = (bf16[192,1536]{1,0:T(8,128)(2,1)S(1)}, bf16[192,1536]{1,0:T(8,128)(2,1)S(1)}, u32[]{:S(2)}, u32[]{:S(2)}) collective-permute-start(bf16[192,1536]{1,0:T(8,128)(2,1)S(1)} %collective-permute-done.18.refs_3_), channel_id=1, source_target_pairs={{0,1},{1,2},{2,3},{3,0},{4,5},{5,6},{6,7},{7,4},{8,9},{9,10},{10,1... | collective-permute-start | bytes 1769480 | tf_op jit(solution)/shard_map/ppermute | solution.py:868
  577.0 53.9 %copy-start.1 = (bf16[768,768]{1,0:T(8,128)(2,1)}, bf16[768,768]{1,0:T(8,128)(2,1)S(1)}, u32[]{:S(2)}) copy-start(bf16[768,768]{1,0:T(8,128)(2,1)S(1)} %collective-permute-done.24.refs_2_) | copy-start | bytes 3538948
  577.0 82.7 %collective-permute-start.25 = (bf16[768,768]{1,0:T(8,128)(2,1)S(1)}, bf16[768,768]{1,0:T(8,128)(2,1)S(1)}, u32[]{:S(2)}, u32[]{:S(2)}) collective-permute-start(bf16[768,768]{1,0:T(8,128)(2,1)S(1)} %collective-permute-done.24.refs_2_), channel_id=1, source_target_pairs={{0,1},{1,2},{2,3},{3,0},{4,5},{5,6},{6,7},{7,4},{8,9},{9,10},{10,1... | collective-permute-start | bytes 3538952 | tf_op jit(solution)/shard_map/ppermute | solution.py:868
  593.9 16.7 %copy-start.8 = (bf16[192,2304]{1,0:T(8,128)(2,1)}, bf16[192,2304]{1,0:T(8,128)(2,1)S(1)}, u32[]{:S(2)}) copy-start(bf16[192,2304]{1,0:T(8,128)(2,1)S(1)} %collective-permute-done.8.refs_2_) | copy-start | bytes 2654212
  593.9 63.2 %collective-permute-start.1 = (bf16[192,2304]{1,0:T(8,128)(2,1)}, bf16[192,2304]{1,0:T(8,128)(2,1)}, u32[]{:S(2)}, u32[]{:S(2)}) collective-permute-start(bf16[192,2304]{1,0:T(8,128)(2,1)} %collective-permute-done.refs_4_), channel_id=1, source_target_pairs={{0,3},{1,0},{2,1},{3,2},{4,7},{5,4},{6,5},{7,6},{8,11},{9,8},{10,9... | collective-permute-start | bytes 2654216 | tf_op jit(solution)/shard_map/ppermute | solution.py:868
  593.9 1.1 copy-start.3
  595.0 64.6 %collective-permute-start.27 = (bf16[512,768]{1,0:T(8,128)(2,1)}, bf16[512,768]{1,0:T(8,128)(2,1)S(1)}, u32[]{:S(2)}, u32[]{:S(2)}) collective-permute-start(bf16[512,768]{1,0:T(8,128)(2,1)} %collective-permute-done.26.refs_5_), channel_id=1, source_target_pairs={{0,3},{1,0},{2,1},{3,2},{4,7},{5,4},{6,5},{7,6},{8,11},{9,8},{10,9... | collective-permute-start | bytes 2359304 | tf_op jit(solution)/shard_map/ppermute | solution.py:868
  606.5 24.4 %copy-start.16 = (bf16[192,1536]{1,0:T(8,128)(2,1)}, bf16[192,1536]{1,0:T(8,128)(2,1)S(1)}, u32[]{:S(2)}) copy-start(bf16[192,1536]{1,0:T(8,128)(2,1)S(1)} %collective-permute-done.19.refs_1_) | copy-start | bytes 1769476
  606.5 50.6 %collective-permute-start.3 = (bf16[192,1536]{1,0:T(8,128)(2,1)}, bf16[192,1536]{1,0:T(8,128)(2,1)}, u32[]{:S(2)}, u32[]{:S(2)}) collective-permute-start(bf16[192,1536]{1,0:T(8,128)(2,1)} %collective-permute-done.2.refs_3_), channel_id=1, source_target_pairs={{0,1},{1,2},{2,3},{3,0},{4,5},{5,6},{6,7},{7,4},{8,9},{9,10},{10,1... | collective-permute-start | bytes 1769480 | tf_op jit(solution)/shard_map/ppermute | solution.py:868
  609.6 0.9 copy-start.7
  609.6 44.9 %collective-permute-start.13 = (bf16[192,768]{1,0:T(8,128)(2,1)}, bf16[192,768]{1,0:T(8,128)(2,1)S(1)}, u32[]{:S(2)}, u32[]{:S(2)}) collective-permute-start(bf16[192,768]{1,0:T(8,128)(2,1)} %collective-permute-done.12.refs_2_), channel_id=1, source_target_pairs={{0,1},{1,2},{2,3},{3,0},{4,5},{5,6},{6,7},{7,4},{8,9},{9,10},{10,1... | collective-permute-start | bytes 884744 | tf_op jit(solution)/shard_map/ppermute | solution.py:868
  654.6 0.7 copy-start.20
  659.6 0.9 copy-start.10
  660.5 1.1 copy-start.2
